TPU v7x, 32 devices: a whole 2x2x4 slice. The times are simulated.
32 devices in a mesh: fsdp: 8 (over y, x, core), tensor: 4 (over z).
Axes of the slice: x: 2, y: 2, z: 4, core: 2. Of those that a mesh axis runs over, the one named last changes fastest.
Arguments:
- inputs: bfloat16 [4096, 2048], P(('fsdp', 'tensor')), may hold values from -6 to 6
- cotangent: bfloat16 [4096, 2048], P(('fsdp', 'tensor')), may hold values from -6 to 6
- segments: int32 [4096], replicated, may hold values from 0 to 31, never falling along the last dimension, each value on 1 to 512 neighbouring positions
- positions: int32 [4096], P('fsdp'), may hold values from 0 to 2047
- qkv_weight: float32 [2048, 8, 768], P('fsdp', 'tensor')
- qkv_bias: float32 [8, 768], P('tensor'), may hold values from -0.6 to 0.6
- dense_weight: float32 [2048, 2048], P('fsdp', 'tensor'), may hold values from -1 to 1
- expand_weight: float32 [2048, 8192], P('fsdp', 'tensor'), may hold values from -0.125 to 0.125
- expand_bias: float32 [8192], P('tensor'), may hold values from -0.6 to 0.6
- contract_weight: float32 [2048, 8192], P('fsdp', 'tensor'), may hold values from -0.0625 to 0.0625
- norm_bias_vectors: float32 [6, 2048], replicated
- moment_qkv_weight: float32 [2048, 8, 768], P('fsdp', 'tensor'), may hold values from -24 to 24
- moment_qkv_bias: float32 [8, 768], P('tensor'), may hold values from -24 to 24
- moment_dense_weight: float32 [2048, 2048], P('fsdp', 'tensor'), may hold values from -24 to 24
- moment_expand_weight: float32 [2048, 8192], P('fsdp', 'tensor'), may hold values from -24 to 24
- moment_expand_bias: float32 [8192], P('tensor'), may hold values from -24 to 24
- moment_contract_weight: float32 [2048, 8192], P('fsdp', 'tensor'), may hold values from -24 to 24
- moment_norm_vectors: float32 [6, 2048], replicated, may hold values from -64 to 64
- second_qkv_weight: float32 [2048, 8, 768], P('fsdp', 'tensor'), may hold values from 122.88 to 491.52
- second_qkv_bias: float32 [8, 768], P('tensor'), may hold values from 122.88 to 491.52
- second_dense_weight: float32 [2048, 2048], P('fsdp', 'tensor'), may hold values from 122.88 to 491.52
- second_expand_weight: float32 [2048, 8192], P('fsdp', 'tensor'), may hold values from 122.88 to 491.52
- second_expand_bias: float32 [8192], P('tensor'), may hold values from 122.88 to 491.52
- second_contract_weight: float32 [2048, 8192], P('fsdp', 'tensor'), may hold values from 122.88 to 491.52
- second_norm_vectors: float32 [6, 2048], replicated, may hold values from 1228.8 to 4915.2
Outputs:
- output: float32 [4096, 2048], P(('fsdp', 'tensor'))
- block_input_gradient: float32 [4096, 2048], P(('fsdp', 'tensor'))
- gradient_qkv_weight: float32 [2048, 8, 768], P('fsdp', 'tensor')
- new_qkv_weight: float32 [2048, 8, 768], P('fsdp', 'tensor')
- new_moment_qkv_weight: float32 [2048, 8, 768], P('fsdp', 'tensor')
- new_second_qkv_weight: float32 [2048, 8, 768], P('fsdp', 'tensor')
- gradient_qkv_bias: float32 [8, 768], P('tensor')
- new_qkv_bias: float32 [8, 768], P('tensor')
- new_moment_qkv_bias: float32 [8, 768], P('tensor')
- new_second_qkv_bias: float32 [8, 768], P('tensor')
- gradient_dense_weight: float32 [2048, 2048], P('fsdp', 'tensor')
- new_dense_weight: float32 [2048, 2048], P('fsdp', 'tensor')
- new_moment_dense_weight: float32 [2048, 2048], P('fsdp', 'tensor')
- new_second_dense_weight: float32 [2048, 2048], P('fsdp', 'tensor')
- gradient_expand_weight: float32 [2048, 8192], P('fsdp', 'tensor')
- new_expand_weight: float32 [2048, 8192], P('fsdp', 'tensor')
- new_moment_expand_weight: float32 [2048, 8192], P('fsdp', 'tensor')
- new_second_expand_weight: float32 [2048, 8192], P('fsdp', 'tensor')
- gradient_expand_bias: float32 [8192], P('tensor')
- new_expand_bias: float32 [8192], P('tensor')
- new_moment_expand_bias: float32 [8192], P('tensor')
- new_second_expand_bias: float32 [8192], P('tensor')
- gradient_contract_weight: float32 [2048, 8192], P('fsdp', 'tensor')
- new_contract_weight: float32 [2048, 8192], P('fsdp', 'tensor')
- new_moment_contract_weight: float32 [2048, 8192], P('fsdp', 'tensor')
- new_second_contract_weight: float32 [2048, 8192], P('fsdp', 'tensor')
- gradient_norm_vectors: float32 [6, 2048], replicated
- new_norm_vectors: float32 [6, 2048], replicated
- new_moment_norm_vectors: float32 [6, 2048], replicated
- new_second_norm_vectors: float32 [6, 2048], replicated
Inputs may be any that keep to these rules, and one draw needn't show every extreme that they name: `segments`: segment numbers never fall along the token stream; every document holds at most 512 tokens and one holds exactly 512.
All inputs are finite; a program needn't handle non-finite values.
Results may differ from a plain program's by a relative error of at most 0.0065.
The roundings to bfloat16 on the way count: a program that leaves them out, or rounds other values in their place, can miss the bound.
Values may be sent and summed in bfloat16 or wider, within the bound.
No kernel may reach another device: no remote copies, remote signals or barrier semaphores. Data moves between devices by JAX's collectives and lax.ppermute only.
A program may use at most 256 MiB of HBM per device.

v0:
```python
import jax
import jax.numpy as jnp
from jax import lax
from jax.sharding import PartitionSpec as P

ROT = 64
STEP = 3


norm_eps = 1e-05
masked_score = -1e30
beta_one = 0.9
beta_two = 0.95
adam_eps = 1e-08
decay_matrix = 0.01
rate_qkv_weight = 0.005
rate_qkv_bias = 0.02
rate_dense_weight = 0.04
rate_expand_weight = 0.005
rate_expand_bias = 0.02
rate_contract_weight = 0.003
rate_norm_vectors = 0.1


def shifted(value, axis, steps):
    count = lax.axis_size(axis)
    first, last = (max(0, -steps), min(count, count - steps))
    return lax.ppermute(value, axis, [(source, source + steps) for source in range(first, last)])


def normalized_row_block(row_values):
    center = row_values - jnp.mean(row_values, axis=-1, keepdims=True)
    variance = jnp.mean(center * center, axis=-1, keepdims=True)
    inverse_deviation = lax.rsqrt(variance + norm_eps)
    return (center * inverse_deviation, inverse_deviation)


def norm_backward_term(upstream_gradient, gain_vector_row, centered_normalized, inverse_deviation):
    scaled_rows = upstream_gradient * gain_vector_row
    return inverse_deviation * (
        scaled_rows
        - jnp.mean(scaled_rows, axis=-1, keepdims=True)
        - centered_normalized * jnp.mean(scaled_rows * centered_normalized, axis=-1, keepdims=True)
    )


def rotary_tables(token_pos):
    half_rot = ROT // 2
    frequency = 10000.0 ** (-(jnp.arange(half_rot, dtype=jnp.float32) * 2.0 / ROT))
    angles = token_pos.astype(jnp.float32)[:, None] * frequency[None, :]
    return (jnp.cos(angles)[:, None, :], jnp.sin(angles)[:, None, :])


def rotate(head_values, cosine_rotation, sine_rotation_table, direction):
    half_rot = ROT // 2
    first_half = head_values[..., :half_rot]
    second_half = head_values[..., half_rot:ROT]
    return jnp.concatenate(
        [
            first_half * cosine_rotation - direction * second_half * sine_rotation_table,
            second_half * cosine_rotation + direction * first_half * sine_rotation_table,
            head_values[..., ROT:],
        ],
        axis=-1,
    )


def gelu_slope(pre_values):
    return (
        0.5 * (1.0 + lax.erf(pre_values * 0.7071067811865476))
        + pre_values * jnp.exp(-0.5 * pre_values * pre_values) * 0.3989422804014327
    )


def key_mask(seg_query, query_index, seg_keys, group_rows, has_prev):
    key_index = jnp.arange(seg_keys.shape[0], dtype=jnp.int32)
    causal = key_index[None, :] <= query_index[:, None]
    same_doc = seg_keys[None, :] == seg_query[:, None]
    present = (key_index[None, :] >= group_rows) | has_prev
    return causal & same_doc & present


def block_scores(query_blk, keys_all, allowed, score_scale):
    scores = (
        jnp.einsum("qhc,khc->hqk", query_blk, keys_all, preferred_element_type=jnp.float32)
        * score_scale
    )
    return jnp.where(allowed[None], scores, masked_score)


def adam_step(parameter, gradient, moment, second, step_rate, decay_weight):
    moment_new = beta_one * moment + (1.0 - beta_one) * gradient
    second_new = beta_two * second + (1.0 - beta_two) * gradient * gradient
    moment_hat = moment_new / (1.0 - beta_one**STEP)
    second_hat = second_new / (1.0 - beta_two**STEP)
    updated = parameter - step_rate * (
        moment_hat / (jnp.sqrt(second_hat) + adam_eps) + decay_weight * parameter
    )
    return (updated, moment_new, second_new)


def contract_rows(left_rows, right_rows):
    return lax.dot_general(
        left_rows, right_rows, (((0,), (0,)), ((), ())), preferred_element_type=jnp.float32
    )


def contract_cols(left_cols, right_cols):
    return lax.dot_general(
        left_cols, right_cols, (((1,), (1,)), ((), ())), preferred_element_type=jnp.float32
    )


def per_device(
    inputs,
    cotangent,
    segments,
    positions,
    qkv_weight,
    qkv_bias,
    dense_weight,
    expand_weight,
    expand_bias,
    contract_weight,
    norm_bias_vectors,
    moment_qkv_weight,
    moment_qkv_bias,
    moment_dense_weight,
    moment_expand_weight,
    moment_expand_bias,
    moment_contract_weight,
    moment_norm_vectors,
    second_qkv_weight,
    second_qkv_bias,
    second_dense_weight,
    second_expand_weight,
    second_expand_bias,
    second_contract_weight,
    second_norm_vectors,
):
    fsdp_index = lax.axis_index("fsdp")
    input_row_block, rows_dy = (
        lax.all_gather(inputs, "tensor", axis=0, tiled=True),
        lax.all_gather(cotangent, "tensor", axis=0, tiled=True),
    )
    group_rows = input_row_block.shape[0]
    shards_bf = (
        qkv_weight.astype(jnp.bfloat16),
        dense_weight.astype(jnp.bfloat16),
        expand_weight.astype(jnp.bfloat16),
        contract_weight.astype(jnp.bfloat16),
    )
    forward_set = (
        lax.all_gather(shards_bf[0], "fsdp", axis=0, tiled=True),
        lax.all_gather(shards_bf[1], "fsdp", axis=0, tiled=True),
        lax.all_gather(shards_bf[2], "fsdp", axis=0, tiled=True),
        lax.all_gather(shards_bf[3], "fsdp", axis=0, tiled=True),
    )
    full_qkv, full_dense, full_expand, full_contract = forward_set
    row_centered_normalized, inverse_row_deviation = normalized_row_block(
        input_row_block.astype(jnp.float32)
    )
    attention_normalized_input = (
        row_centered_normalized * norm_bias_vectors[0] + norm_bias_vectors[1]
    ).astype(jnp.bfloat16)
    feedforward_normalized_input = (
        row_centered_normalized * norm_bias_vectors[2] + norm_bias_vectors[3]
    ).astype(jnp.bfloat16)
    projected = (
        jnp.einsum(
            "rd,dhc->rhc", attention_normalized_input, full_qkv, preferred_element_type=jnp.float32
        )
        + qkv_bias[None]
    )
    heads_dev = projected.shape[1]
    head_dim = projected.shape[2] // 3
    score_scale = head_dim ** (-0.5)
    cosine_rotation, sine_rotation_table = rotary_tables(positions)
    query_rows = rotate(
        projected[..., :head_dim], cosine_rotation, sine_rotation_table, 1.0
    ).astype(jnp.bfloat16)
    local_segment_keys = rotate(
        projected[..., head_dim : 2 * head_dim], cosine_rotation, sine_rotation_table, 1.0
    ).astype(jnp.bfloat16)
    local_segment_values = projected[..., 2 * head_dim :].astype(jnp.bfloat16)
    keys_prev, values_prev = shifted((local_segment_keys, local_segment_values), "fsdp", 1)
    keys_all = jnp.concatenate([keys_prev, local_segment_keys], axis=0)
    values_all = jnp.concatenate([values_prev, local_segment_values], axis=0)
    seg_own = lax.dynamic_slice_in_dim(segments, fsdp_index * group_rows, group_rows)
    seg_prev = lax.dynamic_slice_in_dim(
        segments, jnp.maximum(fsdp_index - 1, 0) * group_rows, group_rows
    )
    seg_keys = jnp.concatenate([seg_prev, seg_own], axis=0)
    has_prev = fsdp_index > 0
    block_rows = min(512, group_rows)
    blocks = group_rows // block_rows
    starts = jnp.arange(blocks, dtype=jnp.int32) * block_rows
    local_index = jnp.arange(block_rows, dtype=jnp.int32)
    query_blocks = query_rows.reshape(blocks, block_rows, heads_dev, head_dim)
    seg_blocks = seg_own.reshape(blocks, block_rows)

    def forward_block(block_data):
        query_blk, seg_blk, start = block_data
        allowed = key_mask(
            seg_blk, group_rows + start + local_index, seg_keys, group_rows, has_prev
        )
        scores = block_scores(query_blk, keys_all, allowed, score_scale)
        row_max = jnp.max(scores, axis=-1, keepdims=True)
        row_total = jnp.sum(jnp.exp(scores - row_max), axis=-1, keepdims=True)
        log_total = row_max + jnp.log(row_total)
        prob_bf = jnp.exp(scores - log_total).astype(jnp.bfloat16)
        result = jnp.einsum("hqk,khc->qhc", prob_bf, values_all, preferred_element_type=jnp.float32)
        return (result.astype(jnp.bfloat16), log_total[..., 0])

    attn_blocks, lse_blocks = lax.map(forward_block, (query_blocks, seg_blocks, starts))
    attended = attn_blocks.reshape(group_rows, heads_dev * head_dim)
    expand_preactivation = (
        jnp.dot(feedforward_normalized_input, full_expand, preferred_element_type=jnp.float32)
        + expand_bias
    )
    gelu_activated_rows = jax.nn.gelu(expand_preactivation, approximate=False).astype(jnp.bfloat16)
    branch_sum = lax.psum_scatter(
        contract_cols(attended, full_dense) + contract_cols(gelu_activated_rows, full_contract),
        "tensor",
        scatter_dimension=0,
        tiled=True,
    )
    output = inputs.astype(jnp.float32) + branch_sum + norm_bias_vectors[4] + norm_bias_vectors[5]
    back_qkv, back_dense, back_expand, back_contract = forward_set
    act_grad = jnp.dot(rows_dy, back_contract, preferred_element_type=jnp.float32)
    pre_grad32 = act_grad * gelu_slope(expand_preactivation)
    pre_grad = pre_grad32.astype(jnp.bfloat16)
    attn_grad = jnp.dot(rows_dy, back_dense, preferred_element_type=jnp.float32).astype(
        jnp.bfloat16
    )
    attn_heads = attn_grad.reshape(group_rows, heads_dev, head_dim)
    row_delta = jnp.sum(
        attn_heads.astype(jnp.float32)
        * attended.reshape(group_rows, heads_dev, head_dim).astype(jnp.float32),
        axis=-1,
    )

    def backward_block(inner_carry, block_data):
        key_acc, value_acc = inner_carry
        query_blk, seg_blk, start, grad_blk, delta_blk, lse_blk = block_data
        allowed = key_mask(
            seg_blk, group_rows + start + local_index, seg_keys, group_rows, has_prev
        )
        scores = block_scores(query_blk, keys_all, allowed, score_scale)
        prob_f32 = jnp.exp(scores - lse_blk[..., None])
        prob_bf = prob_f32.astype(jnp.bfloat16)
        dot_grad = jnp.einsum(
            "qhc,khc->hqk", grad_blk, values_all, preferred_element_type=jnp.float32
        )
        score_grad = (
            prob_f32 * (dot_grad - jnp.transpose(delta_blk)[..., None]) * score_scale
        ).astype(jnp.bfloat16)
        query_grad = jnp.einsum(
            "hqk,khc->qhc", score_grad, keys_all, preferred_element_type=jnp.float32
        )
        key_acc = key_acc + jnp.einsum(
            "hqk,qhc->khc", score_grad, query_blk, preferred_element_type=jnp.float32
        )
        value_acc = value_acc + jnp.einsum(
            "hqk,qhc->khc", prob_bf, grad_blk, preferred_element_type=jnp.float32
        )
        return ((key_acc, value_acc), query_grad)

    zero_keys = jnp.zeros((2 * group_rows, heads_dev, head_dim), jnp.float32)
    inner_final, query_grads = lax.scan(
        backward_block,
        (zero_keys, zero_keys),
        (
            query_blocks,
            seg_blocks,
            starts,
            attn_heads.reshape(blocks, block_rows, heads_dev, head_dim),
            row_delta.reshape(blocks, block_rows, heads_dev),
            lse_blocks,
        ),
    )
    key_acc, value_acc = inner_final
    later_key_grad, later_value_grad = shifted(
        (key_acc[:group_rows], value_acc[:group_rows]), "fsdp", -1
    )
    key_grad = key_acc[group_rows:] + later_key_grad
    value_grad = value_acc[group_rows:] + later_value_grad
    query_grad = query_grads.reshape(group_rows, heads_dev, head_dim)
    qkv_grad32 = jnp.concatenate(
        [
            rotate(query_grad, cosine_rotation, sine_rotation_table, -1.0),
            rotate(key_grad, cosine_rotation, sine_rotation_table, -1.0),
            value_grad,
        ],
        axis=-1,
    )
    qkv_grad = qkv_grad32.astype(jnp.bfloat16)
    attn_norm_grad = jnp.einsum(
        "rhc,dhc->rd", qkv_grad, back_qkv, preferred_element_type=jnp.float32
    )
    mlp_norm_grad = contract_cols(pre_grad, back_expand)
    qkv_part = jnp.einsum(
        "rd,rhc->dhc", attention_normalized_input, qkv_grad, preferred_element_type=jnp.float32
    )
    dense_part = contract_rows(rows_dy, attended)
    expand_part = contract_rows(feedforward_normalized_input, pre_grad)
    contract_part = contract_rows(rows_dy, gelu_activated_rows)
    local_centered_normalized, inverse_local_deviation = normalized_row_block(
        inputs.astype(jnp.float32)
    )
    dy_local = cotangent.astype(jnp.float32)
    dy_column_sum = jnp.sum(dy_local, axis=0)
    attention_backward_term, feedforward_backward_term = (
        lax.psum_scatter(attn_norm_grad, "tensor", scatter_dimension=0, tiled=True),
        lax.psum_scatter(mlp_norm_grad, "tensor", scatter_dimension=0, tiled=True),
    )
    block_input_gradient = (
        dy_local
        + norm_backward_term(
            attention_backward_term,
            norm_bias_vectors[0],
            local_centered_normalized,
            inverse_local_deviation,
        )
        + norm_backward_term(
            feedforward_backward_term,
            norm_bias_vectors[2],
            local_centered_normalized,
            inverse_local_deviation,
        )
    )
    vector_part = jnp.stack(
        [
            jnp.sum(attention_backward_term * local_centered_normalized, axis=0),
            jnp.sum(attention_backward_term, axis=0),
            jnp.sum(feedforward_backward_term * local_centered_normalized, axis=0),
            jnp.sum(feedforward_backward_term, axis=0),
            dy_column_sum,
            dy_column_sum,
        ]
    )
    qkv_bias_part = jnp.sum(qkv_grad32, axis=0)
    expand_bias_part = jnp.sum(pre_grad32, axis=0)
    grad_qkv_weight, grad_dense_weight, grad_expand_weight, grad_contract_weight = (
        lax.psum_scatter(qkv_part, "fsdp", scatter_dimension=0, tiled=True),
        lax.psum_scatter(dense_part, "fsdp", scatter_dimension=0, tiled=True),
        lax.psum_scatter(expand_part, "fsdp", scatter_dimension=0, tiled=True),
        lax.psum_scatter(contract_part, "fsdp", scatter_dimension=0, tiled=True),
    )
    grad_qkv_bias, grad_expand_bias, vector_fsdp = lax.psum(
        (qkv_bias_part, expand_bias_part, vector_part), "fsdp"
    )
    grad_norm_vectors = lax.psum(vector_fsdp, "tensor")
    new_qkv_weight, new_moment_qkv_weight, new_second_qkv_weight = adam_step(
        qkv_weight,
        grad_qkv_weight,
        moment_qkv_weight,
        second_qkv_weight,
        rate_qkv_weight,
        decay_matrix,
    )
    new_qkv_bias, new_moment_qkv_bias, new_second_qkv_bias = adam_step(
        qkv_bias, grad_qkv_bias, moment_qkv_bias, second_qkv_bias, rate_qkv_bias, 0.0
    )
    new_dense_weight, new_moment_dense_weight, new_second_dense_weight = adam_step(
        dense_weight,
        grad_dense_weight,
        moment_dense_weight,
        second_dense_weight,
        rate_dense_weight,
        decay_matrix,
    )
    new_expand_weight, new_moment_expand_weight, new_second_expand_weight = adam_step(
        expand_weight,
        grad_expand_weight,
        moment_expand_weight,
        second_expand_weight,
        rate_expand_weight,
        decay_matrix,
    )
    new_expand_bias, new_moment_expand_bias, new_second_expand_bias = adam_step(
        expand_bias, grad_expand_bias, moment_expand_bias, second_expand_bias, rate_expand_bias, 0.0
    )
    new_contract_weight, new_moment_contract_weight, new_second_contract_weight = adam_step(
        contract_weight,
        grad_contract_weight,
        moment_contract_weight,
        second_contract_weight,
        rate_contract_weight,
        decay_matrix,
    )
    new_norm_vectors, new_moment_norm_vectors, new_second_norm_vectors = adam_step(
        norm_bias_vectors,
        grad_norm_vectors,
        moment_norm_vectors,
        second_norm_vectors,
        rate_norm_vectors,
        0.0,
    )
    return (
        output,
        block_input_gradient,
        grad_qkv_weight,
        new_qkv_weight,
        new_moment_qkv_weight,
        new_second_qkv_weight,
        grad_qkv_bias,
        new_qkv_bias,
        new_moment_qkv_bias,
        new_second_qkv_bias,
        grad_dense_weight,
        new_dense_weight,
        new_moment_dense_weight,
        new_second_dense_weight,
        grad_expand_weight,
        new_expand_weight,
        new_moment_expand_weight,
        new_second_expand_weight,
        grad_expand_bias,
        new_expand_bias,
        new_moment_expand_bias,
        new_second_expand_bias,
        grad_contract_weight,
        new_contract_weight,
        new_moment_contract_weight,
        new_second_contract_weight,
        grad_norm_vectors,
        new_norm_vectors,
        new_moment_norm_vectors,
        new_second_norm_vectors,
    )


def solution(mesh):
    return jax.shard_map(
        per_device,
        mesh=mesh,
        in_specs=(
            P(("fsdp", "tensor"), None),
            P(("fsdp", "tensor"), None),
            P(),
            P("fsdp"),
            P("fsdp", "tensor", None),
            P("tensor", None),
            P("fsdp", "tensor"),
            P("fsdp", "tensor"),
            P("tensor"),
            P("fsdp", "tensor"),
            P(),
            P("fsdp", "tensor", None),
            P("tensor", None),
            P("fsdp", "tensor"),
            P("fsdp", "tensor"),
            P("tensor"),
            P("fsdp", "tensor"),
            P(),
            P("fsdp", "tensor", None),
            P("tensor", None),
            P("fsdp", "tensor"),
            P("fsdp", "tensor"),
            P("tensor"),
            P("fsdp", "tensor"),
            P(),
        ),
        out_specs=(
            P(("fsdp", "tensor"), None),
            P(("fsdp", "tensor"), None),
            P("fsdp", "tensor", None),
            P("fsdp", "tensor", None),
            P("fsdp", "tensor", None),
            P("fsdp", "tensor", None),
            P("tensor", None),
            P("tensor", None),
            P("tensor", None),
            P("tensor", None),
            P("fsdp", "tensor"),
            P("fsdp", "tensor"),
            P("fsdp", "tensor"),
            P("fsdp", "tensor"),
            P("fsdp", "tensor"),
            P("fsdp", "tensor"),
            P("fsdp", "tensor"),
            P("fsdp", "tensor"),
            P("tensor"),
            P("tensor"),
            P("tensor"),
            P("tensor"),
            P("fsdp", "tensor"),
            P("fsdp", "tensor"),
            P("fsdp", "tensor"),
            P("fsdp", "tensor"),
            P(),
            P(),
            P(),
            P(),
        ),
        check_vma=False,
    )
```

profile of v0, /device:TPU:0, one launch (start us, length us, event | category | flops | bytes accessed | tf_op | source)
XLA Modules:
  0.0 958.7 jit_solution(7499303931956926961)
XLA Ops:
  8.0 2.7 convert_element_type.79
  12.2 45.8 %all-gather.7.cloned.1.call-done = bf16[512,2048]{1,0:T(8,128)(2,1)} async-done(((bf16[128,2048]{1,0:T(8,128)(2,1)}), bf16[512,2048]{1,0:T(8,128)(2,1)}) %all-gather.7.cloned.1.call-update) | async-done | bytes 2097168 | tf_op jit(solution)/shard_map/all_gather | solution.py:143
  58.0 2.1 convert_reduce_fusion
  60.9 52.6 %all-gather.13.cloned.1.call-done = bf16[2048,2048]{1,0:T(8,128)(2,1)} async-done(((bf16[256,2048]{1,0:T(8,128)(2,1)}), bf16[2048,2048]{1,0:T(8,128)(2,1)}) %all-gather.13.cloned.1.call-update) | async-done | bytes 8388624 | tf_op jit(solution)/shard_map/all_gather | solution.py:156
  113.6 17.2 %fusion.11 = (bf16[512,2048]{1,0:T(8,128)(2,1)}, f32[512,2048]{1,0:T(8,128)}) fusion(f32[2048]{0:T(1024)S(1)} %copy-done.49, bf16[2048,2048]{1,0:T(8,128)(2,1)} %all-gather.13.cloned.1.call-done, bf16[512,2048]{1,0:T(8,128)(2,1)S(1)} %copy-done.2, f32[2048]{0:T(1024)S(1)} %bitcast.77, f32[2048]{0:T(1024)S(1)} %bitcast.61, f32[512]{0:T(512)S(1)} %add_rsqrt_fusion, ...), kind=kOutput, calls=%fused_computation.16 | convolution fusion | flops 4370464768 | bytes 16805888 | tf_op jit(solution)/shard_map/dot_general | solution.py:218
  130.8 30.1 %all-gather.17.cloned.1.call-done = bf16[512,2048]{1,0:T(8,128)(2,1)} async-done(((bf16[128,2048]{1,0:T(8,128)(2,1)}), bf16[512,2048]{1,0:T(8,128)(2,1)}) %all-gather.17.cloned.1.call-update) | async-done | bytes 2097168 | tf_op jit(solution)/shard_map/all_gather | solution.py:144
  160.8 12.5 %convolution_bitcast_fusion = f32[2048,2048]{1,0:T(8,128)} fusion(bf16[512,2048]{1,0:T(8,128)(2,1)} %get-tuple-element.201, bf16[512,2048]{1,0:T(8,128)(2,1)} %all-gather.17.cloned.1.call-done), kind=kOutput, calls=%fused_computation | convolution fusion | flops 4294967296 | bytes 20971520 | tf_op jit(solution)/shard_map/dot_general | solution.py:103
  173.4 2.4 copy.107
  177.0 111.5 %reduce-scatter.20.cloned.1.call-done = f32[256,2048]{1,0:T(8,128)} async-done(((f32[2048,2048]{1,0:T(8,128)}), f32[256,2048]{1,0:T(8,128)}) %reduce-scatter.20.cloned.1.call-update) | async-done | bytes 2097168 | tf_op jit(solution)/shard_map/reduce_scatter | solution.py:348
  288.5 8.6 multiply_subtract_fusion
  298.1 1.8 broadcast_multiply_fusion
  299.9 36.3 %all-gather.9.cloned.1.call-done = bf16[2048,2,768]{2,0,1:T(8,128)(2,1)} async-done(((bf16[256,2,768]{2,0,1:T(8,128)(2,1)}), bf16[2048,2,768]{2,0,1:T(8,128)(2,1)}) %all-gather.9.cloned.1.call-update) | async-done | bytes 6291472 | tf_op jit(solution)/shard_map/all_gather | solution.py:154
  336.3 6.4 fusion.87
  342.7 1.3 fusion.84
  345.2 1.3 pad_maximum_fusion.4
  346.5 2.9 collective-permute-start.1
  350.0 16.4 %all-gather.11.cloned.1.call-done = bf16[2048,512]{1,0:T(8,128)(2,1)} async-done(((bf16[256,512]{1,0:T(8,128)(2,1)}), bf16[2048,512]{1,0:T(8,128)(2,1)}) %all-gather.11.cloned.1.call-update) | async-done | bytes 2097168 | tf_op jit(solution)/shard_map/all_gather | solution.py:155
  366.4 3.0 convolution_convert_fusion
  369.4 1.3 slice.105
  370.7 2.6 collective-permute-start
  373.4 2.7 fusion.25
  377.3 1.6 multiply_reduce_fusion
  379.8 3.4 convolution_bitcast_fusion.1
  384.5 3.6 multiply_convert_fusion
  388.2 1.3 convolution_bitcast_fusion.4
  390.5 1.3 collective-permute-start.2
  391.8 1.9 convolution_bitcast_fusion.5
  396.2 3.9 convolution_bitcast_fusion.3
  401.3 1.6 collective-permute-start.3
  403.9 1.4 slice_add_fusion.1
  405.6 1.3 multiply_add_fusion.3
  406.9 1.3 copy.62
  412.2 3.4 collective-permute-done.3
  415.6 1.4 fusion.53
  417.0 1.6 copy-done.9
  418.7 7.6 fusion.58
  426.4 9.2 convolution_bitcast_fusion.2
  435.9 9.4 fusion.88
  445.4 1.3 copy-done.62
  446.7 10.2 %fusion.56 = f32[512,2048]{1,0:T(8,128)} fusion(bf16[2048,2048]{1,0:T(8,128)(2,1)} %all-gather.13.cloned.1.call-done, bf16[512,2048]{1,0:T(8,128)(2,1)S(1)} %get-tuple-element.204), kind=kOutput, calls=%fused_computation.103 | convolution fusion | flops 4294967296 | bytes 14680064 | tf_op jit(solution)/shard_map/dot_general | solution.py:109
  457.0 7.8 fusion.89
  464.8 3.3 convolution_add_fusion
  468.2 10.3 %fusion.54 = f32[2048,2048]{1,0:T(8,128)} fusion(bf16[512,2048]{1,0:T(8,128)(2,1)} %copy-done.62, bf16[512,2048]{1,0:T(8,128)(2,1)S(1)} %copy-done.3, f32[2048]{0:T(1024)S(1)} %bitcast.78, f32[2048]{0:T(1024)S(1)} %bitcast.62, f32[512]{0:T(512)S(1)} %add_rsqrt_fusion, f32[512]{0:T(512)S(1)} %broadcast_multiply_fusion.1), kind=kOutput, calls=%fused_computation.101 | convolution fusion | flops 4301258752 | bytes 20992000 | tf_op jit(solution)/shard_map/dot_general | solution.py:103
  482.3 2.2 reduce_sum.164
  484.5 5.7 reduce-scatter.16.cloned.1.call-done
  490.2 2.8 multiply_subtract_fusion.3
  493.0 2.0 copy.85
  495.0 2.0 copy.86
  497.0 2.0 copy.87
  500.1 85.7 %reduce-scatter.14.cloned.1.call-done = f32[256,2,768]{2,0,1:T(8,128)} async-done(((f32[2048,2,768]{2,0,1:T(8,128)}), f32[256,2,768]{2,0,1:T(8,128)}) %reduce-scatter.14.cloned.1.call-update) | async-done | bytes 1572880 | tf_op jit(solution)/shard_map/reduce_scatter | solution.py:345
  585.8 3.5 multiply_subtract_fusion.2
  589.4 2.4 copy.81
  591.7 2.4 copy.82
  594.1 2.4 copy.83
  596.4 2.4 copy.80
  598.8 66.0 %reduce-scatter.10.cloned.1.call-done = f32[128,2048]{1,0:T(8,128)} async-done(((f32[512,2048]{1,0:T(8,128)}), f32[128,2048]{1,0:T(8,128)}) %reduce-scatter.10.cloned.1.call-update) | async-done | bytes 1048592 | tf_op jit(solution)/shard_map/reduce_scatter | solution.py:314
  664.8 79.6 %reduce-scatter.12.cloned.1.call-done = f32[128,2048]{1,0:T(8,128)} async-done(((f32[512,2048]{1,0:T(8,128)}), f32[128,2048]{1,0:T(8,128)}) %reduce-scatter.12.cloned.1.call-update) | async-done | bytes 1048592 | tf_op jit(solution)/shard_map/reduce_scatter | solution.py:315
  744.4 2.3 fusion.48
  746.7 77.2 %reduce-scatter.8.cloned.1.call-done = f32[128,2048]{1,0:T(8,128)} async-done(((f32[512,2048]{1,0:T(8,128)}), f32[128,2048]{1,0:T(8,128)}) %reduce-scatter.8.cloned.1.call-update) | async-done | bytes 1048592 | tf_op jit(solution)/shard_map/reduce_scatter | solution.py:222
  824.0 4.2 convert_reduce_fusion.2
  828.3 24.6 %all-reduce = (f32[2,768]{1,0:T(2,128)S(1)}, f32[2048]{0:T(1024)S(1)}, f32[6,2048]{1,0:T(8,128)S(1)}) all-reduce(f32[2,768]{1,0:T(2,128)S(1)} %reduce_sum.164, f32[2048]{0:T(1024)S(1)} %get-tuple-element.203, f32[6,2048]{1,0:T(8,128)S(1)} %stack.24), channel_id=1, replica_groups=mesh['fsdp'=8,'tensor'=4] {'fsdp'}, use_global_device_ids=true, to_apply=%region_16.17 | all-reduce | flops 15872 | bytes 126976 | tf_op jit(solution)/shard_map/psum | solution.py:350
  853.0 19.8 %psum.31 = f32[6,2048]{1,0:T(8,128)S(1)} all-reduce(f32[6,2048]{1,0:T(8,128)S(1)} %get-tuple-element.146), channel_id=1, replica_groups=mesh['fsdp'=8,'tensor'=4] {'tensor'}, use_global_device_ids=true, to_apply=%region_28.29 | all-reduce | flops 12288 | bytes 98304 | tf_op jit(solution)/shard_map/psum | solution.py:353
  874.8 70.0 %reduce-scatter.18.cloned.1.call-done = f32[256,2048]{1,0:T(8,128)} async-done(((f32[2048,2048]{1,0:T(8,128)}), f32[256,2048]{1,0:T(8,128)}) %reduce-scatter.18.cloned.1.call-update) | async-done | bytes 2097168 | tf_op jit(solution)/shard_map/reduce_scatter | solution.py:347
  944.8 6.9 multiply_subtract_fusion.1
  (198 shorter events, 27.5 us)
Async XLA Ops:
  7.2 4.3 copy-start.43
  7.2 50.8 %all-gather.7.cloned.1.call-start = ((), (), s32[]{:S(2)}) async-start(), calls=%async_computation.7 | async-start | bytes 2621440 | tf_op jit(solution)/shard_map/all_gather | solution.py:143
  7.9 105.6 %all-gather.13.cloned.1.call-start = ((), (), s32[]{:S(2)}) async-start(), calls=%async_computation.10 | async-start | bytes 9437184 | tf_op jit(solution)/shard_map/all_gather | solution.py:156
  10.7 102.9 %copy-start.49 = (f32[2048]{0:T(1024)S(1)}, f32[2048]{0:T(1024)}, u32[]{:S(2)}) copy-start(f32[2048]{0:T(1024)} %param.33) | copy-start | bytes 24580
  10.7 150.1 %all-gather.17.cloned.1.call-start = ((), (), s32[]{:S(2)}) async-start(), calls=%async_computation.13 | async-start | bytes 2621440 | tf_op jit(solution)/shard_map/all_gather | solution.py:144
  11.5 277.0 %reduce-scatter.20.cloned.1.call-start = ((), (), s32[]{:S(2)}) async-start(), calls=%async_computation.19 | async-start | bytes 18874368 | tf_op jit(solution)/shard_map/reduce_scatter | solution.py:348
  173.4 162.9 %all-gather.9.cloned.1.call-start = ((), (), s32[]{:S(2)}) async-start(), calls=%async_computation.8 | async-start | bytes 7077888 | tf_op jit(solution)/shard_map/all_gather | solution.py:154
  175.9 190.5 %all-gather.11.cloned.1.call-start = ((), (), s32[]{:S(2)}) async-start(), calls=%async_computation.9 | async-start | bytes 2359296 | tf_op jit(solution)/shard_map/all_gather | solution.py:155
  176.7 120.5 %copy-start.57 = (s32[512]{0:T(512)S(1)}, s32[512]{0:T(512)}, u32[]{:S(2)}) copy-start(s32[512]{0:T(512)} %param.28) | copy-start | bytes 6148
  176.7 159.6 %copy-start.53 = (f32[2,768]{1,0:T(2,128)S(1)}, f32[2,768]{1,0:T(2,128)}, u32[]{:S(2)}) copy-start(f32[2,768]{1,0:T(2,128)} %param.30) | copy-start | bytes 18436
  176.7 259.2 %all-gather.15.cloned.1.call-start = ((), (), s32[]{:S(2)}) async-start(), calls=%async_computation.11 | async-start | bytes 9437184 | tf_op jit(solution)/shard_map/all_gather | solution.py:157
  297.1 193.0 %reduce-scatter.16.cloned.1.call-start = ((), (), s32[]{:S(2)}) async-start(), calls=%async_computation.17 | async-start | bytes 4718592 | tf_op jit(solution)/shard_map/reduce_scatter | solution.py:346
  336.3 7.7 copy-start.36
  342.7 3.8 copy-start.25
  344.0 22.4 %copy-start.17 = (bf16[512,2048]{1,0:T(8,128)(2,1)S(1)}, bf16[512,2048]{1,0:T(8,128)(2,1)}, u32[]{:S(2)}) copy-start(bf16[512,2048]{1,0:T(8,128)(2,1)} %all-gather.17.cloned.1.call-done) | copy-start | bytes 6291460
  345.2 4.2 copy-start.30
  345.2 4.2 copy-start.33
  346.5 26.9 %collective-permute-start.1 = (bf16[512,2,256]{2,0,1:T(8,128)(2,1)}, bf16[512,2,256]{2,0,1:T(8,128)(2,1)}, u32[]{:S(2)}, u32[]{:S(2)}) collective-permute-start(bf16[512,2,256]{2,0,1:T(8,128)(2,1)} %pad_maximum_fusion.4), channel_id=1, source_target_pairs={{0,4},{4,8},{8,12},{12,16},{16,20},{20,24},{24,28},{1,5},{5,9},{9,... | collective-permute-start | bytes 1572872 | tf_op jit(solution)/shard_map/ppermute | solution.py:28
  350.0 33.2 %copy-start.16 = (pred[512,1024]{1,0:T(8,128)(4,1)}, pred[512,1024]{1,0:T(8,128)(4,1)S(1)}, u32[]{:S(2)}) copy-start(pred[512,1024]{1,0:T(8,128)(4,1)S(1)} %fusion.30) | copy-start | bytes 1572868
  366.4 6.9 copy-start.20
  366.4 6.9 copy-start.26
  366.4 6.9 copy-start.28
  366.4 7.0 copy-start.31
  366.4 6.9 copy-start.34
  369.4 7.9 copy-start.60
  370.7 6.6 copy-start.40
  370.7 6.6 collective-permute-start
  383.2 202.7 %reduce-scatter.14.cloned.1.call-start = ((), (), s32[]{:S(2)}) async-start(), calls=%async_computation.16 | async-start | bytes 14155776 | tf_op jit(solution)/shard_map/reduce_scatter | solution.py:345
  384.5 3.6 copy-start.21
  384.5 3.6 copy-start.27
  384.5 3.6 copy-start.29
  388.1 3.7 copy-start.32
  388.1 3.7 copy-start.35
  390.5 13.4 %collective-permute-start.2 = (f32[512,2,256]{2,0,1:T(8,128)}, f32[512,2,256]{2,0,1:T(8,128)}, u32[]{:S(2)}, u32[]{:S(2)}) collective-permute-start(f32[512,2,256]{2,0,1:T(8,128)} %slice.116), channel_id=1, source_target_pairs={{4,0},{8,4},{12,8},{16,12},{20,16},{24,20},{28,24},{5,1},{9,5},{13... | collective-permute-start | bytes 3145736 | tf_op jit(solution)/shard_map/ppermute | solution.py:28
  400.1 5.5 copy-start.12
  401.3 4.3 copy-start.8
  401.3 4.3 copy-start.37
  401.3 14.3 %collective-permute-start.3 = (f32[512,2,256]{0,2,1:T(8,128)}, f32[512,2,256]{0,2,1:T(8,128)}, u32[]{:S(2)}, u32[]{:S(2)}) collective-permute-start(f32[512,2,256]{0,2,1:T(8,128)} %slice.121), channel_id=1, source_target_pairs={{4,0},{8,4},{12,8},{16,12},{20,16},{24,20},{28,24},{5,1},{9,5},{13... | collective-permute-start | bytes 3145736 | tf_op jit(solution)/shard_map/ppermute | solution.py:28
  406.9 4.1 copy-start.10
  411.0 4.6 copy-start.13
  411.1 7.6 copy-start.3
  426.3 238.5 %reduce-scatter.10.cloned.1.call-start = ((), (), s32[]{:S(2)}) async-start(), calls=%async_computation.14 | async-start | bytes 5242880 | tf_op jit(solution)/shard_map/reduce_scatter | solution.py:314
  435.7 308.8 %reduce-scatter.12.cloned.1.call-start = ((), (), s32[]{:S(2)}) async-start(), calls=%async_computation.15 | async-start | bytes 5242880 | tf_op jit(solution)/shard_map/reduce_scatter | solution.py:315
  456.9 7.9 copy-start.24
  457.0 366.9 %reduce-scatter.8.cloned.1.call-start = ((), (), s32[]{:S(2)}) async-start(), calls=%async_computation.12 | async-start | bytes 5242880 | tf_op jit(solution)/shard_map/reduce_scatter | solution.py:222
  457.0 7.8 copy-start.22
  468.2 476.6 %reduce-scatter.18.cloned.1.call-start = ((), (), s32[]{:S(2)}) async-start(), calls=%async_computation.18 | async-start | bytes 18874368 | tf_op jit(solution)/shard_map/reduce_scatter | solution.py:347
  484.5 101.4 %copy-start.4 = (f32[256,2,768]{2,1,0:T(2,128)S(1)}, f32[256,2,768]{2,1,0:T(2,128)}, u32[]{:S(2)}) copy-start(f32[256,2,768]{2,1,0:T(2,128)} %param.29) | copy-start | bytes 4718596
  490.2 8.9 copy-start.15
  591.7 4.7 copy-start.5
  596.4 227.5 %copy-start.14 = (bf16[128,2048]{1,0:T(8,128)(2,1)S(1)}, bf16[128,2048]{1,0:T(8,128)(2,1)}, u32[]{:S(2)}) copy-start(bf16[128,2048]{1,0:T(8,128)(2,1)} %param.26) | copy-start | bytes 1572868
  596.4 227.5 %copy-start.47 = (f32[1,2048]{1,0:T(1,128)S(1)}, f32[1,2048]{1,0:T(1,128)}, u32[]{:S(2)}) copy-start(f32[1,2048]{1,0:T(1,128)} %get-tuple-element.184) | copy-start | bytes 24580
  596.4 227.5 %copy-start.48 = (f32[1,2048]{1,0:T(1,128)S(1)}, f32[1,2048]{1,0:T(1,128)}, u32[]{:S(2)}) copy-start(f32[1,2048]{1,0:T(1,128)} %get-tuple-element.189) | copy-start | bytes 24580
  823.9 48.9 %copy-start.54 = (f32[2,768]{1,0:T(2,128)S(1)}, f32[2,768]{1,0:T(2,128)}, u32[]{:S(2)}) copy-start(f32[2,768]{1,0:T(2,128)} %param.37) | copy-start | bytes 18436
  823.9 48.9 %copy-start.55 = (f32[2,768]{1,0:T(2,128)S(1)}, f32[2,768]{1,0:T(2,128)}, u32[]{:S(2)}) copy-start(f32[2,768]{1,0:T(2,128)} %param.44) | copy-start | bytes 18436
  823.9 49.5 %copy-start.50 = (f32[2048]{0:T(1024)S(1)}, f32[2048]{0:T(1024)}, u32[]{:S(2)}) copy-start(f32[2048]{0:T(1024)} %param.40) | copy-start | bytes 24580
  823.9 49.5 %copy-start.51 = (f32[2048]{0:T(1024)S(1)}, f32[2048]{0:T(1024)}, u32[]{:S(2)}) copy-start(f32[2048]{0:T(1024)} %param.47) | copy-start | bytes 24580
  824.0 50.1 %copy-start.44 = (f32[6,2048]{1,0:T(8,128)S(1)}, f32[6,2048]{1,0:T(8,128)}, u32[]{:S(2)}) copy-start(f32[6,2048]{1,0:T(8,128)} %param.35) | copy-start | bytes 147460
  824.0 50.1 %copy-start.45 = (f32[6,2048]{1,0:T(8,128)S(1)}, f32[6,2048]{1,0:T(8,128)}, u32[]{:S(2)}) copy-start(f32[6,2048]{1,0:T(8,128)} %param.42) | copy-start | bytes 147460
  824.0 50.1 %copy-start.46 = (f32[6,2048]{1,0:T(8,128)S(1)}, f32[6,2048]{1,0:T(8,128)}, u32[]{:S(2)}) copy-start(f32[6,2048]{1,0:T(8,128)} %param.49) | copy-start | bytes 147460
  824.0 120.8 %copy-start.1 = (f32[256,2048]{1,0:T(8,128)S(1)}, f32[256,2048]{1,0:T(8,128)}, u32[]{:S(2)}) copy-start(f32[256,2048]{1,0:T(8,128)} %param.32) | copy-start | bytes 6291460
  853.0 98.7 %copy-start.52 = (f32[2048]{0:T(1024)}, f32[2048]{0:T(1024)S(1)}, u32[]{:S(2)}) copy-start(f32[2048]{0:T(1024)S(1)} %get-tuple-element.145) | copy-start | bytes 24580
  853.0 98.7 %copy-start.56 = (f32[2,768]{1,0:T(2,128)}, f32[2,768]{1,0:T(2,128)S(1)}, u32[]{:S(2)}) copy-start(f32[2,768]{1,0:T(2,128)S(1)} %get-tuple-element.144) | copy-start | bytes 18436
  872.8 78.9 %copy-start.42 = (f32[6,2048]{1,0:T(8,128)}, f32[6,2048]{1,0:T(8,128)S(1)}, u32[]{:S(2)}) copy-start(f32[6,2048]{1,0:T(8,128)S(1)} %psum.31) | copy-start | bytes 147460
  (16 other events, 25.4 us)
Sparse Core Ops, SparseCore 0:
  9.6 48.3 all-gather.6
  60.5 53.0 all-gather.12
  115.1 45.6 all-gather.16
  173.5 114.9 reduce-scatter.19
  290.8 45.3 all-gather.8
  338.6 27.7 all-gather.10
  368.9 65.0 all-gather.14
  437.4 52.7 reduce-scatter.15
  493.7 92.0 reduce-scatter.13
  588.0 76.7 reduce-scatter.9
  667.1 77.2 reduce-scatter.11
  746.6 77.2 reduce-scatter.7
  828.0 116.7 reduce-scatter.17
where the time goes:
time: 969 us; the launch traced here: 959 us
  waiting for transfers between devices  683 us (70%)
  matrix products  115 us (12%)
  other arithmetic  49.4 us (5%)
  blocking collectives  44.4 us (5%)
  local copies, waits for them, and re-layouts  41.9 us (4%)
  between operations  15.3 us (2%)
    reduce_scatter x1, waiting for transfers between devices, per_device(): lax.psum_scatter(contract_part, 'fsdp', scatter_dimension=0, tiled=True)  112 us
    reduce_scatter x1, waiting for transfers between devices, per_device(): lax.psum_scatter(qkv_part, 'fsdp', scatter_dimension=0, tiled=True)  85.7 us
    reduce_scatter x1, waiting for transfers between devices, per_device(): lax.psum_scatter(mlp_norm_grad, 'tensor', scatter_dimension=0, tiled=True)  79.6 us
    reduce_scatter x1, waiting for transfers between devices, per_device(): lax.psum_scatter(contract_cols(attended, full_dense) + contract_cols(gelu...  77.2 us
    reduce_scatter x1, waiting for transfers between devices, per_device(): lax.psum_scatter(expand_part, 'fsdp', scatter_dimension=0, tiled=True)  70 us
    reduce_scatter x1, waiting for transfers between devices, per_device(): lax.psum_scatter(attn_norm_grad, 'tensor', scatter_dimension=0, tiled=True)  66 us
    all_gather x1, waiting for transfers between devices, per_device(): lax.all_gather(shards_bf[2], 'fsdp', axis=0, tiled=True)  52.6 us
    all_gather x1, waiting for transfers between devices, per_device(): lax.all_gather(inputs, 'tensor', axis=0, tiled=True)  45.8 us
  transfers between devices with their start and end apart: 17, of which 14 were waited for; matrix products, arithmetic and copies ran while one was open for 19% of the time, Pallas kernels for 0%

commit v1 on v0

--- a/solution.py
+++ b/solution.py
@@ -111,7 +111,7 @@
     )
 
 
-def per_device(
+def per_device_generic(
     inputs,
     cotangent,
     segments,
@@ -431,7 +431,408 @@
     )
 
 
+def send(value, axis, pairs):
+    return lax.ppermute(value, axis, pairs)
+
+
+def product(left, right):
+    return jnp.dot(left, right, preferred_element_type=jnp.float32)
+
+
+def relative_features(value, chip):
+    width = value.shape[-1] // 4
+    blocks = [
+        lax.dynamic_slice_in_dim(value, (chip ^ r) * width, width, axis=value.ndim - 1)
+        for r in range(4)
+    ]
+    return jnp.concatenate(blocks, axis=-1)
+
+
+def per_device_paired(
+    inputs,
+    cotangent,
+    segments,
+    positions,
+    qkv_weight,
+    qkv_bias,
+    dense_weight,
+    expand_weight,
+    expand_bias,
+    contract_weight,
+    norm_bias_vectors,
+    moment_qkv_weight,
+    moment_qkv_bias,
+    moment_dense_weight,
+    moment_expand_weight,
+    moment_expand_bias,
+    moment_contract_weight,
+    moment_norm_vectors,
+    second_qkv_weight,
+    second_qkv_bias,
+    second_dense_weight,
+    second_expand_weight,
+    second_expand_bias,
+    second_contract_weight,
+    second_norm_vectors,
+):
+    bf16, f32 = jnp.bfloat16, jnp.float32
+    fsdp_index = lax.axis_index("fsdp")
+    z = lax.axis_index("tensor")
+    n_z = lax.axis_size("tensor")
+    core = fsdp_index % 2
+    chip = fsdp_index // 2
+    devices = range(lax.axis_size("fsdp"))
+    to_core = [(i, i ^ 1) for i in devices]
+    to_x = [(i, i ^ 2) for i in devices]
+    to_y = [(i, i ^ 4) for i in devices]
+    to_next = [(i, i + 2) for i in devices if i + 2 < len(devices)]
+    to_prev = [(i + 2, i) for i in devices if i + 2 < len(devices)]
+    first = core == 0
+    head_dim = qkv_weight.shape[2] // 3
+    score_scale = head_dim ** (-0.5)
+    shard_rows = inputs.shape[0]
+    group_rows = n_z * shard_rows
+    hidden = expand_weight.shape[1] // 2
+    qkv_cols = 3 * head_dim
+    shard_feat = expand_weight.shape[0]
+    chip_feat = 2 * shard_feat
+
+    def half_columns(k):
+        return (
+            lax.dynamic_slice_in_dim(expand_weight, k * hidden, hidden, axis=1).astype(bf16),
+            jnp.concatenate(
+                [
+                    lax.dynamic_index_in_dim(qkv_weight, k, axis=1, keepdims=False),
+                    lax.dynamic_slice_in_dim(dense_weight, k * head_dim, head_dim, axis=1),
+                ],
+                axis=1,
+            ).astype(bf16),
+            lax.dynamic_slice_in_dim(contract_weight, k * hidden, hidden, axis=1).astype(bf16),
+        )
+
+    def rows_of_chip(own, other):
+        return jnp.concatenate(
+            [jnp.where(first, own, other), jnp.where(first, other, own)], axis=0
+        )
+
+    x_rel = relative_features(inputs, chip)
+    dy_rel = relative_features(cotangent, chip)
+    vectors = relative_features(norm_bias_vectors, chip)
+
+    def gather_tokens(own):
+        pieces = [own]
+        for k in range(1, n_z):
+            pieces.append(send(own, "tensor", [(i, (i + k) % n_z) for i in range(n_z)]))
+        return jnp.concatenate(pieces, axis=0)
+
+    mine = half_columns(core)
+    theirs = half_columns(1 - core)
+    gathered = []
+    for own, other in zip(mine, theirs):
+        block = rows_of_chip(own, send(other, "fsdp", to_core))
+        from_x = send(block, "fsdp", to_x)
+        from_y = send(block, "fsdp", to_y)
+        diag_top = send(from_y[:shard_feat], "fsdp", to_x)
+        diag_bottom = send(from_x[shard_feat:], "fsdp", to_y)
+        gathered.append(jnp.concatenate([block, from_x, from_y, diag_top, diag_bottom], axis=0))
+    full_expand, full_qd, full_contract = gathered
+    full_qkv = full_qd[:, :qkv_cols]
+    full_dense = full_qd[:, qkv_cols:]
+
+    x_group = gather_tokens(x_rel)
+    dy_group = gather_tokens(dy_rel)
+    x_all = jnp.concatenate([x_group, send(x_group, "fsdp", to_core)], axis=0)
+    dy_all = jnp.concatenate([dy_group, send(dy_group, "fsdp", to_core)], axis=0)
+
+    local = jnp.arange(group_rows, dtype=jnp.int32)
+    order = ((z - local // shard_rows) % n_z) * shard_rows + local % shard_rows
+
+    def token_block(values, start):
+        blocks = [
+            lax.dynamic_slice_in_dim(
+                values, start + ((z - k) % n_z) * shard_rows, shard_rows
+            )
+            for k in range(n_z)
+        ]
+        return jnp.concatenate(blocks)
+
+    chip_start = chip * 2 * group_rows
+    prev_start = jnp.maximum(chip_start - group_rows, 0)
+    seg_first = token_block(segments, chip_start)
+    seg_second = token_block(segments, chip_start + group_rows)
+    seg_halo = token_block(segments, prev_start)
+    position_other = send(positions, "fsdp", to_core)
+    position_all = jnp.concatenate([token_block(positions, 0), token_block(position_other, 0)])
+
+    xhat, inverse_deviation = normalized_row_block(x_all.astype(f32))
+    xa = (xhat * vectors[0] + vectors[1]).astype(bf16)
+    xm = (xhat * vectors[2] + vectors[3]).astype(bf16)
+
+    expand_bias_half = lax.dynamic_slice_in_dim(expand_bias, core * hidden, hidden)
+    expand_pre = product(xm, full_expand) + expand_bias_half
+    activated = jax.nn.gelu(expand_pre, approximate=False).astype(bf16)
+
+    head_bias = lax.dynamic_index_in_dim(qkv_bias, core, axis=0, keepdims=False)
+    projected = (product(xa, full_qkv) + head_bias)[:, None, :]
+    cosines, sines = rotary_tables(position_all)
+    queries = rotate(projected[..., :head_dim], cosines, sines, 1.0)[:, 0].astype(bf16)
+    keys = rotate(projected[..., head_dim : 2 * head_dim], cosines, sines, 1.0)[:, 0].astype(bf16)
+    values = projected[:, 0, 2 * head_dim :].astype(bf16)
+    kv = jnp.concatenate([keys, values], axis=1)
+    kv_own, kv_other = kv[:group_rows], kv[group_rows:]
+    kv_halo = send(jnp.where(first, kv_other, kv_own), "fsdp", to_next)
+    kv_blocks = jnp.stack(
+        [
+            jnp.concatenate([jnp.where(first, kv_halo, kv_other), kv_own], axis=0),
+            jnp.concatenate([jnp.where(first, kv_own, kv_halo), kv_other], axis=0),
+        ]
+    )
+    keys_blocks, values_blocks = kv_blocks[..., :head_dim], kv_blocks[..., head_dim:]
+    seg_own = jnp.where(first, seg_first, seg_second)
+    seg_other = jnp.where(first, seg_second, seg_first)
+    seg_keys = jnp.stack(
+        [
+            jnp.concatenate([jnp.where(first, seg_halo, seg_first), seg_own]),
+            jnp.concatenate([jnp.where(first, seg_first, seg_halo), seg_other]),
+        ]
+    )
+    seg_queries = jnp.stack([seg_own, seg_other])
+    key_order = jnp.concatenate([order, order + group_rows])
+    causal = key_order[None, :] <= (order + group_rows)[:, None]
+    halo_block = jnp.stack([first, ~first])
+    present = (
+        (jnp.arange(2 * group_rows) >= group_rows)[None, :]
+        | ~halo_block[:, None]
+        | (chip > 0)
+    )
+    allowed = (
+        causal[None] & (seg_queries[:, :, None] == seg_keys[:, None, :]) & present[:, None, :]
+    )
+    query_blocks = queries.reshape(2, group_rows, head_dim)
+    scores = (
+        jnp.einsum("bqc,bkc->bqk", query_blocks, keys_blocks, preferred_element_type=f32)
+        * score_scale
+    )
+    scores = jnp.where(allowed, scores, masked_score)
+    row_max = jnp.max(scores, axis=-1, keepdims=True)
+    log_total = row_max + jnp.log(jnp.sum(jnp.exp(scores - row_max), axis=-1, keepdims=True))
+    probs = jnp.exp(scores - log_total)
+    probs_bf = probs.astype(bf16)
+    attended_blocks = jnp.einsum(
+        "bqk,bkc->bqc", probs_bf, values_blocks, preferred_element_type=f32
+    ).astype(bf16)
+    attended = attended_blocks.reshape(2 * group_rows, head_dim)
+
+    def reduce_features(rows_left, rows_right):
+        def block(r):
+            parts = [
+                contract_rows(left[:, r * chip_feat : (r + 1) * chip_feat], right)
+                for left, right in zip(rows_left, rows_right)
+            ]
+            return parts[0] if len(parts) == 1 else jnp.concatenate(parts, axis=1)
+
+        diag = block(3).astype(bf16)
+        from_x = send(diag[:shard_feat], "fsdp", to_x)
+        from_y = send(diag[shard_feat:], "fsdp", to_y)
+        zero = jnp.zeros_like(from_x)
+        for_x = (block(1) + jnp.concatenate([zero, from_y], axis=0).astype(f32)).astype(bf16)
+        for_y = (block(2) + jnp.concatenate([from_x, zero], axis=0).astype(f32)).astype(bf16)
+        got_x = send(for_x, "fsdp", to_x)
+        got_y = send(for_y, "fsdp", to_y)
+        own = block(0) + got_x.astype(f32) + got_y.astype(f32)
+        kept = lax.dynamic_slice_in_dim(own, core * shard_feat, shard_feat, axis=0)
+        given = lax.dynamic_slice_in_dim(own, (1 - core) * shard_feat, shard_feat, axis=0)
+        taken = send(given, "fsdp", to_core)
+        return jnp.where(first, kept, taken), jnp.where(first, taken, kept)
+
+    def reduce_tokens(part):
+        other = send(part[group_rows:].astype(bf16), "fsdp", to_core)
+        rows = part[:group_rows] + other.astype(f32)
+        total = rows[:shard_rows]
+        for k in range(1, n_z):
+            piece = rows[k * shard_rows : (k + 1) * shard_rows].astype(bf16)
+            total = total + send(
+                piece, "tensor", [(i, (i - k) % n_z) for i in range(n_z)]
+            ).astype(f32)
+        return total
+
+    contract_halves = reduce_features([dy_all], [activated])
+
+    act_grad = product(dy_all, full_contract)
+    pre_grad32 = act_grad * gelu_slope(expand_pre)
+    pre_grad = pre_grad32.astype(bf16)
+    expand_bias_part = jnp.sum(pre_grad32, axis=0)
+    expand_halves = reduce_features([xm], [pre_grad])
+
+    attn_grad = product(dy_all, full_dense).astype(bf16)
+    row_delta = jnp.sum(attn_grad.astype(f32) * attended.astype(f32), axis=-1)
+    grad_blocks = attn_grad.reshape(2, group_rows, head_dim)
+    dot_grad = jnp.einsum("bqc,bkc->bqk", grad_blocks, values_blocks, preferred_element_type=f32)
+    score_grad = (
+        probs * (dot_grad - row_delta.reshape(2, group_rows, 1)) * score_scale
+    ).astype(bf16)
+    query_grad = jnp.einsum(
+        "bqk,bkc->bqc", score_grad, keys_blocks, preferred_element_type=f32
+    ).reshape(2 * group_rows, head_dim)
+    key_parts = jnp.einsum("bqk,bqc->bkc", score_grad, query_blocks, preferred_element_type=f32)
+    value_parts = jnp.einsum("bqk,bqc->bkc", probs_bf, grad_blocks, preferred_element_type=f32)
+    kv_parts = jnp.concatenate([key_parts, value_parts], axis=2)
+    before_own, after_own = kv_parts[0, :group_rows], kv_parts[0, group_rows:]
+    before_other, after_other = kv_parts[1, :group_rows], kv_parts[1, group_rows:]
+    from_later = send(jnp.where(first, before_own, before_other), "fsdp", to_prev)
+    kv_grad = jnp.concatenate(
+        [
+            after_own + jnp.where(first, before_other, from_later),
+            after_other + jnp.where(first, from_later, before_own),
+        ],
+        axis=0,
+    )
+    qkv_grad32 = jnp.concatenate(
+        [
+            rotate(query_grad[:, None, :], cosines, sines, -1.0)[:, 0],
+            rotate(kv_grad[:, None, :head_dim], cosines, sines, -1.0)[:, 0],
+            kv_grad[:, head_dim:],
+        ],
+        axis=-1,
+    )
+    qkv_grad = qkv_grad32.astype(bf16)
+    qkv_bias_part = jnp.sum(qkv_grad32, axis=0)
+    qd_halves = reduce_features([xa, dy_all], [qkv_grad, attended])
+
+    branch_part = contract_cols(attended, full_dense) + contract_cols(activated, full_contract)
+    branch_sum = reduce_tokens(branch_part)
+    output = relative_features(
+        x_rel.astype(f32) + branch_sum + vectors[4] + vectors[5], chip
+    )
+    attn_back = contract_cols(qkv_grad, full_qkv)
+    mlp_back = contract_cols(pre_grad, full_expand)
+    weighted = reduce_tokens(attn_back * vectors[0] + mlp_back * vectors[2])
+    xhat_own, inverse_own = xhat[:shard_rows], inverse_deviation[:shard_rows]
+    input_gradient = dy_rel.astype(f32) + inverse_own * (
+        weighted
+        - jnp.mean(weighted, axis=-1, keepdims=True)
+        - xhat_own * jnp.mean(weighted * xhat_own, axis=-1, keepdims=True)
+    )
+    block_input_gradient = relative_features(input_gradient, chip)
+
+    vector_part = relative_features(
+        jnp.stack(
+            [
+                jnp.sum(attn_back * xhat, axis=0),
+                jnp.sum(attn_back, axis=0),
+                jnp.sum(mlp_back * xhat, axis=0),
+                jnp.sum(mlp_back, axis=0),
+                jnp.sum(dy_rel.astype(f32), axis=0),
+            ]
+        ),
+        chip,
+    )
+    bias_part = jnp.concatenate([qkv_bias_part, expand_bias_part])
+    n_vector = vector_part.size
+    small = jnp.concatenate([vector_part.reshape(-1), bias_part]).reshape(-1, 128)
+    small = small + send(small, "fsdp", to_x)
+    small = small + send(small, "fsdp", to_y)
+    small_other = send(small, "fsdp", to_core)
+    flat, flat_other = small.reshape(-1), small_other.reshape(-1)
+    vector_sum = (flat[:n_vector] + flat_other[:n_vector]).reshape(-1, 128)
+    for bit in (1, 2):
+        vector_sum = vector_sum + send(
+            vector_sum, "tensor", [(i, i ^ bit) for i in range(n_z)]
+        )
+    vector_sum = vector_sum.reshape(vector_part.shape)
+    grad_norm_vectors = jnp.concatenate([vector_sum, vector_sum[4:]], axis=0)
+    bias_first = jnp.where(first, flat[n_vector:], flat_other[n_vector:])
+    bias_second = jnp.where(first, flat_other[n_vector:], flat[n_vector:])
+    grad_qkv_bias = jnp.stack([bias_first[:qkv_cols], bias_second[:qkv_cols]])
+    grad_expand_bias = jnp.concatenate([bias_first[qkv_cols:], bias_second[qkv_cols:]])
+
+    grad_contract_weight = jnp.concatenate(contract_halves, axis=1)
+    grad_expand_weight = jnp.concatenate(expand_halves, axis=1)
+    grad_qkv_weight = jnp.stack([part[:, :qkv_cols] for part in qd_halves], axis=1)
+    grad_dense_weight = jnp.concatenate([part[:, qkv_cols:] for part in qd_halves], axis=1)
+    new_qkv_weight, new_moment_qkv_weight, new_second_qkv_weight = adam_step(
+        qkv_weight,
+        grad_qkv_weight,
+        moment_qkv_weight,
+        second_qkv_weight,
+        rate_qkv_weight,
+        decay_matrix,
+    )
+    new_qkv_bias, new_moment_qkv_bias, new_second_qkv_bias = adam_step(
+        qkv_bias, grad_qkv_bias, moment_qkv_bias, second_qkv_bias, rate_qkv_bias, 0.0
+    )
+    new_dense_weight, new_moment_dense_weight, new_second_dense_weight = adam_step(
+        dense_weight,
+        grad_dense_weight,
+        moment_dense_weight,
+        second_dense_weight,
+        rate_dense_weight,
+        decay_matrix,
+    )
+    new_expand_weight, new_moment_expand_weight, new_second_expand_weight = adam_step(
+        expand_weight,
+        grad_expand_weight,
+        moment_expand_weight,
+        second_expand_weight,
+        rate_expand_weight,
+        decay_matrix,
+    )
+    new_expand_bias, new_moment_expand_bias, new_second_expand_bias = adam_step(
+        expand_bias, grad_expand_bias, moment_expand_bias, second_expand_bias, rate_expand_bias, 0.0
+    )
+    new_contract_weight, new_moment_contract_weight, new_second_contract_weight = adam_step(
+        contract_weight,
+        grad_contract_weight,
+        moment_contract_weight,
+        second_contract_weight,
+        rate_contract_weight,
+        decay_matrix,
+    )
+    new_norm_vectors, new_moment_norm_vectors, new_second_norm_vectors = adam_step(
+        norm_bias_vectors,
+        grad_norm_vectors,
+        moment_norm_vectors,
+        second_norm_vectors,
+        rate_norm_vectors,
+        0.0,
+    )
+    return (
+        output,
+        block_input_gradient,
+        grad_qkv_weight,
+        new_qkv_weight,
+        new_moment_qkv_weight,
+        new_second_qkv_weight,
+        grad_qkv_bias,
+        new_qkv_bias,
+        new_moment_qkv_bias,
+        new_second_qkv_bias,
+        grad_dense_weight,
+        new_dense_weight,
+        new_moment_dense_weight,
+        new_second_dense_weight,
+        grad_expand_weight,
+        new_expand_weight,
+        new_moment_expand_weight,
+        new_second_expand_weight,
+        grad_expand_bias,
+        new_expand_bias,
+        new_moment_expand_bias,
+        new_second_expand_bias,
+        grad_contract_weight,
+        new_contract_weight,
+        new_moment_contract_weight,
+        new_second_contract_weight,
+        grad_norm_vectors,
+        new_norm_vectors,
+        new_moment_norm_vectors,
+        new_second_norm_vectors,
+    )
+
+
 def solution(mesh):
+    paired = mesh.shape["fsdp"] == 8 and mesh.shape["tensor"] == 4
+    per_device = per_device_paired if paired else per_device_generic
     return jax.shard_map(
         per_device,
         mesh=mesh,

time: 969 us -> 522 us (0.54)
  waiting for transfers between devices: 683 us -> 170 us
  starting transfers between devices: 9.34 us -> 87.9 us
  blocking collectives: 44.4 us -> 0 us
  other arithmetic: 49.4 us -> 81.5 us
  local copies, waits for them, and re-layouts: 41.9 us -> 68.9 us
  between operations: 15.3 us -> 2.83 us
    reduce_scatter x7 -> x0, waiting for transfers between devices: 496 us -> none  [the longest x1 112 us: per_device(): lax.psum_scatter(contract_part, 'fsdp', scatter_dimension=0, tiled=True)]
    all_gather x6 -> x0, waiting for transfers between devices: 181 us -> none  [the longest x1 52.6 us: per_device(): lax.all_gather(shards_bf[2], 'fsdp', axis=0, tiled=True)]
    ppermute x4 -> x54, waiting for transfers between devices: 4.4 us -> 170 us  [send(): return lax.ppermute(value, axis, pairs)]
    ppermute x4 -> x54, starting transfers between devices: 8.39 us -> 87.9 us  [send(): return lax.ppermute(value, axis, pairs)]
    psum x2 -> x0, blocking collectives: 44.4 us -> none  [the longest x1 24.6 us: per_device(): lax.psum((qkv_bias_part, expand_bias_part, vector_part), 'fsdp')]
    dot_general x12 -> x10, matrix products: 67.9 us -> 39.5 us  [the longest x4 29.1 us: product(): return jnp.dot(left, right, preferred_element_type=jnp.float32)]
    concatenate x2 -> x14, other arithmetic: 1.44 us -> 15.2 us  [the longest x2 7.38 us: gather_tokens(): return jnp.concatenate(pieces, axis=0)]
    sub x7, other arithmetic: 23.8 us -> 12.6 us  [adam_step(): parameter - step_rate * (moment_hat / (jnp.sqrt(second_hat) + adam_eps) +...]
  transfers between devices with their start and end apart: 17 -> 54, of which waited for: 14 -> 22; matrix products, arithmetic and copies ran while one was open for 19% -> 40% of each run, Pallas kernels for 0% -> 0%
where the time goes in v1:
time: 522 us; the launch traced here: 517 us
  waiting for transfers between devices  170 us (33%)
  matrix products  106 us (20%)
  starting transfers between devices  87.9 us (17%)
  other arithmetic  81.5 us (16%)
  local copies, waits for them, and re-layouts  68.9 us (13%)
    ppermute x54, waiting for transfers between devices, send(): return lax.ppermute(value, axis, pairs)  170 us
    ppermute x54, starting transfers between devices, send(): return lax.ppermute(value, axis, pairs)  87.9 us
    unnamed x247, local copies, waits for them, and re-layouts  40.6 us
    dot_general x16, matrix products, contract_rows(): lax.dot_general(left_rows, right_rows, (((0,), (0,)), ((), ())), preferre...  37.2 us
    dot_general x4, matrix products, contract_cols(): lax.dot_general(left_cols, right_cols, (((1,), (1,)), ((), ())), preferre...  29.4 us
    dot_general x4, matrix products, product(): return jnp.dot(left, right, preferred_element_type=jnp.float32)  29.1 us
    sub x7, other arithmetic, adam_step(): parameter - step_rate * (moment_hat / (jnp.sqrt(second_hat) + adam_eps) +...  12.6 us
  transfers between devices with their start and end apart: 54, of which 22 were waited for; matrix products, arithmetic and copies ran while one was open for 40% of the time, Pallas kernels for 0%

profile of v1, /device:TPU:0, one launch (start us, length us, event | category | flops | bytes accessed | tf_op | source)
XLA Modules:
  0.0 516.9 jit_solution(16333777874485157798)
XLA Ops:
  3.7 5.1 collective-permute-start.27
  9.8 2.4 copy.55
  36.5 2.2 pad_maximum_fusion.14
  54.1 2.9 collective-permute-start.2
  61.2 18.0 %collective-permute-done = bf16[128,2048]{1,0:T(8,128)(2,1)S(1)} collective-permute-done((bf16[128,2048]{1,0:T(8,128)(2,1)S(1)}, bf16[128,2048]{1,0:T(8,128)(2,1)S(1)}, u32[]{:S(2)}, u32[]{:S(2)}) %collective-permute-start) | collective-permute-done | bytes 524320 | tf_op jit(solution)/shard_map/ppermute | solution.py:435
  80.9 7.6 %collective-permute-done.1 = bf16[128,2048]{1,0:T(8,128)(2,1)S(1)} collective-permute-done((bf16[128,2048]{1,0:T(8,128)(2,1)S(1)}, bf16[128,2048]{1,0:T(8,128)(2,1)S(1)}, u32[]{:S(2)}, u32[]{:S(2)}) %collective-permute-start.1) | collective-permute-done | bytes 524320 | tf_op jit(solution)/shard_map/ppermute | solution.py:435
  90.1 3.0 collective-permute-done.2
  94.7 3.3 pad_maximum_fusion
  100.2 5.1 collective-permute-done.5
  106.4 4.1 pad_maximum_fusion.1
  110.5 3.9 collective-permute-done.18
  116.0 11.7 %collective-permute-done.17 = bf16[512,1024]{1,0:T(8,128)(2,1)S(1)} collective-permute-done((bf16[512,1024]{1,0:T(8,128)(2,1)S(1)}, bf16[512,1024]{1,0:T(8,128)(2,1)S(1)}, u32[]{:S(2)}, u32[]{:S(2)}) %collective-permute-start.17) | collective-permute-done | bytes 1048608 | tf_op jit(solution)/shard_map/ppermute | solution.py:435
  129.6 7.3 %collective-permute-done.13 = bf16[512,1024]{1,0:T(8,128)(2,1)S(1)} collective-permute-done((bf16[512,1024]{1,0:T(8,128)(2,1)S(1)}, bf16[512,1024]{1,0:T(8,128)(2,1)S(1)}, u32[]{:S(2)}, u32[]{:S(2)}) %collective-permute-start.13) | collective-permute-done | bytes 1048608 | tf_op jit(solution)/shard_map/ppermute | solution.py:435
  138.4 11.8 %collective-permute-done.12 = bf16[512,1024]{1,0:T(8,128)(2,1)S(1)} collective-permute-done((bf16[512,1024]{1,0:T(8,128)(2,1)S(1)}, bf16[512,1024]{1,0:T(8,128)(2,1)S(1)}, u32[]{:S(2)}, u32[]{:S(2)}) %collective-permute-start.12) | collective-permute-done | bytes 1048608 | tf_op jit(solution)/shard_map/ppermute | solution.py:435
  151.8 9.6 %collective-permute-done.7 = bf16[256,1024]{1,0:T(8,128)(2,1)S(1)} collective-permute-done((bf16[256,1024]{1,0:T(8,128)(2,1)S(1)}, bf16[256,1024]{1,0:T(8,128)(2,1)S(1)}, u32[]{:S(2)}, u32[]{:S(2)}) %collective-permute-start.7) | collective-permute-done | bytes 524320 | tf_op jit(solution)/shard_map/ppermute | solution.py:435
  164.7 7.9 %collective-permute-done.19 = bf16[256,1024]{1,0:T(8,128)(2,1)S(1)} collective-permute-done((bf16[256,1024]{1,0:T(8,128)(2,1)S(1)}, bf16[256,1024]{1,0:T(8,128)(2,1)S(1)}, u32[]{:S(2)}, u32[]{:S(2)}) %collective-permute-start.19) | collective-permute-done | bytes 524320 | tf_op jit(solution)/shard_map/ppermute | solution.py:435
  172.8 8.3 %collective-permute-done.14 = bf16[256,1024]{1,0:T(8,128)(2,1)S(1)} collective-permute-done((bf16[256,1024]{1,0:T(8,128)(2,1)S(1)}, bf16[256,1024]{1,0:T(8,128)(2,1)S(1)}, u32[]{:S(2)}, u32[]{:S(2)}) %collective-permute-start.14) | collective-permute-done | bytes 524320 | tf_op jit(solution)/shard_map/ppermute | solution.py:435
  184.5 3.2 add_convert_fusion.1
  187.7 5.2 %fusion.169 = (bf16[1024,1,768]{0,2,1:T(8,128)(2,1)S(1)}, f32[1024,1,768]{0,2,1:T(8,128)}) fusion(f32[768]{0:T(1024)S(1)} %fusion.132, bf16[1024,2048]{1,0:T(8,128)(2,1)S(1)} %get-tuple-element.121, bf16[2048,1024]{1,0:T(8,128)(2,1)S(1)} %constant_dynamic-update-slice_fusion.5), kind=kOutput, calls=%fused_computation.409 | convolution fusion | flops 3222798336 | bytes 12062720 | tf_op jit(solution)/shard_map/dot_general | solution.py:439
  193.8 14.8 %fusion.5 = (bf16[1024,1024]{1,0:T(8,128)(2,1)S(1)}, f32[1024,1024]{1,0:T(8,128)S(1)}) fusion(f32[1024]{0:T(1024)S(1)} %dynamic_slice.217, bf16[1024,2048]{1,0:T(8,128)(2,1)S(1)} %get-tuple-element.122, bf16[2048,1024]{1,0:T(8,128)(2,1)} %copy-done.75), kind=kOutput, calls=%fused_computation.21 | convolution fusion | flops 4364173312 | bytes 14684160 | tf_op jit(solution)/shard_map/dot_general | solution.py:439
  208.9 4.2 copy-done.77
  213.1 6.3 %fusion.161 = (f32[1024]{0:T(1024)S(1)}, bf16[1024,1024]{1,0:T(8,128)(2,1)S(1)}) fusion(f32[1024,1024]{1,0:T(8,128)S(1)} %get-tuple-element.211, f32[1024]{0:T(1024)S(1)} %dynamic_slice.217, bf16[1024,2048]{1,0:T(8,128)(2,1)S(1)} %constant_dynamic-update-slice_fusion.24, bf16[2048,1024]{1,0:T(8,128)(2,1)S(1)} %copy-done.77), kind=kOutput, calls=%fused_computation.401 | convolution fusion | flops 4307549184 | bytes 14688256 | tf_op jit(solution)/shard_map/dot_general | solution.py:439
  219.4 2.2 convolution_convert_fusion.1
  221.6 2.6 fusion.52
  225.6 6.9 %fusion.171 = f32[1024,2048]{1,0:T(8,128)} fusion(bf16[1024,1024]{1,0:T(8,128)(2,1)S(1)} %get-tuple-element.210, bf16[2048,1024]{1,0:T(8,128)(2,1)S(1)} %copy-done.77), kind=kOutput, calls=%fused_computation.411 | convolution fusion | flops 4294967296 | bytes 14680064 | tf_op jit(solution)/shard_map/dot_general | solution.py:109
  232.5 2.3 fusion.118
  235.7 2.2 convert_element_type.174
  240.8 3.8 collective-permute-start.10
  250.7 2.6 fusion.78
  253.4 3.1 collective-permute-done.10
  260.5 2.7 multiply_reduce_fusion.3
  263.3 3.1 multiply_convert_fusion
  273.0 3.3 fusion.86
  279.7 3.3 add_convert_fusion.2
  283.0 3.1 collective-permute-start.50
  286.1 3.3 add_convert_fusion.3
  291.0 3.4 add_convert_fusion.4
  294.6 3.4 add_convert_fusion.5
  298.5 2.5 convolution_add_fusion
  313.5 5.8 %fusion.20 = f32[1024,2048]{1,0:T(8,128)} fusion(bf16[1024,768]{0,1:T(8,128)(2,1)S(1)} %fusion.85, bf16[2048,1024]{1,0:T(8,128)(2,1)S(1)} %copy-done.66), kind=kOutput, calls=%fused_computation.57 | convolution fusion | flops 3221225472 | bytes 13107200 | tf_op jit(solution)/shard_map/dot_general | solution.py:109
  319.3 14.2 %fusion.146 = (f32[2048]{0:T(1024)S(1)}, f32[2048]{0:T(1024)S(1)}, f32[1024,2048]{1,0:T(8,128)}, f32[2048]{0:T(1024)S(1)}, f32[2048]{0:T(1024)S(1)}, /*index=5*/f32[1024,2048]{1,0:T(8,128)}) fusion(f32[1024]{0:T(1024)S(1)} %add_rsqrt_fusion, f32[1024]{0:T(1024)S(1)} %broadcast_multiply_fusion, bf16[1024,2048]{1,0:T(8,128)(2,1)S(1)} %copy-done.3, ...), kind=kOutput, calls=%fused_computation.396 | convolution fusion | flops 4320124928 | bytes 35708928 | tf_op jit(solution)/shard_map/dot_general | solution.py:109
  336.1 2.6 convolution_convert_fusion.2
  351.3 2.2 fusion.57
  353.5 3.5 collective-permute-done.39
  362.3 3.8 slice.616
  366.2 22.9 %collective-permute-start.52 = (f32[80,128]{1,0:T(8,128)S(1)}, f32[80,128]{1,0:T(8,128)S(1)}, u32[]{:S(2)}, u32[]{:S(2)}) collective-permute-start(f32[80,128]{1,0:T(8,128)S(1)} %slice_add_fusion.4), channel_id=1, source_target_pairs={{0,1},{1,0},{2,3},{3,2},{4,5},{5,4},{6,7},{7,6},{8,9},{9,8},{10,11... | collective-permute-start | bytes 122888 | tf_op jit(solution)/shard_map/ppermute | solution.py:435
  391.3 3.7 collective-permute-start.53
  398.3 2.9 fusion.28
  402.8 2.3 fusion.27
  405.7 3.7 fusion.159
  410.5 2.6 collective-permute-start.22
  414.6 4.0 multiply_subtract_fusion.1
  419.0 7.5 %collective-permute-done.37 = bf16[512,1024]{1,0:T(8,128)(2,1)} collective-permute-done((bf16[512,1024]{1,0:T(8,128)(2,1)}, bf16[512,1024]{1,0:T(8,128)(2,1)}, u32[]{:S(2)}, u32[]{:S(2)}) %collective-permute-start.37) | collective-permute-done | bytes 1048608 | tf_op jit(solution)/shard_map/ppermute | solution.py:435
  426.6 2.9 collective-permute-start.23
  429.5 4.0 multiply_subtract_fusion
  433.6 2.2 fusion.26
  436.0 3.3 collective-permute-done.24
  439.3 20.9 %collective-permute-done.23 = bf16[128,2048]{1,0:T(8,128)(2,1)S(1)} collective-permute-done((bf16[128,2048]{1,0:T(8,128)(2,1)S(1)}, bf16[128,2048]{1,0:T(8,128)(2,1)S(1)}, u32[]{:S(2)}, u32[]{:S(2)}) %collective-permute-start.23) | collective-permute-done | bytes 524320 | tf_op jit(solution)/shard_map/ppermute | solution.py:435
  470.1 2.4 copy.74
  472.5 2.4 copy.75
  474.8 2.4 copy.76
  477.2 2.4 copy.73
  479.5 11.6 %collective-permute-done.31 = bf16[128,2048]{1,0:T(8,128)(2,1)S(1)} collective-permute-done((bf16[128,2048]{1,0:T(8,128)(2,1)S(1)}, bf16[128,2048]{1,0:T(8,128)(2,1)S(1)}, u32[]{:S(2)}, u32[]{:S(2)}) %collective-permute-start.31) | collective-permute-done | bytes 524320 | tf_op jit(solution)/shard_map/ppermute | solution.py:435
  491.2 19.6 %collective-permute-done.32 = bf16[128,2048]{1,0:T(8,128)(2,1)S(1)} collective-permute-done((bf16[128,2048]{1,0:T(8,128)(2,1)S(1)}, bf16[128,2048]{1,0:T(8,128)(2,1)S(1)}, u32[]{:S(2)}, u32[]{:S(2)}) %collective-permute-start.32) | collective-permute-done | bytes 524320 | tf_op jit(solution)/shard_map/ppermute | solution.py:435
  (464 shorter events, 156.3 us)
Async XLA Ops:
  3.7 94.4 %collective-permute-start.27 = (bf16[128,2048]{1,0:T(8,128)(2,1)S(1)}, bf16[128,2048]{1,0:T(8,128)(2,1)}, u32[]{:S(2)}, u32[]{:S(2)}) collective-permute-start(bf16[128,2048]{1,0:T(8,128)(2,1)S(1)} %get-tuple-element.91), channel_id=1, source_target_pairs={{0,3},{1,0},{2,1},{3,2},{4,7},{5,4},{6,5},{7,6},{8,11},{9,8},{10,9... | collective-permute-start | bytes 1572872 | tf_op jit(solution)/shard_map/ppermute | solution.py:435
  8.8 49.8 %collective-permute-start.26 = (bf16[128,2048]{1,0:T(8,128)(2,1)S(1)}, bf16[128,2048]{1,0:T(8,128)(2,1)}, u32[]{:S(2)}, u32[]{:S(2)}) collective-permute-start(bf16[128,2048]{1,0:T(8,128)(2,1)S(1)} %get-tuple-element.91), channel_id=1, source_target_pairs={{0,2},{1,3},{2,0},{3,1},{4,6},{5,7},{6,4},{7,5},{8,10},{9,11},{10,... | collective-permute-start | bytes 1572872 | tf_op jit(solution)/shard_map/ppermute | solution.py:435
  8.8 45.3 %collective-permute-start.25 = (bf16[128,2048]{1,0:T(8,128)(2,1)S(1)}, bf16[128,2048]{1,0:T(8,128)(2,1)}, u32[]{:S(2)}, u32[]{:S(2)}) collective-permute-start(bf16[128,2048]{1,0:T(8,128)(2,1)S(1)} %get-tuple-element.91), channel_id=1, source_target_pairs={{0,1},{1,2},{2,3},{3,0},{4,5},{5,6},{6,7},{7,4},{8,9},{9,10},{10,1... | collective-permute-start | bytes 1572872 | tf_op jit(solution)/shard_map/ppermute | solution.py:435
  9.8 31.1 %collective-permute-start.9 = (s32[512]{0:T(512)}, s32[512]{0:T(512)}, u32[]{:S(2)}, u32[]{:S(2)}) collective-permute-start(s32[512]{0:T(512)} %param.28), channel_id=1, source_target_pairs={{0,4},{4,0},{8,12},{12,8},{16,20},{20,16},{24,28},{28,24},{1,5},{5... | collective-permute-start | bytes 6152 | tf_op jit(solution)/shard_map/ppermute | solution.py:435
  14.9 32.2 %collective-permute-start.4 = (bf16[256,1024]{1,0:T(8,128)(2,1)}, bf16[256,1024]{1,0:T(8,128)(2,1)S(1)}, u32[]{:S(2)}, u32[]{:S(2)}) collective-permute-start(bf16[256,1024]{1,0:T(8,128)(2,1)} %pad_maximum_fusion.16), channel_id=1, source_target_pairs={{0,4},{4,0},{8,12},{12,8},{16,20},{20,16},{24,28},{28,24},{1,5},{5... | collective-permute-start | bytes 1572872 | tf_op jit(solution)/shard_map/ppermute | solution.py:435
  40.9 11.5 %collective-permute-start.16 = (bf16[256,1024]{1,0:T(8,128)(2,1)}, bf16[256,1024]{1,0:T(8,128)(2,1)S(1)}, u32[]{:S(2)}, u32[]{:S(2)}) collective-permute-start(bf16[256,1024]{1,0:T(8,128)(2,1)} %dynamic-slice_convert_fusion), channel_id=1, source_target_pairs={{0,4},{4,0},{8,12},{12,8},{16,20},{20,16},{24,28},{28,24},{1,5},{5... | collective-permute-start | bytes 1572872 | tf_op jit(solution)/shard_map/ppermute | solution.py:435
  47.2 3.0 collective-permute-start.11
  50.2 38.3 %collective-permute-start.1 = (bf16[128,2048]{1,0:T(8,128)(2,1)S(1)}, bf16[128,2048]{1,0:T(8,128)(2,1)S(1)}, u32[]{:S(2)}, u32[]{:S(2)}) collective-permute-start(bf16[128,2048]{1,0:T(8,128)(2,1)S(1)} %copy-done.69), channel_id=1, source_target_pairs={{0,2},{1,3},{2,0},{3,1},{4,6},{5,7},{6,4},{7,5},{8,10},{9,11},{10,... | collective-permute-start | bytes 1572872 | tf_op jit(solution)/shard_map/ppermute | solution.py:435
  52.4 26.8 %collective-permute-start = (bf16[128,2048]{1,0:T(8,128)(2,1)S(1)}, bf16[128,2048]{1,0:T(8,128)(2,1)S(1)}, u32[]{:S(2)}, u32[]{:S(2)}) collective-permute-start(bf16[128,2048]{1,0:T(8,128)(2,1)S(1)} %copy-done.69), channel_id=1, source_target_pairs={{0,1},{1,2},{2,3},{3,0},{4,5},{5,6},{6,7},{7,4},{8,9},{9,10},{10,1... | collective-permute-start | bytes 1572872 | tf_op jit(solution)/shard_map/ppermute | solution.py:435
  54.1 39.0 %collective-permute-start.2 = (bf16[128,2048]{1,0:T(8,128)(2,1)S(1)}, bf16[128,2048]{1,0:T(8,128)(2,1)S(1)}, u32[]{:S(2)}, u32[]{:S(2)}) collective-permute-start(bf16[128,2048]{1,0:T(8,128)(2,1)S(1)} %copy-done.69), channel_id=1, source_target_pairs={{0,3},{1,0},{2,1},{3,2},{4,7},{5,4},{6,5},{7,6},{8,11},{9,8},{10,9... | collective-permute-start | bytes 1572872 | tf_op jit(solution)/shard_map/ppermute | solution.py:435
  58.5 36.2 %copy-start.32 = (bf16[128,512]{1,0:T(8,128)(2,1)S(1)}, bf16[128,512]{1,0:T(8,128)(2,1)}, u32[]{:S(2)}) copy-start(bf16[128,512]{1,0:T(8,128)(2,1)} %get-tuple-element.223) | copy-start | bytes 393220
  58.5 36.2 %copy-start.34 = (bf16[128,512]{1,0:T(8,128)(2,1)S(1)}, bf16[128,512]{1,0:T(8,128)(2,1)}, u32[]{:S(2)}) copy-start(bf16[128,512]{1,0:T(8,128)(2,1)} %get-tuple-element.224) | copy-start | bytes 393220
  58.5 36.2 %copy-start.36 = (bf16[128,512]{1,0:T(8,128)(2,1)S(1)}, bf16[128,512]{1,0:T(8,128)(2,1)}, u32[]{:S(2)}) copy-start(bf16[128,512]{1,0:T(8,128)(2,1)} %get-tuple-element.225) | copy-start | bytes 393220
  58.5 36.2 %copy-start.38 = (bf16[128,512]{1,0:T(8,128)(2,1)S(1)}, bf16[128,512]{1,0:T(8,128)(2,1)}, u32[]{:S(2)}) copy-start(bf16[128,512]{1,0:T(8,128)(2,1)} %get-tuple-element.226) | copy-start | bytes 393220
  58.5 41.1 %collective-permute-start.6 = (bf16[512,1024]{1,0:T(8,128)(2,1)S(1)}, bf16[512,1024]{1,0:T(8,128)(2,1)S(1)}, u32[]{:S(2)}, u32[]{:S(2)}) collective-permute-start(bf16[512,1024]{1,0:T(8,128)(2,1)S(1)} %pad_maximum_fusion.7), channel_id=1, source_target_pairs={{0,16},{4,20},{8,24},{12,28},{16,0},{20,4},{24,8},{28,12},{1,17},{... | collective-permute-start | bytes 3145736 | tf_op jit(solution)/shard_map/ppermute | solution.py:435
  79.2 26.0 %collective-permute-start.5 = (bf16[512,1024]{1,0:T(8,128)(2,1)S(1)}, bf16[512,1024]{1,0:T(8,128)(2,1)S(1)}, u32[]{:S(2)}, u32[]{:S(2)}) collective-permute-start(bf16[512,1024]{1,0:T(8,128)(2,1)S(1)} %pad_maximum_fusion.7), channel_id=1, source_target_pairs={{0,8},{4,12},{8,0},{12,4},{16,24},{20,28},{24,16},{28,20},{1,9},{5... | collective-permute-start | bytes 3145736 | tf_op jit(solution)/shard_map/ppermute | solution.py:435
  88.5 26.0 %collective-permute-start.18 = (bf16[512,1024]{1,0:T(8,128)(2,1)S(1)}, bf16[512,1024]{1,0:T(8,128)(2,1)S(1)}, u32[]{:S(2)}, u32[]{:S(2)}) collective-permute-start(bf16[512,1024]{1,0:T(8,128)(2,1)S(1)} %pad_maximum_fusion.9), channel_id=1, source_target_pairs={{0,16},{4,20},{8,24},{12,28},{16,0},{20,4},{24,8},{28,12},{1,17},{... | collective-permute-start | bytes 3145736 | tf_op jit(solution)/shard_map/ppermute | solution.py:435
  93.1 34.6 %collective-permute-start.17 = (bf16[512,1024]{1,0:T(8,128)(2,1)S(1)}, bf16[512,1024]{1,0:T(8,128)(2,1)S(1)}, u32[]{:S(2)}, u32[]{:S(2)}) collective-permute-start(bf16[512,1024]{1,0:T(8,128)(2,1)S(1)} %pad_maximum_fusion.9), channel_id=1, source_target_pairs={{0,8},{4,12},{8,0},{12,4},{16,24},{20,28},{24,16},{28,20},{1,9},{5... | collective-permute-start | bytes 3145736 | tf_op jit(solution)/shard_map/ppermute | solution.py:435
  98.1 38.9 %collective-permute-start.13 = (bf16[512,1024]{1,0:T(8,128)(2,1)S(1)}, bf16[512,1024]{1,0:T(8,128)(2,1)S(1)}, u32[]{:S(2)}, u32[]{:S(2)}) collective-permute-start(bf16[512,1024]{1,0:T(8,128)(2,1)S(1)} %pad_maximum_fusion.8), channel_id=1, source_target_pairs={{0,16},{4,20},{8,24},{12,28},{16,0},{20,4},{24,8},{28,12},{1,17},{... | collective-permute-start | bytes 3145736 | tf_op jit(solution)/shard_map/ppermute | solution.py:435
  99.7 50.5 %collective-permute-start.12 = (bf16[512,1024]{1,0:T(8,128)(2,1)S(1)}, bf16[512,1024]{1,0:T(8,128)(2,1)S(1)}, u32[]{:S(2)}, u32[]{:S(2)}) collective-permute-start(bf16[512,1024]{1,0:T(8,128)(2,1)S(1)} %pad_maximum_fusion.8), channel_id=1, source_target_pairs={{0,8},{4,12},{8,0},{12,4},{16,24},{20,28},{24,16},{28,20},{1,9},{5... | collective-permute-start | bytes 3145736 | tf_op jit(solution)/shard_map/ppermute | solution.py:435
  105.3 76.0 %collective-permute-start.3 = (bf16[512,2048]{1,0:T(8,128)(2,1)S(1)}, bf16[512,2048]{1,0:T(8,128)(2,1)S(1)}, u32[]{:S(2)}, u32[]{:S(2)}) collective-permute-start(bf16[512,2048]{1,0:T(8,128)(2,1)S(1)} %pad_maximum_fusion), channel_id=1, source_target_pairs={{0,4},{4,0},{8,12},{12,8},{16,20},{20,16},{24,28},{28,24},{1,5},{5... | collective-permute-start | bytes 6291464 | tf_op jit(solution)/shard_map/ppermute | solution.py:435
  114.5 47.0 %collective-permute-start.7 = (bf16[256,1024]{1,0:T(8,128)(2,1)S(1)}, bf16[256,1024]{1,0:T(8,128)(2,1)S(1)}, u32[]{:S(2)}, u32[]{:S(2)}) collective-permute-start(bf16[256,1024]{1,0:T(8,128)(2,1)S(1)} %slice.374), channel_id=1, source_target_pairs={{0,8},{4,12},{8,0},{12,4},{16,24},{20,28},{24,16},{28,20},{1,9},{5... | collective-permute-start | bytes 1572872 | tf_op jit(solution)/shard_map/ppermute | solution.py:435
  127.7 35.3 %collective-permute-start.8 = (bf16[256,1024]{1,0:T(8,128)(2,1)S(1)}, bf16[256,1024]{1,0:T(8,128)(2,1)S(1)}, u32[]{:S(2)}, u32[]{:S(2)}) collective-permute-start(bf16[256,1024]{1,0:T(8,128)(2,1)S(1)} %slice.375), channel_id=1, source_target_pairs={{0,16},{4,20},{8,24},{12,28},{16,0},{20,4},{24,8},{28,12},{1,17},{... | collective-permute-start | bytes 1572872 | tf_op jit(solution)/shard_map/ppermute | solution.py:435
  137.0 35.7 %collective-permute-start.19 = (bf16[256,1024]{1,0:T(8,128)(2,1)S(1)}, bf16[256,1024]{1,0:T(8,128)(2,1)S(1)}, u32[]{:S(2)}, u32[]{:S(2)}) collective-permute-start(bf16[256,1024]{1,0:T(8,128)(2,1)S(1)} %slice.391), channel_id=1, source_target_pairs={{0,8},{4,12},{8,0},{12,4},{16,24},{20,28},{24,16},{28,20},{1,9},{5... | collective-permute-start | bytes 1572872 | tf_op jit(solution)/shard_map/ppermute | solution.py:435
  150.2 22.5 %collective-permute-start.20 = (bf16[256,1024]{1,0:T(8,128)(2,1)S(1)}, bf16[256,1024]{1,0:T(8,128)(2,1)S(1)}, u32[]{:S(2)}, u32[]{:S(2)}) collective-permute-start(bf16[256,1024]{1,0:T(8,128)(2,1)S(1)} %slice.392), channel_id=1, source_target_pairs={{0,16},{4,20},{8,24},{12,28},{16,0},{20,4},{24,8},{28,12},{1,17},{... | collective-permute-start | bytes 1572872 | tf_op jit(solution)/shard_map/ppermute | solution.py:435
  161.4 19.7 %collective-permute-start.14 = (bf16[256,1024]{1,0:T(8,128)(2,1)S(1)}, bf16[256,1024]{1,0:T(8,128)(2,1)S(1)}, u32[]{:S(2)}, u32[]{:S(2)}) collective-permute-start(bf16[256,1024]{1,0:T(8,128)(2,1)S(1)} %slice.389), channel_id=1, source_target_pairs={{0,8},{4,12},{8,0},{12,4},{16,24},{20,28},{24,16},{28,20},{1,9},{5... | collective-permute-start | bytes 1572872 | tf_op jit(solution)/shard_map/ppermute | solution.py:435
  163.1 18.1 %collective-permute-start.15 = (bf16[256,1024]{1,0:T(8,128)(2,1)S(1)}, bf16[256,1024]{1,0:T(8,128)(2,1)S(1)}, u32[]{:S(2)}, u32[]{:S(2)}) collective-permute-start(bf16[256,1024]{1,0:T(8,128)(2,1)S(1)} %slice.390), channel_id=1, source_target_pairs={{0,16},{4,20},{8,24},{12,28},{16,0},{20,4},{24,8},{28,12},{1,17},{... | collective-permute-start | bytes 1572872 | tf_op jit(solution)/shard_map/ppermute | solution.py:435
  172.7 36.0 %collective-permute-start.28 = (bf16[512,2048]{1,0:T(8,128)(2,1)S(1)}, bf16[512,2048]{1,0:T(8,128)(2,1)S(1)}, u32[]{:S(2)}, u32[]{:S(2)}) collective-permute-start(bf16[512,2048]{1,0:T(8,128)(2,1)S(1)} %pad_maximum_fusion.1), channel_id=1, source_target_pairs={{0,4},{4,0},{8,12},{12,8},{16,20},{20,16},{24,28},{28,24},{1,5},{5... | collective-permute-start | bytes 6291464 | tf_op jit(solution)/shard_map/ppermute | solution.py:435
  184.4 134.8 %copy-start.91 = (f32[1024]{0:T(1024)}, f32[1024]{0:T(1024)S(1)}, u32[]{:S(2)}) copy-start(f32[1024]{0:T(1024)S(1)} %add_rsqrt_fusion) | copy-start | bytes 12292
  208.6 42.1 %copy-start.16 = (bf16[1024,1024]{1,0:T(8,128)(2,1)}, bf16[1024,1024]{1,0:T(8,128)(2,1)S(1)}, u32[]{:S(2)}) copy-start(bf16[1024,1024]{1,0:T(8,128)(2,1)S(1)} %get-tuple-element.210) | copy-start | bytes 6291460
  240.8 15.7 %collective-permute-start.10 = (bf16[512,512]{0,1:T(8,128)(2,1)S(1)}, bf16[512,512]{0,1:T(8,128)(2,1)S(1)}, u32[]{:S(2)}, u32[]{:S(2)}) collective-permute-start(bf16[512,512]{0,1:T(8,128)(2,1)S(1)} %get-tuple-element.100), channel_id=1, source_target_pairs={{0,8},{4,12},{8,16},{12,20},{16,24},{20,28},{1,9},{5,13},{9,17},{1... | collective-permute-start | bytes 1572872 | tf_op jit(solution)/shard_map/ppermute | solution.py:435
  245.6 49.0 %collective-permute-start.42 = (bf16[256,1024]{1,0:T(8,128)(2,1)}, bf16[256,1024]{1,0:T(8,128)(2,1)}, u32[]{:S(2)}, u32[]{:S(2)}) collective-permute-start(bf16[256,1024]{1,0:T(8,128)(2,1)} %get-tuple-element.148), channel_id=1, source_target_pairs={{0,16},{4,20},{8,24},{12,28},{16,0},{20,4},{24,8},{28,12},{1,17},{... | collective-permute-start | bytes 1572872 | tf_op jit(solution)/shard_map/ppermute | solution.py:435
  247.1 43.9 %collective-permute-start.44 = (bf16[256,1024]{1,0:T(8,128)(2,1)}, bf16[256,1024]{1,0:T(8,128)(2,1)}, u32[]{:S(2)}, u32[]{:S(2)}) collective-permute-start(bf16[256,1024]{1,0:T(8,128)(2,1)} %get-tuple-element.149), channel_id=1, source_target_pairs={{0,8},{4,12},{8,0},{12,4},{16,24},{20,28},{24,16},{28,20},{1,9},{5... | collective-permute-start | bytes 1572872 | tf_op jit(solution)/shard_map/ppermute | solution.py:435
  248.2 38.0 %collective-permute-start.47 = (bf16[256,1024]{1,0:T(8,128)(2,1)}, bf16[256,1024]{1,0:T(8,128)(2,1)}, u32[]{:S(2)}, u32[]{:S(2)}) collective-permute-start(bf16[256,1024]{1,0:T(8,128)(2,1)} %get-tuple-element.146), channel_id=1, source_target_pairs={{0,16},{4,20},{8,24},{12,28},{16,0},{20,4},{24,8},{28,12},{1,17},{... | collective-permute-start | bytes 1572872 | tf_op jit(solution)/shard_map/ppermute | solution.py:435
  250.2 29.6 %collective-permute-start.49 = (bf16[256,1024]{1,0:T(8,128)(2,1)}, bf16[256,1024]{1,0:T(8,128)(2,1)}, u32[]{:S(2)}, u32[]{:S(2)}) collective-permute-start(bf16[256,1024]{1,0:T(8,128)(2,1)} %get-tuple-element.147), channel_id=1, source_target_pairs={{0,8},{4,12},{8,0},{12,4},{16,24},{20,28},{24,16},{28,20},{1,9},{5... | collective-permute-start | bytes 1572872 | tf_op jit(solution)/shard_map/ppermute | solution.py:435
  276.6 32.0 %collective-permute-start.29 = (f32[512,512]{0,1:T(8,128)S(1)}, f32[512,512]{0,1:T(8,128)S(1)}, u32[]{:S(2)}, u32[]{:S(2)}) collective-permute-start(f32[512,512]{0,1:T(8,128)S(1)} %broadcast_select_fusion), channel_id=1, source_target_pairs={{8,0},{12,4},{16,8},{20,12},{24,16},{28,20},{9,1},{13,5},{17,9},{2... | collective-permute-start | bytes 3145736 | tf_op jit(solution)/shard_map/ppermute | solution.py:435
  283.0 56.9 %collective-permute-start.50 = (bf16[512,1024]{1,0:T(8,128)(2,1)}, bf16[512,1024]{1,0:T(8,128)(2,1)}, u32[]{:S(2)}, u32[]{:S(2)}) collective-permute-start(bf16[512,1024]{1,0:T(8,128)(2,1)} %add_convert_fusion.2), channel_id=1, source_target_pairs={{0,16},{4,20},{8,24},{12,28},{16,0},{20,4},{24,8},{28,12},{1,17},{... | collective-permute-start | bytes 3145736 | tf_op jit(solution)/shard_map/ppermute | solution.py:435
  289.4 52.2 %collective-permute-start.48 = (bf16[512,1024]{1,0:T(8,128)(2,1)}, bf16[512,1024]{1,0:T(8,128)(2,1)}, u32[]{:S(2)}, u32[]{:S(2)}) collective-permute-start(bf16[512,1024]{1,0:T(8,128)(2,1)} %add_convert_fusion.3), channel_id=1, source_target_pairs={{0,8},{4,12},{8,0},{12,4},{16,24},{20,28},{24,16},{28,20},{1,9},{5... | collective-permute-start | bytes 3145736 | tf_op jit(solution)/shard_map/ppermute | solution.py:435
  294.5 54.1 %collective-permute-start.45 = (bf16[512,1024]{1,0:T(8,128)(2,1)}, bf16[512,1024]{1,0:T(8,128)(2,1)}, u32[]{:S(2)}, u32[]{:S(2)}) collective-permute-start(bf16[512,1024]{1,0:T(8,128)(2,1)} %add_convert_fusion.4), channel_id=1, source_target_pairs={{0,16},{4,20},{8,24},{12,28},{16,0},{20,4},{24,8},{28,12},{1,17},{... | collective-permute-start | bytes 3145736 | tf_op jit(solution)/shard_map/ppermute | solution.py:435
  298.1 50.5 %collective-permute-start.43 = (bf16[512,1024]{1,0:T(8,128)(2,1)}, bf16[512,1024]{1,0:T(8,128)(2,1)}, u32[]{:S(2)}, u32[]{:S(2)}) collective-permute-start(bf16[512,1024]{1,0:T(8,128)(2,1)} %add_convert_fusion.5), channel_id=1, source_target_pairs={{0,8},{4,12},{8,0},{12,4},{16,24},{20,28},{24,16},{28,20},{1,9},{5... | collective-permute-start | bytes 3145736 | tf_op jit(solution)/shard_map/ppermute | solution.py:435
  308.6 96.4 %collective-permute-start.21 = (bf16[512,2048]{1,0:T(8,128)(2,1)}, bf16[512,2048]{1,0:T(8,128)(2,1)}, u32[]{:S(2)}, u32[]{:S(2)}) collective-permute-start(bf16[512,2048]{1,0:T(8,128)(2,1)} %slice.617), channel_id=1, source_target_pairs={{0,4},{4,0},{8,12},{12,8},{16,20},{20,16},{24,28},{28,24},{1,5},{5... | collective-permute-start | bytes 6291464 | tf_op jit(solution)/shard_map/ppermute | solution.py:435
  339.9 61.3 %collective-permute-start.34 = (bf16[256,1024]{1,0:T(8,128)(2,1)}, bf16[256,1024]{1,0:T(8,128)(2,1)}, u32[]{:S(2)}, u32[]{:S(2)}) collective-permute-start(bf16[256,1024]{1,0:T(8,128)(2,1)} %get-tuple-element.150), channel_id=1, source_target_pairs={{0,16},{4,20},{8,24},{12,28},{16,0},{20,4},{24,8},{28,12},{1,17},{... | collective-permute-start | bytes 1572872 | tf_op jit(solution)/shard_map/ppermute | solution.py:435
  341.6 56.2 %collective-permute-start.36 = (bf16[256,1024]{1,0:T(8,128)(2,1)}, bf16[256,1024]{1,0:T(8,128)(2,1)}, u32[]{:S(2)}, u32[]{:S(2)}) collective-permute-start(bf16[256,1024]{1,0:T(8,128)(2,1)} %get-tuple-element.151), channel_id=1, source_target_pairs={{0,8},{4,12},{8,0},{12,4},{16,24},{20,28},{24,16},{28,20},{1,9},{5... | collective-permute-start | bytes 1572872 | tf_op jit(solution)/shard_map/ppermute | solution.py:435
  348.6 70.0 %collective-permute-start.51 = (f32[256,1024]{1,0:T(8,128)}, f32[256,1024]{1,0:T(8,128)S(1)}, u32[]{:S(2)}, u32[]{:S(2)}) collective-permute-start(f32[256,1024]{1,0:T(8,128)} %constant_dynamic-slice_fusion), channel_id=1, source_target_pairs={{0,4},{4,0},{8,12},{12,8},{16,20},{20,16},{24,28},{28,24},{1,5},{5... | collective-permute-start | bytes 3145736 | tf_op jit(solution)/shard_map/ppermute | solution.py:435
  348.6 8.4 %collective-permute-start.39 = (f32[94,128]{1,0:T(8,128)S(1)}, f32[94,128]{1,0:T(8,128)S(1)}, u32[]{:S(2)}, u32[]{:S(2)}) collective-permute-start(f32[94,128]{1,0:T(8,128)S(1)} %maximum_bitcast_fusion.5), channel_id=1, source_target_pairs={{0,8},{4,12},{8,0},{12,4},{16,24},{20,28},{24,16},{28,20},{1,9},{5... | collective-permute-start | bytes 144392 | tf_op jit(solution)/shard_map/ppermute | solution.py:435
  357.0 4.2 collective-permute-start.40
  359.6 35.4 %copy-start.92 = (f32[2,768]{1,0:T(2,128)S(1)}, f32[2,768]{1,0:T(2,128)}, u32[]{:S(2)}) copy-start(f32[2,768]{1,0:T(2,128)} %param.30) | copy-start | bytes 18436
  359.6 37.4 %copy-start.73 = (f32[6,2048]{1,0:T(8,128)S(1)}, f32[6,2048]{1,0:T(8,128)}, u32[]{:S(2)}) copy-start(f32[6,2048]{1,0:T(8,128)} %param.35) | copy-start | bytes 147460
  359.6 37.4 %copy-start.78 = (f32[6,2048]{1,0:T(8,128)S(1)}, f32[6,2048]{1,0:T(8,128)}, u32[]{:S(2)}) copy-start(f32[6,2048]{1,0:T(8,128)} %param.42) | copy-start | bytes 147460
  359.6 37.4 %copy-start.79 = (f32[6,2048]{1,0:T(8,128)S(1)}, f32[6,2048]{1,0:T(8,128)}, u32[]{:S(2)}) copy-start(f32[6,2048]{1,0:T(8,128)} %param.49) | copy-start | bytes 147460
  361.2 5.0 collective-permute-start.41
  366.2 25.1 %collective-permute-start.52 = (f32[80,128]{1,0:T(8,128)S(1)}, f32[80,128]{1,0:T(8,128)S(1)}, u32[]{:S(2)}, u32[]{:S(2)}) collective-permute-start(f32[80,128]{1,0:T(8,128)S(1)} %slice_add_fusion.4), channel_id=1, source_target_pairs={{0,1},{1,0},{2,3},{3,2},{4,5},{5,4},{6,7},{7,6},{8,9},{9,8},{10,11... | collective-permute-start | bytes 122888 | tf_op jit(solution)/shard_map/ppermute | solution.py:435
  391.3 5.7 %collective-permute-start.53 = (f32[80,128]{1,0:T(8,128)S(1)}, f32[80,128]{1,0:T(8,128)S(1)}, u32[]{:S(2)}, u32[]{:S(2)}) collective-permute-start(f32[80,128]{1,0:T(8,128)S(1)} %add.665), channel_id=1, source_target_pairs={{0,2},{1,3},{2,0},{3,1},{4,6},{5,7},{6,4},{7,5},{8,10},{9,11},{10,... | collective-permute-start | bytes 122888 | tf_op jit(solution)/shard_map/ppermute | solution.py:435
  397.0 13.5 %collective-permute-start.46 = (f32[256,1024]{1,0:T(8,128)}, f32[256,1024]{1,0:T(8,128)}, u32[]{:S(2)}, u32[]{:S(2)}) collective-permute-start(f32[256,1024]{1,0:T(8,128)} %constant_dynamic-slice_fusion.1), channel_id=1, source_target_pairs={{0,4},{4,0},{8,12},{12,8},{16,20},{20,16},{24,28},{28,24},{1,5},{5... | collective-permute-start | bytes 3145736 | tf_op jit(solution)/shard_map/ppermute | solution.py:435
  397.8 65.3 %collective-permute-start.30 = (bf16[512,2048]{1,0:T(8,128)(2,1)}, bf16[512,2048]{1,0:T(8,128)(2,1)S(1)}, u32[]{:S(2)}, u32[]{:S(2)}) collective-permute-start(bf16[512,2048]{1,0:T(8,128)(2,1)} %slice.616), channel_id=1, source_target_pairs={{0,4},{4,0},{8,12},{12,8},{16,20},{20,16},{24,28},{28,24},{1,5},{5... | collective-permute-start | bytes 6291464 | tf_op jit(solution)/shard_map/ppermute | solution.py:435
  401.2 25.4 %collective-permute-start.37 = (bf16[512,1024]{1,0:T(8,128)(2,1)}, bf16[512,1024]{1,0:T(8,128)(2,1)}, u32[]{:S(2)}, u32[]{:S(2)}) collective-permute-start(bf16[512,1024]{1,0:T(8,128)(2,1)} %fusion.28), channel_id=1, source_target_pairs={{0,16},{4,20},{8,24},{12,28},{16,0},{20,4},{24,8},{28,12},{1,17},{... | collective-permute-start | bytes 3145736 | tf_op jit(solution)/shard_map/ppermute | solution.py:435
  405.1 28.5 %collective-permute-start.35 = (bf16[512,1024]{1,0:T(8,128)(2,1)}, bf16[512,1024]{1,0:T(8,128)(2,1)}, u32[]{:S(2)}, u32[]{:S(2)}) collective-permute-start(bf16[512,1024]{1,0:T(8,128)(2,1)} %fusion.27), channel_id=1, source_target_pairs={{0,8},{4,12},{8,0},{12,4},{16,24},{20,28},{24,16},{28,20},{1,9},{5... | collective-permute-start | bytes 3145736 | tf_op jit(solution)/shard_map/ppermute | solution.py:435
  410.5 25.5 %collective-permute-start.22 = (bf16[128,2048]{1,0:T(8,128)(2,1)}, bf16[128,2048]{1,0:T(8,128)(2,1)}, u32[]{:S(2)}, u32[]{:S(2)}) collective-permute-start(bf16[128,2048]{1,0:T(8,128)(2,1)} %get-tuple-element.138), channel_id=1, source_target_pairs={{0,3},{1,0},{2,1},{3,2},{4,7},{5,4},{6,5},{7,6},{8,11},{9,8},{10,9... | collective-permute-start | bytes 1572872 | tf_op jit(solution)/shard_map/ppermute | solution.py:435
  418.6 20.7 %collective-permute-start.24 = (bf16[128,2048]{1,0:T(8,128)(2,1)}, bf16[128,2048]{1,0:T(8,128)(2,1)}, u32[]{:S(2)}, u32[]{:S(2)}) collective-permute-start(bf16[128,2048]{1,0:T(8,128)(2,1)} %get-tuple-element.139), channel_id=1, source_target_pairs={{0,1},{1,2},{2,3},{3,0},{4,5},{5,6},{6,7},{7,4},{8,9},{9,10},{10,1... | collective-permute-start | bytes 1572872 | tf_op jit(solution)/shard_map/ppermute | solution.py:435
  426.6 33.6 %collective-permute-start.23 = (bf16[128,2048]{1,0:T(8,128)(2,1)S(1)}, bf16[128,2048]{1,0:T(8,128)(2,1)S(1)}, u32[]{:S(2)}, u32[]{:S(2)}) collective-permute-start(bf16[128,2048]{1,0:T(8,128)(2,1)S(1)} %get-tuple-element.140), channel_id=1, source_target_pairs={{0,2},{1,3},{2,0},{3,1},{4,6},{5,7},{6,4},{7,5},{8,10},{9,11},{10,... | collective-permute-start | bytes 1572872 | tf_op jit(solution)/shard_map/ppermute | solution.py:435
  435.9 31.3 %collective-permute-start.38 = (f32[256,1024]{1,0:T(8,128)S(1)}, f32[256,1024]{1,0:T(8,128)S(1)}, u32[]{:S(2)}, u32[]{:S(2)}) collective-permute-start(f32[256,1024]{1,0:T(8,128)S(1)} %constant_dynamic-slice_fusion.6), channel_id=1, source_target_pairs={{0,4},{4,0},{8,12},{12,8},{16,20},{20,16},{24,28},{28,24},{1,5},{5... | collective-permute-start | bytes 3145736 | tf_op jit(solution)/shard_map/ppermute | solution.py:435
  464.4 26.7 %collective-permute-start.31 = (bf16[128,2048]{1,0:T(8,128)(2,1)S(1)}, bf16[128,2048]{1,0:T(8,128)(2,1)S(1)}, u32[]{:S(2)}, u32[]{:S(2)}) collective-permute-start(bf16[128,2048]{1,0:T(8,128)(2,1)S(1)} %get-tuple-element.135), channel_id=1, source_target_pairs={{0,3},{1,0},{2,1},{3,2},{4,7},{5,4},{6,5},{7,6},{8,11},{9,8},{10,9... | collective-permute-start | bytes 1572872 | tf_op jit(solution)/shard_map/ppermute | solution.py:435
  466.6 24.6 %collective-permute-start.33 = (bf16[128,2048]{1,0:T(8,128)(2,1)S(1)}, bf16[128,2048]{1,0:T(8,128)(2,1)S(1)}, u32[]{:S(2)}, u32[]{:S(2)}) collective-permute-start(bf16[128,2048]{1,0:T(8,128)(2,1)S(1)} %get-tuple-element.136), channel_id=1, source_target_pairs={{0,1},{1,2},{2,3},{3,0},{4,5},{5,6},{6,7},{7,4},{8,9},{9,10},{10,1... | collective-permute-start | bytes 1572872 | tf_op jit(solution)/shard_map/ppermute | solution.py:435
  466.6 44.2 %collective-permute-start.32 = (bf16[128,2048]{1,0:T(8,128)(2,1)S(1)}, bf16[128,2048]{1,0:T(8,128)(2,1)S(1)}, u32[]{:S(2)}, u32[]{:S(2)}) collective-permute-start(bf16[128,2048]{1,0:T(8,128)(2,1)S(1)} %get-tuple-element.137), channel_id=1, source_target_pairs={{0,2},{1,3},{2,0},{3,1},{4,6},{5,7},{6,4},{7,5},{8,10},{9,11},{10,... | collective-permute-start | bytes 1572872 | tf_op jit(solution)/shard_map/ppermute | solution.py:435
  (97 other events, 1046.3 us)

commit v2 on v0

--- a/solution.py
+++ b/solution.py
@@ -1,6 +1,8 @@
 import jax
 import jax.numpy as jnp
 from jax import lax
+from jax.experimental import pallas as pl
+from jax.experimental.pallas import tpu as pltpu
 from jax.sharding import PartitionSpec as P
 
 ROT = 64
@@ -111,7 +113,7 @@
     )
 
 
-def per_device(
+def per_device_generic(
     inputs,
     cotangent,
     segments,
@@ -431,7 +433,839 @@
     )
 
 
+def send(value, axis, pairs):
+    return lax.ppermute(value, axis, pairs)
+
+
+def product(left, right):
+    return jnp.dot(left, right, preferred_element_type=jnp.float32)
+
+
+def shape_of(shape, dtype):
+    return jax.ShapeDtypeStruct(shape, dtype)
+
+
+def moved(arrays, index):
+    count = index.shape[0]
+
+    def body(index_ref, *refs):
+        for source, target in zip(refs[: len(arrays)], refs[len(arrays) :]):
+            target[...] = source[...]
+
+    blocks = [(value.shape[0], value.shape[1] // count) for value in arrays]
+    return pl.pallas_call(
+        body,
+        grid_spec=pltpu.PrefetchScalarGridSpec(
+            num_scalar_prefetch=1,
+            grid=(count,),
+            in_specs=[pl.BlockSpec(block, lambda i, index_ref: (0, index_ref[i])) for block in blocks],
+            out_specs=[pl.BlockSpec(block, lambda i, index_ref: (0, i)) for block in blocks],
+        ),
+        out_shape=[shape_of(value.shape, value.dtype) for value in arrays],
+        name="moved",
+    )(index, *arrays)
+
+
+def normalized_tile(tile):
+    row = tile.astype(jnp.float32)
+    center = row - jnp.mean(row, axis=-1, keepdims=True)
+    variance = jnp.mean(center * center, axis=-1, keepdims=True)
+    return center * lax.rsqrt(variance + norm_eps)
+
+
+def normed_inputs(x, vectors):
+    rows, width = x.shape
+    tile = 256
+
+    def body(x_ref, vector_ref, attn_ref, mlp_ref):
+        xhat = normalized_tile(x_ref[...])
+        attn_ref[...] = (xhat * vector_ref[0:1] + vector_ref[1:2]).astype(jnp.bfloat16)
+        mlp_ref[...] = (xhat * vector_ref[2:3] + vector_ref[3:4]).astype(jnp.bfloat16)
+
+    spec = pl.BlockSpec((tile, width), lambda i: (i, 0))
+    return pl.pallas_call(
+        body,
+        grid=(rows // tile,),
+        in_specs=[spec, pl.BlockSpec(vectors.shape, lambda i: (0, 0))],
+        out_specs=[spec, spec],
+        out_shape=[shape_of(x.shape, jnp.bfloat16)] * 2,
+        name="normed",
+    )(x, vectors)
+
+
+def gathered_product(left, pieces, extras, outputs, finish, live, name):
+    tile = 256
+    columns = pieces[0].shape[1]
+    rows = left.shape[0]
+    depth = left.shape[1]
+    piece_rows = pieces[3].shape[0]
+
+    def body(left_ref, block, from_x, from_y, top, bottom, *refs):
+        weight_ref = refs[len(extras)]
+        parts = (
+            (block, 0),
+            (from_x, 0),
+            (from_y, 0),
+            (top, 0),
+            (block, 1),
+            (from_y, 1),
+            (from_x, 1),
+            (bottom, 0),
+        )
+        for i, (part, half) in enumerate(parts):
+            weight_ref[i * piece_rows : (i + 1) * piece_rows, :] = part[
+                half * piece_rows : (half + 1) * piece_rows, :
+            ]
+        step = pl.program_id(0)
+
+        @pl.when(step < live)
+        def _():
+            result = product(left_ref[...], weight_ref[...])
+            finish(step, result, refs[: len(extras)], refs[len(extras) + 1 :])
+
+    def spec_of(height, moves):
+        if moves:
+            return pl.BlockSpec((height, tile), lambda j: (0, jnp.minimum(j, live - 1)))
+        return pl.BlockSpec((height, 128), lambda j: (0, 0))
+
+    column_spec = lambda height: pl.BlockSpec((height, tile), lambda j: (0, j))
+    return pl.pallas_call(
+        body,
+        grid=(columns // tile,),
+        in_specs=[pl.BlockSpec((rows, depth), lambda j: (0, 0))]
+        + [column_spec(piece.shape[0]) for piece in pieces]
+        + [spec_of(extra.shape[0], moves) for extra, moves in extras],
+        out_specs=[column_spec(depth)] + [spec_of(out.shape[0], True) for out in outputs],
+        out_shape=[shape_of((depth, columns), left.dtype)] + outputs,
+        name=name,
+    )(left, *pieces, *[extra for extra, _ in extras])
+
+
+def partner_lanes(head):
+    half_rot = ROT // 2
+    lane = lax.broadcasted_iota(jnp.int32, head.shape, 1)
+    return jnp.where(
+        lane < half_rot,
+        pltpu.roll(head, head.shape[1] - half_rot, 1),
+        pltpu.roll(head, half_rot, 1),
+    )
+
+
+def qkv_product(left, pieces, bias, cosines, sines):
+    rows = left.shape[0]
+    columns = bias.shape[1]
+
+    def finish(step, result, extras, outs):
+        bias_ref, cosine_ref, sine_ref = extras
+        value = result + bias_ref[...]
+        head = value[:, :128]
+        turned = head * cosine_ref[...] + partner_lanes(head) * sine_ref[...]
+        outs[0][:, :128] = jnp.where(step < 2, turned, head).astype(jnp.bfloat16)
+        outs[0][:, 128:] = value[:, 128:].astype(jnp.bfloat16)
+
+    return gathered_product(
+        left,
+        pieces,
+        [(bias, True), (cosines, False), (sines, False)],
+        [shape_of((rows, columns), jnp.bfloat16)],
+        finish,
+        3,
+        "qkv",
+    )
+
+
+def expand_product(left, pieces, bias):
+    shape = (left.shape[0], bias.shape[1])
+
+    def finish(step, result, extras, outs):
+        pre = result + extras[0][...]
+        distribution = 0.5 * (1.0 + lax.erf(pre * 0.7071067811865476))
+        outs[0][...] = (pre * distribution).astype(jnp.bfloat16)
+        outs[1][...] = distribution + pre * jnp.exp(-0.5 * pre * pre) * 0.3989422804014327
+
+    return gathered_product(
+        left,
+        pieces,
+        [(bias, True)],
+        [shape_of(shape, jnp.bfloat16), shape_of(shape, jnp.float32)],
+        finish,
+        4,
+        "expand",
+    )
+
+
+def contract_product(left, pieces, slope):
+    def finish(step, result, extras, outs):
+        gradient = result * extras[0][...]
+        outs[0][...] = gradient.astype(jnp.bfloat16)
+        outs[1][...] = jnp.sum(gradient, axis=0, keepdims=True)
+
+    return gathered_product(
+        left,
+        pieces,
+        [(slope, True)],
+        [shape_of(slope.shape, jnp.bfloat16), shape_of((1, slope.shape[1]), jnp.float32)],
+        finish,
+        4,
+        "contract",
+    )
+
+
+def nt(left, right):
+    return lax.dot_general(
+        left, right, (((1,), (1,)), ((), ())), preferred_element_type=jnp.float32
+    )
+
+
+def attention_call(body, halo_of, operands, extras, outputs, name):
+    qkv, halo, seg_rows, token_rows, seg_columns, token_columns, seg_halo, token_halo = operands
+    rows = qkv.shape[0] // 2
+    head = qkv.shape[1] // 3
+    block = lambda column, flip: pl.BlockSpec(
+        (rows, head), lambda b, h: ((1 - b) if flip else b, column)
+    )
+    column_vector = pl.BlockSpec((rows, 1), lambda b, h: (b, 0))
+    row_vector = lambda flip: pl.BlockSpec((1, rows), lambda b, h: (0, (1 - b) if flip else b))
+    fixed = lambda value: pl.BlockSpec(value.shape, lambda b, h: (0, 0))
+    by_block = lambda value: pl.BlockSpec((rows, value.shape[1]), lambda b, h: (b, 0))
+    return pl.pallas_call(
+        body,
+        grid_spec=pltpu.PrefetchScalarGridSpec(
+            num_scalar_prefetch=1,
+            grid=(2,),
+            in_specs=[
+                block(0, False),
+                block(1, True),
+                block(2, True),
+                block(1, False),
+                block(2, False),
+                fixed(halo),
+                column_vector,
+                column_vector,
+                row_vector(True),
+                row_vector(True),
+                row_vector(False),
+                row_vector(False),
+                fixed(seg_halo),
+                fixed(token_halo),
+            ]
+            + [by_block(extra) for extra in extras],
+            out_specs=[by_block(out) for out in outputs],
+        ),
+        out_shape=outputs,
+        name=name,
+    )(
+        halo_of,
+        qkv,
+        qkv,
+        qkv,
+        qkv,
+        qkv,
+        halo,
+        seg_columns,
+        token_columns,
+        seg_rows,
+        token_rows,
+        seg_rows,
+        token_rows,
+        seg_halo,
+        token_halo,
+        *extras,
+    )
+
+
+def masked_scores(halo_of, refs, score_scale):
+    (
+        q_ref,
+        k_before,
+        v_before,
+        k_ref,
+        v_ref,
+        halo,
+        seg_q,
+        token_q,
+        seg_before,
+        token_before,
+        seg_k,
+        token_k,
+        seg_halo,
+        token_halo,
+    ) = refs
+    use_halo = halo_of[pl.program_id(0)] == 1
+    head = q_ref.shape[1]
+    keys_before = jnp.where(use_halo, halo[:, :head], k_before[...])
+    values_before = jnp.where(use_halo, halo[:, head:], v_before[...])
+    segments_before = jnp.where(use_halo, seg_halo[...], seg_before[...])
+    tokens_before = jnp.where(use_halo, token_halo[...], token_before[...])
+    query = q_ref[...]
+
+    def scores(keys, key_segments, key_tokens):
+        allowed = (key_segments == seg_q[...]) & (key_tokens <= token_q[...])
+        return jnp.where(allowed, nt(query, keys) * score_scale, masked_score)
+
+    return (
+        query,
+        (keys_before, k_ref[...]),
+        (values_before, v_ref[...]),
+        (
+            scores(keys_before, segments_before, tokens_before),
+            scores(k_ref[...], seg_k[...], token_k[...]),
+        ),
+    )
+
+
+def attention_forward(halo_of, operands):
+    rows, columns = operands[0].shape
+    head = columns // 3
+    score_scale = head ** (-0.5)
+
+    def body(halo_ref, *refs):
+        _, _, values, scores = masked_scores(halo_ref, refs[:14], score_scale)
+        out_ref, lse_ref = refs[14:]
+        row_max = jnp.maximum(
+            jnp.max(scores[0], axis=-1, keepdims=True), jnp.max(scores[1], axis=-1, keepdims=True)
+        )
+        powers = [jnp.exp(part - row_max) for part in scores]
+        total = jnp.sum(powers[0], axis=-1, keepdims=True) + jnp.sum(
+            powers[1], axis=-1, keepdims=True
+        )
+        inverse = 1.0 / total
+        out_ref[...] = (
+            product((powers[0] * inverse).astype(jnp.bfloat16), values[0])
+            + product((powers[1] * inverse).astype(jnp.bfloat16), values[1])
+        ).astype(jnp.bfloat16)
+        lse_ref[...] = row_max + jnp.log(total)
+
+    return attention_call(
+        body,
+        halo_of,
+        operands,
+        [],
+        [shape_of((rows, head), jnp.bfloat16), shape_of((rows, 1), jnp.float32)],
+        "attention",
+    )
+
+
+def attention_backward(halo_of, operands, lse, attended, attn_grad):
+    rows, columns = operands[0].shape
+    head = columns // 3
+    score_scale = head ** (-0.5)
+
+    def body(halo_ref, *refs):
+        query, keys, values, scores = masked_scores(halo_ref, refs[:14], score_scale)
+        lse_ref, attended_ref, grad_ref, query_out, before_out, own_out = refs[14:]
+        gradient = grad_ref[...]
+        row_delta = jnp.sum(
+            gradient.astype(jnp.float32) * attended_ref[...].astype(jnp.float32),
+            axis=-1,
+            keepdims=True,
+        )
+        query_grad = 0.0
+        for part, out in enumerate((before_out, own_out)):
+            probs = jnp.exp(scores[part] - lse_ref[...])
+            score_grad = (
+                probs * (nt(gradient, values[part]) - row_delta) * score_scale
+            ).astype(jnp.bfloat16)
+            query_grad = query_grad + product(score_grad, keys[part])
+            out[:, :head] = contract_rows(score_grad, query)
+            out[:, head:] = contract_rows(probs.astype(jnp.bfloat16), gradient)
+        query_out[...] = query_grad
+
+    return attention_call(
+        body,
+        halo_of,
+        operands,
+        [lse, attended, attn_grad],
+        [
+            shape_of((rows, head), jnp.float32),
+            shape_of((rows, 2 * head), jnp.float32),
+            shape_of((rows, 2 * head), jnp.float32),
+        ],
+        "attention_back",
+    )
+
+
+def rotated_back(later_of, query_grad, own_part, before_part, from_later, cosines, sines):
+    rows = query_grad.shape[0] // 2
+    head = query_grad.shape[1]
+
+    def body(later_ref, query_ref, own_ref, before_ref, later_grad, cosine, sine, out, bias_out):
+        step = pl.program_id(0)
+        extra = jnp.where(later_ref[step] == 1, later_grad[...], before_ref[...])
+        pairs = own_ref[...] + extra
+
+        def back(value):
+            lanes = value[:, :128]
+            lanes = lanes * cosine[...] - partner_lanes(lanes) * sine[...]
+            return jnp.concatenate([lanes, value[:, 128:]], axis=1)
+
+        @pl.when(step == 0)
+        def _():
+            bias_out[...] = jnp.zeros_like(bias_out)
+
+        parts = (back(query_ref[...]), back(pairs[:, :head]), pairs[:, head:])
+        for i, part in enumerate(parts):
+            columns = slice(i * head, (i + 1) * head)
+            out[:, columns] = part.astype(jnp.bfloat16)
+            bias_out[:, columns] += jnp.sum(part, axis=0, keepdims=True)
+
+    by_block = lambda width: pl.BlockSpec((rows, width), lambda b, h: (b, 0))
+    return pl.pallas_call(
+        body,
+        grid_spec=pltpu.PrefetchScalarGridSpec(
+            num_scalar_prefetch=1,
+            grid=(2,),
+            in_specs=[
+                by_block(head),
+                by_block(2 * head),
+                pl.BlockSpec((rows, 2 * head), lambda b, h: (1 - b, 0)),
+                pl.BlockSpec((rows, 2 * head), lambda b, h: (0, 0)),
+                by_block(128),
+                by_block(128),
+            ],
+            out_specs=[by_block(3 * head), pl.BlockSpec((1, 3 * head), lambda b, h: (0, 0))],
+        ),
+        out_shape=[
+            shape_of((2 * rows, 3 * head), jnp.bfloat16),
+            shape_of((1, 3 * head), jnp.float32),
+        ],
+        name="rotated_back",
+    )(later_of, query_grad, own_part, before_part, from_later, cosines, sines)
+
+
+def branch_rows(half, attended, activated, weight_qd, weight_contract, dtype):
+    rows = attended.shape[0] // 2
+    tile = 512
+    depth = weight_qd.shape[0]
+
+    def body(attended_ref, activated_ref, dense_ref, contract_ref, out):
+        out[...] = (
+            nt(attended_ref[...], dense_ref[...]) + nt(activated_ref[...], contract_ref[...])
+        ).astype(dtype)
+
+    return pl.pallas_call(
+        body,
+        grid=(depth // tile,),
+        in_specs=[
+            pl.BlockSpec((rows, attended.shape[1]), lambda j: (half, 0)),
+            pl.BlockSpec((rows, activated.shape[1]), lambda j: (half, 0)),
+            pl.BlockSpec((tile, attended.shape[1]), lambda j: (j, 3)),
+            pl.BlockSpec((tile, activated.shape[1]), lambda j: (j, 0)),
+        ],
+        out_specs=pl.BlockSpec((rows, tile), lambda j: (0, j)),
+        out_shape=shape_of((rows, depth), dtype),
+        name="branch_%d" % half,
+    )(attended, activated, weight_qd, weight_contract)
+
+
+def back_rows(half, qkv_grad, pre_grad, x, weight_qd, weight_expand, vectors, dtype):
+    rows = x.shape[0] // 2
+    tile = 512
+    depth = x.shape[1]
+
+    def body(qkv_ref, pre_ref, x_ref, tile_ref, qd_ref, expand_ref, vector_ref, out, sums, stats):
+        @pl.when(pl.program_id(0) == 0)
+        def _():
+            row = x_ref[...].astype(jnp.float32)
+            mean = jnp.mean(row, axis=-1, keepdims=True)
+            center = row - mean
+            variance = jnp.mean(center * center, axis=-1, keepdims=True)
+            stats[0] = jnp.broadcast_to(mean, stats.shape[1:])
+            stats[1] = jnp.broadcast_to(lax.rsqrt(variance + norm_eps), stats.shape[1:])
+
+        xhat = (tile_ref[...].astype(jnp.float32) - stats[0][:, :1]) * stats[1][:, :1]
+        attn_back = nt(qkv_ref[...], qd_ref[...])
+        mlp_back = nt(pre_ref[...], expand_ref[...])
+        sums[0:1] = jnp.sum(attn_back * xhat, axis=0, keepdims=True)
+        sums[1:2] = jnp.sum(attn_back, axis=0, keepdims=True)
+        sums[2:3] = jnp.sum(mlp_back * xhat, axis=0, keepdims=True)
+        sums[3:4] = jnp.sum(mlp_back, axis=0, keepdims=True)
+        out[...] = (attn_back * vector_ref[0:1] + mlp_back * vector_ref[2:3]).astype(dtype)
+
+    return pl.pallas_call(
+        body,
+        grid=(depth // tile,),
+        in_specs=[
+            pl.BlockSpec((rows, qkv_grad.shape[1]), lambda j: (half, 0)),
+            pl.BlockSpec((rows, pre_grad.shape[1]), lambda j: (half, 0)),
+            pl.BlockSpec((rows, depth), lambda j: (half, 0)),
+            pl.BlockSpec((rows, tile), lambda j: (half, j)),
+            pl.BlockSpec((tile, qkv_grad.shape[1]), lambda j: (j, 0)),
+            pl.BlockSpec((tile, pre_grad.shape[1]), lambda j: (j, 0)),
+            pl.BlockSpec((vectors.shape[0], tile), lambda j: (0, j)),
+        ],
+        out_specs=[
+            pl.BlockSpec((rows, tile), lambda j: (0, j)),
+            pl.BlockSpec((4, tile), lambda j: (0, j)),
+        ],
+        out_shape=[shape_of((rows, depth), dtype), shape_of((4, depth), jnp.float32)],
+        scratch_shapes=[pltpu.VMEM((2, rows, 128), jnp.float32)],
+        name="back_%d" % half,
+    )(qkv_grad, pre_grad, x, x, weight_qd, weight_expand, vectors)
+
+
+def tied(value, *others):
+    return lax.optimization_barrier((value,) + others)[0]
+
+
+def picked(values, index):
+    rows = jnp.arange(values.shape[0], dtype=jnp.int32)
+    chosen = index[:, None, None] == rows[None, :, None]
+    return jnp.sum(jnp.where(chosen, values[None], 0), axis=1)
+
+
+def per_device_paired(
+    inputs,
+    cotangent,
+    segments,
+    positions,
+    qkv_weight,
+    qkv_bias,
+    dense_weight,
+    expand_weight,
+    expand_bias,
+    contract_weight,
+    norm_bias_vectors,
+    moment_qkv_weight,
+    moment_qkv_bias,
+    moment_dense_weight,
+    moment_expand_weight,
+    moment_expand_bias,
+    moment_contract_weight,
+    moment_norm_vectors,
+    second_qkv_weight,
+    second_qkv_bias,
+    second_dense_weight,
+    second_expand_weight,
+    second_expand_bias,
+    second_contract_weight,
+    second_norm_vectors,
+):
+    bf16, f32 = jnp.bfloat16, jnp.float32
+    fsdp_index = lax.axis_index("fsdp")
+    z = lax.axis_index("tensor")
+    n_z = lax.axis_size("tensor")
+    core = fsdp_index & 1
+    chip = fsdp_index >> 1
+    devices = range(lax.axis_size("fsdp"))
+    to_core = [(i, i ^ 1) for i in devices]
+    to_x = [(i, i ^ 2) for i in devices]
+    to_y = [(i, i ^ 4) for i in devices]
+    to_next = [(i, i + 2) for i in devices if i + 2 < len(devices)]
+    to_prev = [(i + 2, i) for i in devices if i + 2 < len(devices)]
+    first = core == 0
+    head_dim = qkv_weight.shape[2] // 3
+    shard_rows = inputs.shape[0]
+    group_rows = n_z * shard_rows
+    hidden = expand_weight.shape[1] // 2
+    qkv_cols = 3 * head_dim
+    shard_feat = expand_weight.shape[0]
+
+    def column_half(weight, k, width):
+        return lax.dynamic_slice_in_dim(weight, k * width, width, axis=1).astype(bf16)
+
+    def head_columns(k):
+        return jnp.concatenate(
+            [
+                lax.dynamic_index_in_dim(qkv_weight, k, axis=1, keepdims=False),
+                lax.dynamic_slice_in_dim(dense_weight, k * head_dim, head_dim, axis=1),
+            ],
+            axis=1,
+        ).astype(bf16)
+
+    def rows_of_chip(own, other):
+        return jnp.concatenate(
+            [jnp.where(first, own, other), jnp.where(first, other, own)], axis=0
+        )
+
+    swapped = [
+        send(head_columns(1 - core), "fsdp", to_core),
+        send(column_half(expand_weight, 1 - core, hidden), "fsdp", to_core),
+        send(column_half(contract_weight, 1 - core, hidden), "fsdp", to_core),
+    ]
+    own_blocks = [
+        rows_of_chip(own, other)
+        for own, other in zip(
+            (
+                head_columns(core),
+                column_half(expand_weight, core, hidden),
+                column_half(contract_weight, core, hidden),
+            ),
+            swapped,
+        )
+    ]
+
+    def spread(block):
+        return block, send(block, "fsdp", to_x), send(block, "fsdp", to_y)
+
+    def relay(from_x, from_y):
+        return (
+            send(from_y[:shard_feat], "fsdp", to_x),
+            send(from_x[shard_feat:], "fsdp", to_y),
+        )
+
+    def gather_tokens(own):
+        pieces = [own]
+        for k in range(1, n_z):
+            pieces.append(send(own, "tensor", [(i, (i + k) % n_z) for i in range(n_z)]))
+        group = jnp.concatenate(pieces, axis=0)
+        return jnp.concatenate([group, send(group, "fsdp", to_core)], axis=0)
+
+    places = jnp.arange(8, dtype=jnp.int32)
+    rank = places & 3
+    rank = jnp.where(places < 4, rank, 2 * (rank & 1) + (rank >> 1))
+    feature_index = 2 * (chip ^ rank) + (places >> 2)
+    x_rel, dy_rel, vectors = moved((inputs, cotangent, norm_bias_vectors), feature_index)
+    spread_1 = spread(own_blocks[0])
+    spread_2 = spread(own_blocks[1])
+    relayed_1 = relay(spread_1[1], spread_1[2])
+    spread_3 = spread(tied(own_blocks[2], spread_1[1], spread_1[2]))
+    relayed_2 = relay(spread_2[1], spread_2[2])
+    relayed_3 = relay(spread_3[1], spread_3[2])
+    x_all = gather_tokens(x_rel)
+    position_other = send(positions, "fsdp", to_core)
+
+    _, segments_in, position_own, position_other = lax.optimization_barrier(
+        (swapped[2], segments, positions, position_other)
+    )
+    local = jnp.arange(group_rows, dtype=jnp.int32)
+    shard_of = (z - jnp.arange(n_z, dtype=jnp.int32)) & (n_z - 1)
+    order = ((z - local // shard_rows) & (n_z - 1)) * shard_rows + local % shard_rows
+    own_group = fsdp_index
+    other_group = fsdp_index ^ 1
+    halo_group = jnp.maximum(2 * chip - 1, 0)
+    wanted = jnp.concatenate([g * n_z + shard_of for g in (own_group, other_group, halo_group)])
+    seg_rows = picked(segments_in.reshape(-1, shard_rows), wanted).reshape(1, 3 * group_rows)
+    seg_halo = jnp.where(chip == 0, -1, seg_rows[:, 2 * group_rows :])
+    seg_rows = seg_rows[:, : 2 * group_rows]
+    token_rows = jnp.concatenate(
+        [order + own_group * group_rows, order + other_group * group_rows]
+    ).reshape(1, 2 * group_rows)
+    token_halo = (order + halo_group * group_rows).reshape(1, group_rows)
+    position_rows = jnp.concatenate(
+        [position_own.reshape(n_z, shard_rows), position_other.reshape(n_z, shard_rows)], axis=0
+    )
+    position_all = picked(
+        position_rows, jnp.concatenate([shard_of, shard_of + n_z])
+    ).reshape(2 * group_rows)
+    lane = jnp.arange(128, dtype=jnp.int32)
+    half_rot = ROT // 2
+    frequency = 10000.0 ** (-((lane % half_rot).astype(f32) * 2.0 / ROT))
+    angles = jnp.where(
+        lane[None, :] < ROT, position_all.astype(f32)[:, None] * frequency[None, :], 0.0
+    )
+    cosines = jnp.cos(angles)
+    sines = jnp.sin(angles) * jnp.where(lane < half_rot, -1.0, 1.0)[None, :]
+    halo_of = jnp.stack([first, ~first]).astype(jnp.int32)
+    later_of = 1 - halo_of
+
+    xa, xm = normed_inputs(x_all, vectors)
+    dy_all = gather_tokens(dy_rel)
+
+    head_bias = lax.dynamic_slice_in_dim(qkv_bias, core, 1, axis=0)
+    pieces_1 = lax.optimization_barrier((spread_1 + relayed_1, spread_2[1:]))[0]
+    weight_qd, qkv = qkv_product(xa, pieces_1, head_bias, cosines, sines)
+    kv_halo = send(
+        jnp.where(first, qkv[group_rows:, head_dim:], qkv[:group_rows, head_dim:]), "fsdp", to_next
+    )
+    operands = (
+        qkv,
+        kv_halo,
+        seg_rows,
+        token_rows,
+        seg_rows.reshape(2 * group_rows, 1),
+        token_rows.reshape(2 * group_rows, 1),
+        seg_halo,
+        token_halo,
+    )
+    attended, lse = attention_forward(halo_of, operands)
+
+    expand_bias_half = lax.dynamic_slice_in_dim(expand_bias, core * hidden, hidden).reshape(1, -1)
+    pieces_2 = lax.optimization_barrier((spread_2 + relayed_2, spread_3[1:]))[0]
+    weight_expand, activated, slope = expand_product(xm, pieces_2, expand_bias_half)
+
+    def reduce_features(left, right):
+        def rows(start, count):
+            return contract_rows(left[:, start : start + count], right)
+
+        got_a = send(rows(2 * shard_feat, 2 * shard_feat).astype(bf16), "fsdp", to_y)
+        got_b = send(rows(6 * shard_feat, 2 * shard_feat).astype(bf16), "fsdp", to_x)
+        pass_a = rows(shard_feat, shard_feat) + got_a[shard_feat:].astype(f32)
+        pass_b = rows(5 * shard_feat, shard_feat) + got_b[shard_feat:].astype(f32)
+        last_a = send(pass_a.astype(bf16), "fsdp", to_x)
+        last_b = send(pass_b.astype(bf16), "fsdp", to_y)
+        sum_a = rows(0, shard_feat) + got_a[:shard_feat].astype(f32) + last_a.astype(f32)
+        sum_b = (
+            rows(4 * shard_feat, shard_feat) + got_b[:shard_feat].astype(f32) + last_b.astype(f32)
+        )
+        taken = send(jnp.where(first, sum_b, sum_a), "fsdp", to_core)
+        kept = jnp.where(first, sum_a, sum_b)
+        return jnp.where(first, kept, taken), jnp.where(first, taken, kept)
+
+    def over_tensor(rows):
+        total = rows[:shard_rows]
+        for k in range(1, n_z):
+            piece = rows[k * shard_rows : (k + 1) * shard_rows].astype(bf16)
+            total = total + send(
+                piece, "tensor", [(i, (i - k) % n_z) for i in range(n_z)]
+            ).astype(f32)
+        return total
+
+    dc_halves = reduce_features(dy_all, jnp.concatenate([attended, activated], axis=1))
+
+    attn_grad = product(dy_all, weight_qd[:, qkv_cols:]).astype(bf16)
+    query_grad, before_part, own_part = attention_backward(
+        halo_of, operands, lse, attended, attn_grad
+    )
+    from_later = send(
+        jnp.where(first, before_part[:group_rows], before_part[group_rows:]), "fsdp", to_prev
+    )
+    qkv_grad, qkv_bias_part = rotated_back(
+        later_of, query_grad, own_part, before_part, from_later, cosines, sines
+    )
+    qkv_halves = reduce_features(xa, qkv_grad)
+
+    weight_contract, pre_grad, expand_bias_part = contract_product(
+        dy_all, spread_3 + relayed_3, slope
+    )
+    expand_halves = reduce_features(xm, pre_grad)
+
+    rows_of = lambda half, dtype: branch_rows(
+        half, attended, activated, weight_qd, weight_contract, dtype
+    )
+    branch_other = send(rows_of(1, bf16), "fsdp", to_core)
+    branch_sum = over_tensor(rows_of(0, f32) + branch_other.astype(f32))
+    output_rel = x_rel.astype(f32) + branch_sum + vectors[4] + vectors[5]
+
+    backs = lambda half, dtype: back_rows(
+        half, qkv_grad, pre_grad, x_all, weight_qd, weight_expand, vectors, dtype
+    )
+    weighted_other, sums_other = backs(1, bf16)
+    weighted_other = send(weighted_other, "fsdp", to_core)
+    weighted_own, sums_own = backs(0, f32)
+    plain_index = jnp.sum(
+        jnp.where(feature_index[None, :] == places[:, None], places[None, :], 0), axis=1
+    )
+    vector_part = jnp.concatenate(
+        [sums_own + sums_other, jnp.sum(dy_rel.astype(f32), axis=0, keepdims=True)], axis=0
+    )
+    (vector_part,) = moved((vector_part,), plain_index)
+    bias_part = jnp.concatenate([qkv_bias_part[0], expand_bias_part[0]])
+    n_vector = vector_part.size
+    small = jnp.concatenate([vector_part.reshape(-1), bias_part]).reshape(-1, 128)
+    small = small + send(small, "fsdp", to_x)
+    (output,) = moved((output_rel,), plain_index)
+    weighted = over_tensor(tied(weighted_own + weighted_other.astype(f32), small))
+    xhat_own, inverse_own = normalized_row_block(x_rel.astype(f32))
+    input_gradient = dy_rel.astype(f32) + inverse_own * (
+        weighted
+        - jnp.mean(weighted, axis=-1, keepdims=True)
+        - xhat_own * jnp.mean(weighted * xhat_own, axis=-1, keepdims=True)
+    )
+    (block_input_gradient,) = moved((input_gradient,), plain_index)
+
+    small = small + send(small, "fsdp", to_y)
+    small_other = send(small, "fsdp", to_core)
+    flat, flat_other = small.reshape(-1), small_other.reshape(-1)
+    vector_sum = (flat[:n_vector] + flat_other[:n_vector]).reshape(-1, 128)
+    for bit in (1, 2):
+        vector_sum = vector_sum + send(
+            vector_sum, "tensor", [(i, i ^ bit) for i in range(n_z)]
+        )
+    vector_sum = vector_sum.reshape(vector_part.shape)
+    grad_norm_vectors = jnp.concatenate([vector_sum, vector_sum[4:]], axis=0)
+    bias_first = jnp.where(first, flat[n_vector:], flat_other[n_vector:])
+    bias_second = jnp.where(first, flat_other[n_vector:], flat[n_vector:])
+    grad_qkv_bias = jnp.stack([bias_first[:qkv_cols], bias_second[:qkv_cols]])
+    grad_expand_bias = jnp.concatenate([bias_first[qkv_cols:], bias_second[qkv_cols:]])
+
+    grad_contract_weight = jnp.concatenate([part[:, head_dim:] for part in dc_halves], axis=1)
+    grad_dense_weight = jnp.concatenate([part[:, :head_dim] for part in dc_halves], axis=1)
+    grad_expand_weight = jnp.concatenate(expand_halves, axis=1)
+    grad_qkv_weight = jnp.stack(qkv_halves, axis=1)
+    new_qkv_weight, new_moment_qkv_weight, new_second_qkv_weight = adam_step(
+        qkv_weight,
+        grad_qkv_weight,
+        moment_qkv_weight,
+        second_qkv_weight,
+        rate_qkv_weight,
+        decay_matrix,
+    )
+    new_qkv_bias, new_moment_qkv_bias, new_second_qkv_bias = adam_step(
+        qkv_bias, grad_qkv_bias, moment_qkv_bias, second_qkv_bias, rate_qkv_bias, 0.0
+    )
+    new_dense_weight, new_moment_dense_weight, new_second_dense_weight = adam_step(
+        dense_weight,
+        grad_dense_weight,
+        moment_dense_weight,
+        second_dense_weight,
+        rate_dense_weight,
+        decay_matrix,
+    )
+    new_expand_weight, new_moment_expand_weight, new_second_expand_weight = adam_step(
+        expand_weight,
+        grad_expand_weight,
+        moment_expand_weight,
+        second_expand_weight,
+        rate_expand_weight,
+        decay_matrix,
+    )
+    new_expand_bias, new_moment_expand_bias, new_second_expand_bias = adam_step(
+        expand_bias, grad_expand_bias, moment_expand_bias, second_expand_bias, rate_expand_bias, 0.0
+    )
+    new_contract_weight, new_moment_contract_weight, new_second_contract_weight = adam_step(
+        contract_weight,
+        grad_contract_weight,
+        moment_contract_weight,
+        second_contract_weight,
+        rate_contract_weight,
+        decay_matrix,
+    )
+    new_norm_vectors, new_moment_norm_vectors, new_second_norm_vectors = adam_step(
+        norm_bias_vectors,
+        grad_norm_vectors,
+        moment_norm_vectors,
+        second_norm_vectors,
+        rate_norm_vectors,
+        0.0,
+    )
+    return (
+        output,
+        block_input_gradient,
+        grad_qkv_weight,
+        new_qkv_weight,
+        new_moment_qkv_weight,
+        new_second_qkv_weight,
+        grad_qkv_bias,
+        new_qkv_bias,
+        new_moment_qkv_bias,
+        new_second_qkv_bias,
+        grad_dense_weight,
+        new_dense_weight,
+        new_moment_dense_weight,
+        new_second_dense_weight,
+        grad_expand_weight,
+        new_expand_weight,
+        new_moment_expand_weight,
+        new_second_expand_weight,
+        grad_expand_bias,
+        new_expand_bias,
+        new_moment_expand_bias,
+        new_second_expand_bias,
+        grad_contract_weight,
+        new_contract_weight,
+        new_moment_contract_weight,
+        new_second_contract_weight,
+        grad_norm_vectors,
+        new_norm_vectors,
+        new_moment_norm_vectors,
+        new_second_norm_vectors,
+    )
+
+
 def solution(mesh):
+    paired = mesh.shape["fsdp"] == 8 and mesh.shape["tensor"] == 4
+    per_device = per_device_paired if paired else per_device_generic
     return jax.shard_map(
         per_device,
         mesh=mesh,

time: 969 us -> 542 us (0.56)
  waiting for transfers between devices: 683 us -> 151 us
  Pallas kernels: 0 us -> 118 us
  starting transfers between devices: 9.34 us -> 101 us
  matrix products: 115 us -> 53.1 us
  blocking collectives: 44.4 us -> 0 us
  local copies, waits for them, and re-layouts: 41.9 us -> 55.8 us
  between operations: 15.3 us -> 1.93 us
    reduce_scatter x7 -> x0, waiting for transfers between devices: 496 us -> none  [the longest x1 112 us: per_device(): lax.psum_scatter(contract_part, 'fsdp', scatter_dimension=0, tiled=True)]
    all_gather x6 -> x0, waiting for transfers between devices: 181 us -> none  [the longest x1 52.6 us: per_device(): lax.all_gather(shards_bf[2], 'fsdp', axis=0, tiled=True)]
    ppermute x4 -> x54, waiting for transfers between devices: 4.4 us -> 151 us  [send(): return lax.ppermute(value, axis, pairs)]
    pallas_call x0 -> x15, Pallas kernels: none -> 118 us  [the longest x3 30.9 us: gathered_product(): pl.pallas_call(body, grid=(columns // tile,), in_specs=[pl.BlockSpec((row...]
    ppermute x4 -> x54, starting transfers between devices: 8.39 us -> 101 us  [send(): return lax.ppermute(value, axis, pairs)]
    dot_general x15 -> x1, matrix products: 89.2 us -> 4.53 us  [product(): return jnp.dot(left, right, preferred_element_type=jnp.float32)]
    psum x2 -> x0, blocking collectives: 44.4 us -> none  [the longest x1 24.6 us: per_device(): lax.psum((qkv_bias_part, expand_bias_part, vector_part), 'fsdp')]
    dot_general x3 -> x18, matrix products: 26.2 us -> 48.5 us  [contract_rows(): lax.dot_general(left_rows, right_rows, (((0,), (0,)), ((), ())), preferre...]
  transfers between devices with their start and end apart: 17 -> 54, of which waited for: 14 -> 15; matrix products, arithmetic and copies ran while one was open for 19% -> 28% of each run, Pallas kernels for 0% -> 13%
where the time goes in v2:
time: 542 us; the launch traced here: 533 us
  waiting for transfers between devices  151 us (28%)
  Pallas kernels  118 us (22%)
  starting transfers between devices  101 us (19%)
  local copies, waits for them, and re-layouts  55.8 us (10%)
  other arithmetic  53.3 us (10%)
  matrix products  53.1 us (10%)
    ppermute x54, waiting for transfers between devices, send(): return lax.ppermute(value, axis, pairs)  151 us
    ppermute x54, starting transfers between devices, send(): return lax.ppermute(value, axis, pairs)  101 us
    dot_general x18, matrix products, contract_rows(): lax.dot_general(left_rows, right_rows, (((0,), (0,)), ((), ())), preferre...  48.5 us
    pallas_call x3, Pallas kernels, gathered_product(): pl.pallas_call(body, grid=(columns // tile,), in_specs=[pl.BlockSpec((row...  30.9 us
    unnamed x156, local copies, waits for them, and re-layouts  27.5 us
    pallas_call x4, Pallas kernels, moved(): pl.pallas_call(body, grid_spec=pltpu.PrefetchScalarGridSpec(num_scalar_pr...  22.3 us
    pallas_call x2, Pallas kernels, back_rows(): pl.pallas_call(body, grid=(depth // tile,), in_specs=[pl.BlockSpec((rows,...  22.3 us
    sub x7, other arithmetic, adam_step(): parameter - step_rate * (moment_hat / (jnp.sqrt(second_hat) + adam_eps) +...  15.6 us
  transfers between devices with their start and end apart: 54, of which 15 were waited for; matrix products, arithmetic and copies ran while one was open for 28% of the time, Pallas kernels for 13%

profile of v2, /device:TPU:0, one launch (start us, length us, event | category | flops | bytes accessed | tf_op | source)
XLA Modules:
  0.0 533.2 jit_solution(8046109197394715074)
XLA Ops:
  1.2 5.8 %moved.4 = (bf16[128,2048]{1,0:T(8,128)(2,1)}, bf16[128,2048]{1,0:T(8,128)(2,1)}, f32[6,2048]{1,0:T(8,128)}) custom-call(s32[8]{0:T(128)} %fusion.76.index_ref, bf16[128,2048]{1,0:T(8,128)(2,1)} %refs_0_.1, bf16[128,2048]{1,0:T(8,128)(2,1)} %refs_1_.1, f32[6,2048]{1,0:T(8,128)} %refs_2_.1), custom_call_target="tpu_custom_call" | custom-call | tf_op jit(solution)/shard_map/moved/pallas_call | solution.py:456
  7.0 3.1 collective-permute-start
  10.0 2.6 collective-permute-start.1
  35.0 13.7 %collective-permute-start.20 = (bf16[128,2048]{1,0:T(8,128)(2,1)S(1)}, bf16[128,2048]{1,0:T(8,128)(2,1)S(1)}, u32[]{:S(2)}, u32[]{:S(2)}) collective-permute-start(bf16[128,2048]{1,0:T(8,128)(2,1)S(1)} %copy-done.9), channel_id=1, source_target_pairs={{0,2},{1,3},{2,0},{3,1},{4,6},{5,7},{6,4},{7,5},{8,10},{9,11},{10,... | collective-permute-start | bytes 1572872 | tf_op jit(solution)/shard_map/ppermute | solution.py:437
  52.5 2.9 pad_maximum_fusion
  59.9 31.9 %collective-permute-done.20 = bf16[128,2048]{1,0:T(8,128)(2,1)S(1)} collective-permute-done((bf16[128,2048]{1,0:T(8,128)(2,1)S(1)}, bf16[128,2048]{1,0:T(8,128)(2,1)S(1)}, u32[]{:S(2)}, u32[]{:S(2)}) %collective-permute-start.20) | collective-permute-done | bytes 524320 | tf_op jit(solution)/shard_map/ppermute | solution.py:437
  102.0 15.8 %collective-permute-done.10.from_x = bf16[512,1024]{1,0:T(8,128)(2,1)S(1)} collective-permute-done((bf16[512,1024]{1,0:T(8,128)(2,1)S(1)}, bf16[512,1024]{1,0:T(8,128)(2,1)S(1)}, u32[]{:S(2)}, u32[]{:S(2)}) %collective-permute-start.10) | collective-permute-done | bytes 1048608 | tf_op jit(solution)/shard_map/ppermute | solution.py:437
  120.9 8.2 %collective-permute-done.7.top = bf16[256,1024]{1,0:T(8,128)(2,1)S(1)} collective-permute-done((bf16[256,1024]{1,0:T(8,128)(2,1)S(1)}, bf16[256,1024]{1,0:T(8,128)(2,1)S(1)}, u32[]{:S(2)}, u32[]{:S(2)}) %collective-permute-start.7) | collective-permute-done | bytes 524320 | tf_op jit(solution)/shard_map/ppermute | solution.py:437
  135.0 3.1 sine_multiply_fusion
  139.8 13.8 %collective-permute-done.8.bottom = bf16[256,1024]{1,0:T(8,128)(2,1)} collective-permute-done((bf16[256,1024]{1,0:T(8,128)(2,1)}, bf16[256,1024]{1,0:T(8,128)(2,1)}, u32[]{:S(2)}, u32[]{:S(2)}) %collective-permute-start.8) | collective-permute-done | bytes 524320 | tf_op jit(solution)/shard_map/ppermute | solution.py:437
  156.2 3.2 constant_dynamic-update-slice_fusion.x_ref.tile_ref
  159.4 7.8 %normed.1 = (bf16[1024,2048]{1,0:T(8,128)(2,1)}, bf16[1024,2048]{1,0:T(8,128)(2,1)}) custom-call(bf16[1024,2048]{1,0:T(8,128)(2,1)} %constant_dynamic-update-slice_fusion.x_ref.tile_ref, f32[6,2048]{1,0:T(8,128)} %get-tuple-element.70.vector_ref), custom_call_target="tpu_custom_call" | custom-call | tf_op jit(solution)/shard_map/normed/pallas_call | solution.py:486
  167.2 9.0 %qkv.1 = (bf16[2048,1024]{1,0:T(8,128)(2,1)}, bf16[1024,768]{1,0:T(8,128)(2,1)}) custom-call(bf16[1024,2048]{1,0:T(8,128)(2,1)} %get-tuple-element.71.left_ref, bf16[512,1024]{1,0:T(8,128)(2,1)} %copy-done.18, bf16[512,1024]{1,0:T(8,128)(2,1)} %copy-done.26, bf16[512,1024]{1,0:T(8,128)(2,1)} %copy-done.23, bf16[256,1024]{1,0:T(8,128)(2,1)} %copy-done.38, ...), custom_call_target="tpu_custom_call" | custom-call | tf_op jit(solution)/shard_map/qkv/pallas_call | solution.py:532
  178.3 4.1 collective-permute-start.14
  185.4 3.2 constant_dynamic-update-slice_fusion.5.left_ref
  188.6 11.3 %expand.1 = (bf16[2048,1024]{1,0:T(8,128)(2,1)}, bf16[1024,1024]{1,0:T(8,128)(2,1)}, f32[1024,1024]{1,0:T(8,128)}) custom-call(bf16[1024,2048]{1,0:T(8,128)(2,1)} %get-tuple-element.82.left_ref, bf16[512,1024]{1,0:T(8,128)(2,1)} %copy-done.19, bf16[512,1024]{1,0:T(8,128)(2,1)} %copy-done.21, bf16[512,1024]{1,0:T(8,128)(2,1)} %copy-done.24, ...), custom_call_target="tpu_custom_call" | custom-call | tf_op jit(solution)/shard_map/expand/pallas_call | solution.py:532
  199.9 4.5 convolution_convert_fusion.6.refs_16_
  205.4 10.5 %contract.1 = (bf16[2048,1024]{1,0:T(8,128)(2,1)}, bf16[1024,1024]{1,0:T(8,128)(2,1)}, f32[1,1024]{1,0:T(1,128)}) custom-call(bf16[1024,2048]{1,0:T(8,128)(2,1)} %constant_dynamic-update-slice_fusion.5.left_ref, bf16[512,1024]{1,0:T(8,128)(2,1)} %copy-done.16, bf16[512,1024]{1,0:T(8,128)(2,1)} %collective-permute-done.17.from_x, ...), custom_call_target="tpu_custom_call" | custom-call | tf_op jit(solution)/shard_map/contract/pallas_call | solution.py:532
  215.9 7.0 %attention.1 = (bf16[1024,256]{1,0:T(8,128)(2,1)}, f32[1024,1]{1,0:T(8,128)}) custom-call(s32[2]{0:T(128)} %get-tuple-element.229.halo_ref, bf16[1024,768]{1,0:T(8,128)(2,1)} %get-tuple-element.79.refs_0_.refs_1_.refs_2_.refs_3_.refs_4_, bf16[1024,768]{1,0:T(8,128)(2,1)} %get-tuple-element.79.refs_0_.refs_1_.refs_2_.refs_3_.refs_4_, ...), custom_call_target="tpu_custom_call" | custom-call | tf_op jit(solution)/shard_map/attention/pallas_call | solution.py:631
  223.0 7.2 %branch_0.1 = f32[512,2048]{1,0:T(8,128)} custom-call(bf16[1024,256]{1,0:T(8,128)(2,1)} %get-tuple-element.81.attended_ref.refs_15_, bf16[1024,1024]{1,0:T(8,128)(2,1)} %get-tuple-element.89.activated_ref, bf16[2048,1024]{1,0:T(8,128)(2,1)} %get-tuple-element.90.dense_ref.qd_ref, bf16[2048,1024]{1,0:T(8,128)(2,1)} %get-tuple-element.93.contract_ref), custom_call_target="tpu_custom_call" | custom-call | tf_op jit(solution)/shard_map/branch_0/pallas_call | solution.py:846
  230.1 6.9 %branch_1.1 = bf16[512,2048]{1,0:T(8,128)(2,1)} custom-call(bf16[1024,256]{1,0:T(8,128)(2,1)} %get-tuple-element.81.attended_ref.refs_15_, bf16[1024,1024]{1,0:T(8,128)(2,1)} %get-tuple-element.89.activated_ref, bf16[2048,1024]{1,0:T(8,128)(2,1)} %get-tuple-element.90.dense_ref.qd_ref, bf16[2048,1024]{1,0:T(8,128)(2,1)} %get-tuple-element.93.contract_ref), custom_call_target="tpu_custom_call" | custom-call | tf_op jit(solution)/shard_map/branch_1/pallas_call | solution.py:846
  237.8 8.1 %attention_back.1 = (f32[1024,256]{1,0:T(8,128)}, f32[1024,512]{1,0:T(8,128)}, f32[1024,512]{1,0:T(8,128)}) custom-call(s32[2]{0:T(128)} %get-tuple-element.229.halo_ref, bf16[1024,768]{1,0:T(8,128)(2,1)} %get-tuple-element.79.refs_0_.refs_1_.refs_2_.refs_3_.refs_4_, bf16[1024,768]{1,0:T(8,128)(2,1)} %get-tuple-element.79.refs_0_.refs_1_.refs_2_.refs_3_.refs_4_, ...), custom_call_target="tpu_custom_call" | custom-call | tf_op jit(solution)/shard_map/attention_back/pallas_call | solution.py:631
  251.0 5.2 convolution_convert_fusion.1
  256.1 3.8 collective-permute-start.42
  259.9 2.3 convolution_convert_fusion.3
  262.3 4.7 convolution_convert_fusion
  267.9 2.3 convolution_convert_fusion.2
  271.8 2.6 collective-permute-start.49
  274.4 5.4 %rotated_back.1 = (bf16[1024,768]{1,0:T(8,128)(2,1)}, f32[1,768]{1,0:T(1,128)}) custom-call(s32[2]{0:T(128)} %get-tuple-element.228.later_ref, f32[1024,256]{1,0:T(8,128)} %get-tuple-element.95.query_ref, f32[1024,512]{1,0:T(8,128)} %get-tuple-element.96.own_ref, f32[1024,512]{1,0:T(8,128)} %get-tuple-element.97.before_ref, f32[512,512]{1,0:T(8,128)} %copy-done.36, ...), custom_call_target="tpu_custom_call" | custom-call | tf_op jit(solution)/shard_map/rotated_back/pallas_call | solution.py:813
  279.9 11.3 %back_0.1 = (f32[512,2048]{1,0:T(8,128)}, f32[4,2048]{1,0:T(4,128)}) custom-call(bf16[1024,768]{1,0:T(8,128)(2,1)} %get-tuple-element.98.qkv_ref, bf16[1024,1024]{1,0:T(8,128)(2,1)} %get-tuple-element.99.pre_ref, bf16[1024,2048]{1,0:T(8,128)(2,1)} %constant_dynamic-update-slice_fusion.x_ref.tile_ref, ...), custom_call_target="tpu_custom_call" | custom-call | tf_op jit(solution)/shard_map/back_0/pallas_call | solution.py:885
  291.2 11.0 %back_1.1 = (bf16[512,2048]{1,0:T(8,128)(2,1)}, f32[4,2048]{1,0:T(4,128)}) custom-call(bf16[1024,768]{1,0:T(8,128)(2,1)} %get-tuple-element.98.qkv_ref, bf16[1024,1024]{1,0:T(8,128)(2,1)} %get-tuple-element.99.pre_ref, bf16[1024,2048]{1,0:T(8,128)(2,1)} %constant_dynamic-update-slice_fusion.x_ref.tile_ref, ...), custom_call_target="tpu_custom_call" | custom-call | tf_op jit(solution)/shard_map/back_1/pallas_call | solution.py:885
  303.6 4.9 moved.6
  309.4 2.7 collective-permute-done.47
  312.1 11.7 %collective-permute-start.31 = (f32[94,128]{1,0:T(8,128)S(1)}, f32[94,128]{1,0:T(8,128)S(1)}, u32[]{:S(2)}, u32[]{:S(2)}) collective-permute-start(f32[94,128]{1,0:T(8,128)S(1)} %maximum_bitcast_fusion), channel_id=1, source_target_pairs={{0,8},{4,12},{8,0},{12,4},{16,24},{20,28},{24,16},{28,20},{1,9},{5... | collective-permute-start | bytes 144392 | tf_op jit(solution)/shard_map/ppermute | solution.py:437
  323.9 2.7 fusion.10
  326.6 3.1 convolution_convert_fusion.4
  329.9 2.7 fusion.11
  334.2 3.1 convolution_convert_fusion.5
  338.0 16.6 %collective-permute-start.52 = (f32[80,128]{1,0:T(8,128)S(1)}, f32[80,128]{1,0:T(8,128)S(1)}, u32[]{:S(2)}, u32[]{:S(2)}) collective-permute-start(f32[80,128]{1,0:T(8,128)S(1)} %slice_add_fusion.1), channel_id=1, source_target_pairs={{0,1},{1,0},{2,3},{3,2},{4,5},{5,4},{6,7},{7,6},{8,9},{9,8},{10,11... | collective-permute-start | bytes 122888 | tf_op jit(solution)/shard_map/ppermute | solution.py:437
  354.6 2.2 collective-permute-done.52
  356.8 5.5 %collective-permute-start.53 = (f32[80,128]{1,0:T(8,128)S(1)}, f32[80,128]{1,0:T(8,128)S(1)}, u32[]{:S(2)}, u32[]{:S(2)}) collective-permute-start(f32[80,128]{1,0:T(8,128)S(1)} %add.453), channel_id=1, source_target_pairs={{0,2},{1,3},{2,0},{3,1},{4,6},{5,7},{6,4},{7,5},{8,10},{9,11},{10,... | collective-permute-start | bytes 122888 | tf_op jit(solution)/shard_map/ppermute | solution.py:437
  366.1 2.9 fusion.2
  370.5 2.9 fusion.3
  373.4 4.9 collective-permute-done.48
  380.6 13.6 %collective-permute-done.50 = bf16[256,1024]{1,0:T(8,128)(2,1)S(1)} collective-permute-done((bf16[256,1024]{1,0:T(8,128)(2,1)S(1)}, bf16[256,1024]{1,0:T(8,128)(2,1)S(1)}, u32[]{:S(2)}, u32[]{:S(2)}) %collective-permute-start.50) | collective-permute-done | bytes 524320 | tf_op jit(solution)/shard_map/ppermute | solution.py:437
  399.2 10.1 %collective-permute-done.43 = bf16[256,1280]{1,0:T(8,128)(2,1)S(1)} collective-permute-done((bf16[256,1280]{1,0:T(8,128)(2,1)S(1)}, bf16[256,1280]{1,0:T(8,128)(2,1)S(1)}, u32[]{:S(2)}, u32[]{:S(2)}) %collective-permute-start.43) | collective-permute-done | bytes 655392 | tf_op jit(solution)/shard_map/ppermute | solution.py:437
  409.8 2.9 fusion.1
  414.7 4.2 broadcast_select_fusion.2
  418.9 2.7 fusion.91
  425.9 3.1 collective-permute-start.27
  432.7 5.7 %multiply_subtract_fusion.1 = (f32[256,2048]{1,0:T(8,128)}, f32[256,2048]{1,0:T(8,128)}, f32[256,2048]{1,0:T(8,128)}, f32[256,2048]{1,0:T(8,128)}) fusion(f32[256,2048]{1,0:T(8,128)S(1)} %copy-done.13, f32[256,2048]{1,0:T(8,128)S(1)} %copy-done.28, f32[256,2048]{1,0:T(8,128)} %param.46, f32[256,1024]{1,0:T(8,128)S(1)} %get-tuple-element.235, ...), kind=kLoop, calls=%fused_computation.23 | loop fusion | flops 8388608 | bytes 16777216 | tf_op jit(solution)/shard_map/sub | solution.py:98
  441.7 2.4 copy.89
  444.1 2.4 copy.90
  446.4 2.4 copy.91
  448.8 2.4 copy.92
  451.2 2.5 convert_add_fusion
  463.3 4.0 multiply_subtract_fusion
  467.4 2.7 multiply_subtract_fusion.3
  472.2 3.1 collective-permute-start.26
  475.3 20.6 %collective-permute-done.33 = bf16[128,2048]{1,0:T(8,128)(2,1)} collective-permute-done((bf16[128,2048]{1,0:T(8,128)(2,1)}, bf16[128,2048]{1,0:T(8,128)(2,1)}, u32[]{:S(2)}, u32[]{:S(2)}) %collective-permute-start.33) | collective-permute-done | bytes 524320 | tf_op jit(solution)/shard_map/ppermute | solution.py:437
  497.9 20.1 %collective-permute-done.26 = bf16[128,2048]{1,0:T(8,128)(2,1)S(1)} collective-permute-done((bf16[128,2048]{1,0:T(8,128)(2,1)S(1)}, bf16[128,2048]{1,0:T(8,128)(2,1)S(1)}, u32[]{:S(2)}, u32[]{:S(2)}) %collective-permute-start.26) | collective-permute-done | bytes 524320 | tf_op jit(solution)/shard_map/ppermute | solution.py:437
  518.0 3.3 convert_add_fusion.3
  521.3 5.9 %moved.5 = f32[128,2048]{1,0:T(8,128)} custom-call(s32[8]{0:T(128)} %select_reduce_fusion.2.index_ref, f32[128,2048]{1,0:T(8,128)} %get-tuple-element.254.refs_0_), custom_call_target="tpu_custom_call" | custom-call | tf_op jit(solution)/shard_map/moved/pallas_call | solution.py:456
  527.2 5.9 %moved.7 = f32[128,2048]{1,0:T(8,128)} custom-call(s32[8]{0:T(128)} %select_reduce_fusion.2.index_ref, f32[128,2048]{1,0:T(8,128)} %get-tuple-element.253.refs_0_), custom_call_target="tpu_custom_call" | custom-call | tf_op jit(solution)/shard_map/moved/pallas_call | solution.py:456
  (328 shorter events, 113.3 us)
Async XLA Ops:
  7.0 28.0 %collective-permute-start = (bf16[128,2048]{1,0:T(8,128)(2,1)}, bf16[128,2048]{1,0:T(8,128)(2,1)}, u32[]{:S(2)}, u32[]{:S(2)}) collective-permute-start(bf16[128,2048]{1,0:T(8,128)(2,1)} %get-tuple-element.69), channel_id=1, source_target_pairs={{0,1},{1,2},{2,3},{3,0},{4,5},{5,6},{6,7},{7,4},{8,9},{9,10},{10,1... | collective-permute-start | bytes 1572872 | tf_op jit(solution)/shard_map/ppermute | solution.py:437
  10.0 40.8 %collective-permute-start.1 = (bf16[128,2048]{1,0:T(8,128)(2,1)}, bf16[128,2048]{1,0:T(8,128)(2,1)}, u32[]{:S(2)}, u32[]{:S(2)}) collective-permute-start(bf16[128,2048]{1,0:T(8,128)(2,1)} %get-tuple-element.69), channel_id=1, source_target_pairs={{0,2},{1,3},{2,0},{3,1},{4,6},{5,7},{6,4},{7,5},{8,10},{9,11},{10,... | collective-permute-start | bytes 1572872 | tf_op jit(solution)/shard_map/ppermute | solution.py:437
  12.6 38.3 %collective-permute-start.2 = (bf16[128,2048]{1,0:T(8,128)(2,1)}, bf16[128,2048]{1,0:T(8,128)(2,1)}, u32[]{:S(2)}, u32[]{:S(2)}) collective-permute-start(bf16[128,2048]{1,0:T(8,128)(2,1)} %get-tuple-element.69), channel_id=1, source_target_pairs={{0,3},{1,0},{2,1},{3,2},{4,7},{5,4},{6,5},{7,6},{8,11},{9,8},{10,9... | collective-permute-start | bytes 1572872 | tf_op jit(solution)/shard_map/ppermute | solution.py:437
  16.1 16.0 %collective-permute-start.9 = (bf16[256,1024]{1,0:T(8,128)(2,1)}, bf16[256,1024]{1,0:T(8,128)(2,1)}, u32[]{:S(2)}, u32[]{:S(2)}) collective-permute-start(bf16[256,1024]{1,0:T(8,128)(2,1)} %dynamic-slice_convert_fusion.2), channel_id=1, source_target_pairs={{0,4},{4,0},{8,12},{12,8},{16,20},{20,16},{24,28},{28,24},{1,5},{5... | collective-permute-start | bytes 1572872 | tf_op jit(solution)/shard_map/ppermute | solution.py:437
  19.6 13.1 %collective-permute-start.4 = (bf16[256,1024]{1,0:T(8,128)(2,1)}, bf16[256,1024]{1,0:T(8,128)(2,1)}, u32[]{:S(2)}, u32[]{:S(2)}) collective-permute-start(bf16[256,1024]{1,0:T(8,128)(2,1)} %pad_maximum_fusion.9), channel_id=1, source_target_pairs={{0,4},{4,0},{8,12},{12,8},{16,20},{20,16},{24,28},{28,24},{1,5},{5... | collective-permute-start | bytes 1572872 | tf_op jit(solution)/shard_map/ppermute | solution.py:437
  32.1 27.7 %collective-permute-start.19 = (bf16[128,2048]{1,0:T(8,128)(2,1)S(1)}, bf16[128,2048]{1,0:T(8,128)(2,1)S(1)}, u32[]{:S(2)}, u32[]{:S(2)}) collective-permute-start(bf16[128,2048]{1,0:T(8,128)(2,1)S(1)} %copy-done.9), channel_id=1, source_target_pairs={{0,1},{1,2},{2,3},{3,0},{4,5},{5,6},{6,7},{7,4},{8,9},{9,10},{10,1... | collective-permute-start | bytes 1572872 | tf_op jit(solution)/shard_map/ppermute | solution.py:437
  32.8 17.8 %collective-permute-start.12 = (bf16[256,1024]{1,0:T(8,128)(2,1)}, bf16[256,1024]{1,0:T(8,128)(2,1)S(1)}, u32[]{:S(2)}, u32[]{:S(2)}) collective-permute-start(bf16[256,1024]{1,0:T(8,128)(2,1)} %dynamic-slice_convert_fusion.1), channel_id=1, source_target_pairs={{0,4},{4,0},{8,12},{12,8},{16,20},{20,16},{24,28},{28,24},{1,5},{5... | collective-permute-start | bytes 1572872 | tf_op jit(solution)/shard_map/ppermute | solution.py:437
  35.0 56.8 %collective-permute-start.20 = (bf16[128,2048]{1,0:T(8,128)(2,1)S(1)}, bf16[128,2048]{1,0:T(8,128)(2,1)S(1)}, u32[]{:S(2)}, u32[]{:S(2)}) collective-permute-start(bf16[128,2048]{1,0:T(8,128)(2,1)S(1)} %copy-done.9), channel_id=1, source_target_pairs={{0,2},{1,3},{2,0},{3,1},{4,6},{5,7},{6,4},{7,5},{8,10},{9,11},{10,... | collective-permute-start | bytes 1572872 | tf_op jit(solution)/shard_map/ppermute | solution.py:437
  50.5 42.7 %collective-permute-start.21 = (bf16[128,2048]{1,0:T(8,128)(2,1)S(1)}, bf16[128,2048]{1,0:T(8,128)(2,1)S(1)}, u32[]{:S(2)}, u32[]{:S(2)}) collective-permute-start(bf16[128,2048]{1,0:T(8,128)(2,1)S(1)} %copy-done.9), channel_id=1, source_target_pairs={{0,3},{1,0},{2,1},{3,2},{4,7},{5,4},{6,5},{7,6},{8,11},{9,8},{10,9... | collective-permute-start | bytes 1572872 | tf_op jit(solution)/shard_map/ppermute | solution.py:437
  50.8 6.5 %collective-permute-start.13 = (s32[512]{0:T(512)S(1)}, s32[512]{0:T(512)S(1)}, u32[]{:S(2)}, u32[]{:S(2)}) collective-permute-start(s32[512]{0:T(512)S(1)} %copy-done.61), channel_id=1, source_target_pairs={{0,4},{4,0},{8,12},{12,8},{16,20},{20,16},{24,28},{28,24},{1,5},{5... | collective-permute-start | bytes 6152 | tf_op jit(solution)/shard_map/ppermute | solution.py:437
  50.9 45.4 %collective-permute-start.6 = (bf16[512,1024]{1,0:T(8,128)(2,1)S(1)}, bf16[512,1024]{1,0:T(8,128)(2,1)S(1)}, u32[]{:S(2)}, u32[]{:S(2)}) collective-permute-start(bf16[512,1024]{1,0:T(8,128)(2,1)S(1)} %pad_maximum_fusion.5.block), channel_id=1, source_target_pairs={{0,16},{4,20},{8,24},{12,28},{16,0},{20,4},{24,8},{28,12},{1,17},{... | collective-permute-start | bytes 3145736 | tf_op jit(solution)/shard_map/ppermute | solution.py:437
  57.4 41.3 %collective-permute-start.5 = (bf16[512,1024]{1,0:T(8,128)(2,1)S(1)}, bf16[512,1024]{1,0:T(8,128)(2,1)S(1)}, u32[]{:S(2)}, u32[]{:S(2)}) collective-permute-start(bf16[512,1024]{1,0:T(8,128)(2,1)S(1)} %pad_maximum_fusion.5.block), channel_id=1, source_target_pairs={{0,8},{4,12},{8,0},{12,4},{16,24},{20,28},{24,16},{28,20},{1,9},{5... | collective-permute-start | bytes 3145736 | tf_op jit(solution)/shard_map/ppermute | solution.py:437
  59.1 37.3 %copy-start.19 = (bf16[512,1024]{1,0:T(8,128)(2,1)}, bf16[512,1024]{1,0:T(8,128)(2,1)S(1)}, u32[]{:S(2)}) copy-start(bf16[512,1024]{1,0:T(8,128)(2,1)S(1)} %pad_maximum_fusion.6.block) | copy-start | bytes 3145732
  59.8 94.9 %collective-permute-start.3 = (bf16[512,2048]{1,0:T(8,128)(2,1)}, bf16[512,2048]{1,0:T(8,128)(2,1)}, u32[]{:S(2)}, u32[]{:S(2)}) collective-permute-start(bf16[512,2048]{1,0:T(8,128)(2,1)} %pad_maximum_fusion), channel_id=1, source_target_pairs={{0,4},{4,0},{8,12},{12,8},{16,20},{20,16},{24,28},{28,24},{1,5},{5... | collective-permute-start | bytes 6291464 | tf_op jit(solution)/shard_map/ppermute | solution.py:437
  91.8 26.0 %collective-permute-start.10 = (bf16[512,1024]{1,0:T(8,128)(2,1)S(1)}, bf16[512,1024]{1,0:T(8,128)(2,1)S(1)}, u32[]{:S(2)}, u32[]{:S(2)}) collective-permute-start(bf16[512,1024]{1,0:T(8,128)(2,1)S(1)} %pad_maximum_fusion.6.block), channel_id=1, source_target_pairs={{0,8},{4,12},{8,0},{12,4},{16,24},{20,28},{24,16},{28,20},{1,9},{5... | collective-permute-start | bytes 3145736 | tf_op jit(solution)/shard_map/ppermute | solution.py:437
  93.3 26.0 %collective-permute-start.11 = (bf16[512,1024]{1,0:T(8,128)(2,1)S(1)}, bf16[512,1024]{1,0:T(8,128)(2,1)S(1)}, u32[]{:S(2)}, u32[]{:S(2)}) collective-permute-start(bf16[512,1024]{1,0:T(8,128)(2,1)S(1)} %pad_maximum_fusion.6.block), channel_id=1, source_target_pairs={{0,16},{4,20},{8,24},{12,28},{16,0},{20,4},{24,8},{28,12},{1,17},{... | collective-permute-start | bytes 3145736 | tf_op jit(solution)/shard_map/ppermute | solution.py:437
  96.4 89.0 %collective-permute-start.22 = (bf16[512,2048]{1,0:T(8,128)(2,1)}, bf16[512,2048]{1,0:T(8,128)(2,1)}, u32[]{:S(2)}, u32[]{:S(2)}) collective-permute-start(bf16[512,2048]{1,0:T(8,128)(2,1)} %pad_maximum_fusion.1), channel_id=1, source_target_pairs={{0,4},{4,0},{8,12},{12,8},{16,20},{20,16},{24,28},{28,24},{1,5},{5... | collective-permute-start | bytes 6291464 | tf_op jit(solution)/shard_map/ppermute | solution.py:437
  98.7 30.3 %collective-permute-start.7 = (bf16[256,1024]{1,0:T(8,128)(2,1)S(1)}, bf16[256,1024]{1,0:T(8,128)(2,1)S(1)}, u32[]{:S(2)}, u32[]{:S(2)}) collective-permute-start(bf16[256,1024]{1,0:T(8,128)(2,1)S(1)} %slice.290), channel_id=1, source_target_pairs={{0,8},{4,12},{8,0},{12,4},{16,24},{20,28},{24,16},{28,20},{1,9},{5... | collective-permute-start | bytes 1572872 | tf_op jit(solution)/shard_map/ppermute | solution.py:437
  99.4 35.6 %copy-start.16 = (bf16[512,1024]{1,0:T(8,128)(2,1)}, bf16[512,1024]{1,0:T(8,128)(2,1)S(1)}, u32[]{:S(2)}) copy-start(bf16[512,1024]{1,0:T(8,128)(2,1)S(1)} %pad_maximum_fusion.7.block) | copy-start | bytes 3145732
  100.3 34.7 %copy-start.64 = (f32[128]{0:T(128)S(1)}, f32[128]{0:T(128)}, u32[]{:S(2)}) copy-start(f32[128]{0:T(128)} %get-tuple-element.279) | copy-start | bytes 1540
  100.3 34.7 %copy-start.65 = (f32[128]{0:T(128)S(1)}, f32[128]{0:T(128)}, u32[]{:S(2)}) copy-start(f32[128]{0:T(128)} %get-tuple-element.280) | copy-start | bytes 1540
  100.3 34.7 %copy-start.66 = (pred[128]{0:T(512)(128)(4,1)S(1)}, pred[128]{0:T(512)(128)(4,1)}, u32[]{:S(2)}) copy-start(pred[128]{0:T(512)(128)(4,1)} %iota_compare_fusion.3) | copy-start | bytes 388
  117.8 65.4 %collective-permute-start.17 = (bf16[512,1024]{1,0:T(8,128)(2,1)S(1)}, bf16[512,1024]{1,0:T(8,128)(2,1)}, u32[]{:S(2)}, u32[]{:S(2)}) collective-permute-start(bf16[512,1024]{1,0:T(8,128)(2,1)S(1)} %pad_maximum_fusion.7.block), channel_id=1, source_target_pairs={{0,8},{4,12},{8,0},{12,4},{16,24},{20,28},{24,16},{28,20},{1,9},{5... | collective-permute-start | bytes 3145736 | tf_op jit(solution)/shard_map/ppermute | solution.py:437
  119.3 59.0 %collective-permute-start.18 = (bf16[512,1024]{1,0:T(8,128)(2,1)S(1)}, bf16[512,1024]{1,0:T(8,128)(2,1)S(1)}, u32[]{:S(2)}, u32[]{:S(2)}) collective-permute-start(bf16[512,1024]{1,0:T(8,128)(2,1)S(1)} %pad_maximum_fusion.7.block), channel_id=1, source_target_pairs={{0,16},{4,20},{8,24},{12,28},{16,0},{20,4},{24,8},{28,12},{1,17},{... | collective-permute-start | bytes 3145736 | tf_op jit(solution)/shard_map/ppermute | solution.py:437
  129.8 23.7 %collective-permute-start.8 = (bf16[256,1024]{1,0:T(8,128)(2,1)}, bf16[256,1024]{1,0:T(8,128)(2,1)}, u32[]{:S(2)}, u32[]{:S(2)}) collective-permute-start(bf16[256,1024]{1,0:T(8,128)(2,1)} %slice.291), channel_id=1, source_target_pairs={{0,16},{4,20},{8,24},{12,28},{16,0},{20,4},{24,8},{28,12},{1,17},{... | collective-permute-start | bytes 1572872 | tf_op jit(solution)/shard_map/ppermute | solution.py:437
  153.5 35.0 %collective-permute-start.15 = (bf16[256,1024]{1,0:T(8,128)(2,1)}, bf16[256,1024]{1,0:T(8,128)(2,1)}, u32[]{:S(2)}, u32[]{:S(2)}) collective-permute-start(bf16[256,1024]{1,0:T(8,128)(2,1)} %slice.294), channel_id=1, source_target_pairs={{0,8},{4,12},{8,0},{12,4},{16,24},{20,28},{24,16},{28,20},{1,9},{5... | collective-permute-start | bytes 1572872 | tf_op jit(solution)/shard_map/ppermute | solution.py:437
  154.7 33.8 %collective-permute-start.16 = (bf16[256,1024]{1,0:T(8,128)(2,1)}, bf16[256,1024]{1,0:T(8,128)(2,1)}, u32[]{:S(2)}, u32[]{:S(2)}) collective-permute-start(bf16[256,1024]{1,0:T(8,128)(2,1)} %slice.295), channel_id=1, source_target_pairs={{0,16},{4,20},{8,24},{12,28},{16,0},{20,4},{24,8},{28,12},{1,17},{... | collective-permute-start | bytes 1572872 | tf_op jit(solution)/shard_map/ppermute | solution.py:437
  178.3 37.7 %collective-permute-start.14 = (bf16[512,512]{1,0:T(8,128)(2,1)}, bf16[512,512]{1,0:T(8,128)(2,1)}, u32[]{:S(2)}, u32[]{:S(2)}) collective-permute-start(bf16[512,512]{1,0:T(8,128)(2,1)} %slice_select_fusion.1), channel_id=1, source_target_pairs={{0,8},{4,12},{8,16},{12,20},{16,24},{20,28},{1,9},{5,13},{9,17},{1... | collective-permute-start | bytes 1572872 | tf_op jit(solution)/shard_map/ppermute | solution.py:437
  183.2 21.2 %collective-permute-start.23 = (bf16[256,1024]{1,0:T(8,128)(2,1)}, bf16[256,1024]{1,0:T(8,128)(2,1)S(1)}, u32[]{:S(2)}, u32[]{:S(2)}) collective-permute-start(bf16[256,1024]{1,0:T(8,128)(2,1)} %slice.296), channel_id=1, source_target_pairs={{0,8},{4,12},{8,0},{12,4},{16,24},{20,28},{24,16},{28,20},{1,9},{5... | collective-permute-start | bytes 1572872 | tf_op jit(solution)/shard_map/ppermute | solution.py:437
  185.4 19.0 %collective-permute-start.24 = (bf16[256,1024]{1,0:T(8,128)(2,1)}, bf16[256,1024]{1,0:T(8,128)(2,1)S(1)}, u32[]{:S(2)}, u32[]{:S(2)}) collective-permute-start(bf16[256,1024]{1,0:T(8,128)(2,1)} %slice.297), channel_id=1, source_target_pairs={{0,16},{4,20},{8,24},{12,28},{16,0},{20,4},{24,8},{28,12},{1,17},{... | collective-permute-start | bytes 1572872 | tf_op jit(solution)/shard_map/ppermute | solution.py:437
  247.9 23.9 %collective-permute-start.29 = (f32[512,512]{1,0:T(8,128)S(1)}, f32[512,512]{1,0:T(8,128)S(1)}, u32[]{:S(2)}, u32[]{:S(2)}) collective-permute-start(f32[512,512]{1,0:T(8,128)S(1)} %slice_select_fusion), channel_id=1, source_target_pairs={{8,0},{12,4},{16,8},{20,12},{24,16},{28,20},{9,1},{13,5},{17,9},{2... | collective-permute-start | bytes 3145736 | tf_op jit(solution)/shard_map/ppermute | solution.py:437
  249.4 169.6 %collective-permute-start.25 = (bf16[512,2048]{1,0:T(8,128)(2,1)}, bf16[512,2048]{1,0:T(8,128)(2,1)}, u32[]{:S(2)}, u32[]{:S(2)}) collective-permute-start(bf16[512,2048]{1,0:T(8,128)(2,1)} %branch_1.1), channel_id=1, source_target_pairs={{0,4},{4,0},{8,12},{12,8},{16,20},{20,16},{24,28},{28,24},{1,5},{5... | collective-permute-start | bytes 6291464 | tf_op jit(solution)/shard_map/ppermute | solution.py:437
  256.1 109.8 %collective-permute-start.42 = (bf16[512,1280]{1,0:T(8,128)(2,1)}, bf16[512,1280]{1,0:T(8,128)(2,1)}, u32[]{:S(2)}, u32[]{:S(2)}) collective-permute-start(bf16[512,1280]{1,0:T(8,128)(2,1)} %convolution_convert_fusion.1), channel_id=1, source_target_pairs={{0,16},{4,20},{8,24},{12,28},{16,0},{20,4},{24,8},{28,12},{1,17},{... | collective-permute-start | bytes 3932168 | tf_op jit(solution)/shard_map/ppermute | solution.py:437
  262.2 49.9 %collective-permute-start.47 = (bf16[512,1024]{1,0:T(8,128)(2,1)}, bf16[512,1024]{1,0:T(8,128)(2,1)}, u32[]{:S(2)}, u32[]{:S(2)}) collective-permute-start(bf16[512,1024]{1,0:T(8,128)(2,1)} %convolution_convert_fusion.3), channel_id=1, source_target_pairs={{0,16},{4,20},{8,24},{12,28},{16,0},{20,4},{24,8},{28,12},{1,17},{... | collective-permute-start | bytes 3145736 | tf_op jit(solution)/shard_map/ppermute | solution.py:437
  266.9 102.1 %collective-permute-start.44 = (bf16[512,1280]{1,0:T(8,128)(2,1)}, bf16[512,1280]{1,0:T(8,128)(2,1)}, u32[]{:S(2)}, u32[]{:S(2)}) collective-permute-start(bf16[512,1280]{1,0:T(8,128)(2,1)} %convolution_convert_fusion), channel_id=1, source_target_pairs={{0,8},{4,12},{8,0},{12,4},{16,24},{20,28},{24,16},{28,20},{1,9},{5... | collective-permute-start | bytes 3932168 | tf_op jit(solution)/shard_map/ppermute | solution.py:437
  271.8 58.0 %collective-permute-start.49 = (bf16[512,1024]{1,0:T(8,128)(2,1)}, bf16[512,1024]{1,0:T(8,128)(2,1)}, u32[]{:S(2)}, u32[]{:S(2)}) collective-permute-start(bf16[512,1024]{1,0:T(8,128)(2,1)} %convolution_convert_fusion.2), channel_id=1, source_target_pairs={{0,8},{4,12},{8,0},{12,4},{16,24},{20,28},{24,16},{28,20},{1,9},{5... | collective-permute-start | bytes 3145736 | tf_op jit(solution)/shard_map/ppermute | solution.py:437
  291.2 32.7 %copy-start.1 = (bf16[1024,1024]{1,0:T(8,128)(2,1)S(1)}, bf16[1024,1024]{1,0:T(8,128)(2,1)}, u32[]{:S(2)}) copy-start(bf16[1024,1024]{1,0:T(8,128)(2,1)} %get-tuple-element.99.pre_ref) | copy-start | bytes 6291460
  312.1 17.6 %collective-permute-start.31 = (f32[94,128]{1,0:T(8,128)S(1)}, f32[94,128]{1,0:T(8,128)S(1)}, u32[]{:S(2)}, u32[]{:S(2)}) collective-permute-start(f32[94,128]{1,0:T(8,128)S(1)} %maximum_bitcast_fusion), channel_id=1, source_target_pairs={{0,8},{4,12},{8,0},{12,4},{16,24},{20,28},{24,16},{28,20},{1,9},{5... | collective-permute-start | bytes 144392 | tf_op jit(solution)/shard_map/ppermute | solution.py:437
  329.8 121.4 %collective-permute-start.30 = (bf16[512,2048]{1,0:T(8,128)(2,1)}, bf16[512,2048]{1,0:T(8,128)(2,1)}, u32[]{:S(2)}, u32[]{:S(2)}) collective-permute-start(bf16[512,2048]{1,0:T(8,128)(2,1)} %get-tuple-element.102), channel_id=1, source_target_pairs={{0,4},{4,0},{8,12},{12,8},{16,20},{20,16},{24,28},{28,24},{1,5},{5... | collective-permute-start | bytes 6291464 | tf_op jit(solution)/shard_map/ppermute | solution.py:437
  329.8 4.2 collective-permute-start.40
  334.1 31.2 %copy-start.42 = (f32[6,2048]{1,0:T(8,128)S(1)}, f32[6,2048]{1,0:T(8,128)}, u32[]{:S(2)}) copy-start(f32[6,2048]{1,0:T(8,128)} %refs_2_.1) | copy-start | bytes 147460
  334.1 31.2 %copy-start.44 = (f32[6,2048]{1,0:T(8,128)S(1)}, f32[6,2048]{1,0:T(8,128)}, u32[]{:S(2)}) copy-start(f32[6,2048]{1,0:T(8,128)} %param.42) | copy-start | bytes 147460
  334.1 31.2 %copy-start.45 = (f32[6,2048]{1,0:T(8,128)S(1)}, f32[6,2048]{1,0:T(8,128)}, u32[]{:S(2)}) copy-start(f32[6,2048]{1,0:T(8,128)} %param.49) | copy-start | bytes 147460
  334.1 3.2 collective-permute-start.41
  338.0 18.8 %collective-permute-start.52 = (f32[80,128]{1,0:T(8,128)S(1)}, f32[80,128]{1,0:T(8,128)S(1)}, u32[]{:S(2)}, u32[]{:S(2)}) collective-permute-start(f32[80,128]{1,0:T(8,128)S(1)} %slice_add_fusion.1), channel_id=1, source_target_pairs={{0,1},{1,0},{2,3},{3,2},{4,5},{5,4},{6,7},{7,6},{8,9},{9,8},{10,11... | collective-permute-start | bytes 122888 | tf_op jit(solution)/shard_map/ppermute | solution.py:437
  356.8 7.8 %collective-permute-start.53 = (f32[80,128]{1,0:T(8,128)S(1)}, f32[80,128]{1,0:T(8,128)S(1)}, u32[]{:S(2)}, u32[]{:S(2)}) collective-permute-start(f32[80,128]{1,0:T(8,128)S(1)} %add.453), channel_id=1, source_target_pairs={{0,2},{1,3},{2,0},{3,1},{4,6},{5,7},{6,4},{7,5},{8,10},{9,11},{10,... | collective-permute-start | bytes 122888 | tf_op jit(solution)/shard_map/ppermute | solution.py:437
  364.6 31.7 %collective-permute-start.35 = (bf16[512,768]{1,0:T(8,128)(2,1)}, bf16[512,768]{1,0:T(8,128)(2,1)}, u32[]{:S(2)}, u32[]{:S(2)}) collective-permute-start(bf16[512,768]{1,0:T(8,128)(2,1)} %convolution_convert_fusion.5), channel_id=1, source_target_pairs={{0,16},{4,20},{8,24},{12,28},{16,0},{20,4},{24,8},{28,12},{1,17},{... | collective-permute-start | bytes 2359304 | tf_op jit(solution)/shard_map/ppermute | solution.py:437
  366.0 12.3 %collective-permute-start.48 = (bf16[256,1024]{1,0:T(8,128)(2,1)}, bf16[256,1024]{1,0:T(8,128)(2,1)S(1)}, u32[]{:S(2)}, u32[]{:S(2)}) collective-permute-start(bf16[256,1024]{1,0:T(8,128)(2,1)} %fusion.10), channel_id=1, source_target_pairs={{0,8},{4,12},{8,0},{12,4},{16,24},{20,28},{24,16},{28,20},{1,9},{5... | collective-permute-start | bytes 1572872 | tf_op jit(solution)/shard_map/ppermute | solution.py:437
  369.1 25.1 %collective-permute-start.50 = (bf16[256,1024]{1,0:T(8,128)(2,1)S(1)}, bf16[256,1024]{1,0:T(8,128)(2,1)S(1)}, u32[]{:S(2)}, u32[]{:S(2)}) collective-permute-start(bf16[256,1024]{1,0:T(8,128)(2,1)S(1)} %copy-done.37), channel_id=1, source_target_pairs={{0,16},{4,20},{8,24},{12,28},{16,0},{20,4},{24,8},{28,12},{1,17},{... | collective-permute-start | bytes 1572872 | tf_op jit(solution)/shard_map/ppermute | solution.py:437
  378.3 20.2 %collective-permute-start.37 = (bf16[512,768]{1,0:T(8,128)(2,1)S(1)}, bf16[512,768]{1,0:T(8,128)(2,1)S(1)}, u32[]{:S(2)}, u32[]{:S(2)}) collective-permute-start(bf16[512,768]{1,0:T(8,128)(2,1)S(1)} %copy-done.68), channel_id=1, source_target_pairs={{0,8},{4,12},{8,0},{12,4},{16,24},{20,28},{24,16},{28,20},{1,9},{5... | collective-permute-start | bytes 2359304 | tf_op jit(solution)/shard_map/ppermute | solution.py:437
  394.2 15.1 %collective-permute-start.43 = (bf16[256,1280]{1,0:T(8,128)(2,1)S(1)}, bf16[256,1280]{1,0:T(8,128)(2,1)S(1)}, u32[]{:S(2)}, u32[]{:S(2)}) collective-permute-start(bf16[256,1280]{1,0:T(8,128)(2,1)S(1)} %fusion.2), channel_id=1, source_target_pairs={{0,8},{4,12},{8,0},{12,4},{16,24},{20,28},{24,16},{28,20},{1,9},{5... | collective-permute-start | bytes 1966088 | tf_op jit(solution)/shard_map/ppermute | solution.py:437
  396.3 16.4 %collective-permute-start.45 = (bf16[256,1280]{1,0:T(8,128)(2,1)S(1)}, bf16[256,1280]{1,0:T(8,128)(2,1)S(1)}, u32[]{:S(2)}, u32[]{:S(2)}) collective-permute-start(bf16[256,1280]{1,0:T(8,128)(2,1)S(1)} %fusion.3), channel_id=1, source_target_pairs={{0,16},{4,20},{8,24},{12,28},{16,0},{20,4},{24,8},{28,12},{1,17},{... | collective-permute-start | bytes 1966088 | tf_op jit(solution)/shard_map/ppermute | solution.py:437
  398.5 32.0 %collective-permute-start.51 = (f32[256,1024]{1,0:T(8,128)S(1)}, f32[256,1024]{1,0:T(8,128)S(1)}, u32[]{:S(2)}, u32[]{:S(2)}) collective-permute-start(f32[256,1024]{1,0:T(8,128)S(1)} %get-tuple-element.269), channel_id=1, source_target_pairs={{0,4},{4,0},{8,12},{12,8},{16,20},{20,16},{24,28},{28,24},{1,5},{5... | collective-permute-start | bytes 3145736 | tf_op jit(solution)/shard_map/ppermute | solution.py:437
  409.3 13.5 %collective-permute-start.36 = (bf16[256,768]{1,0:T(8,128)(2,1)S(1)}, bf16[256,768]{1,0:T(8,128)(2,1)S(1)}, u32[]{:S(2)}, u32[]{:S(2)}) collective-permute-start(bf16[256,768]{1,0:T(8,128)(2,1)S(1)} %fusion.14), channel_id=1, source_target_pairs={{0,8},{4,12},{8,0},{12,4},{16,24},{20,28},{24,16},{28,20},{1,9},{5... | collective-permute-start | bytes 1179656 | tf_op jit(solution)/shard_map/ppermute | solution.py:437
  412.8 13.1 %collective-permute-start.38 = (bf16[256,768]{1,0:T(8,128)(2,1)S(1)}, bf16[256,768]{1,0:T(8,128)(2,1)S(1)}, u32[]{:S(2)}, u32[]{:S(2)}) collective-permute-start(bf16[256,768]{1,0:T(8,128)(2,1)S(1)} %fusion.15), channel_id=1, source_target_pairs={{0,16},{4,20},{8,24},{12,28},{16,0},{20,4},{24,8},{28,12},{1,17},{... | collective-permute-start | bytes 1179656 | tf_op jit(solution)/shard_map/ppermute | solution.py:437
  418.9 38.5 %collective-permute-start.46 = (f32[256,1280]{1,0:T(8,128)}, f32[256,1280]{1,0:T(8,128)S(1)}, u32[]{:S(2)}, u32[]{:S(2)}) collective-permute-start(f32[256,1280]{1,0:T(8,128)} %get-tuple-element.267), channel_id=1, source_target_pairs={{0,4},{4,0},{8,12},{12,8},{16,20},{20,16},{24,28},{28,24},{1,5},{5... | collective-permute-start | bytes 3932168 | tf_op jit(solution)/shard_map/ppermute | solution.py:437
  422.8 75.0 %collective-permute-start.28 = (bf16[128,2048]{1,0:T(8,128)(2,1)}, bf16[128,2048]{1,0:T(8,128)(2,1)}, u32[]{:S(2)}, u32[]{:S(2)}) collective-permute-start(bf16[128,2048]{1,0:T(8,128)(2,1)} %get-tuple-element.246), channel_id=1, source_target_pairs={{0,1},{1,2},{2,3},{3,0},{4,5},{5,6},{6,7},{7,4},{8,9},{9,10},{10,1... | collective-permute-start | bytes 1572872 | tf_op jit(solution)/shard_map/ppermute | solution.py:437
  425.9 72.0 %collective-permute-start.27 = (bf16[128,2048]{1,0:T(8,128)(2,1)}, bf16[128,2048]{1,0:T(8,128)(2,1)}, u32[]{:S(2)}, u32[]{:S(2)}) collective-permute-start(bf16[128,2048]{1,0:T(8,128)(2,1)} %get-tuple-element.247), channel_id=1, source_target_pairs={{0,2},{1,3},{2,0},{3,1},{4,6},{5,7},{6,4},{7,5},{8,10},{9,11},{10,... | collective-permute-start | bytes 1572872 | tf_op jit(solution)/shard_map/ppermute | solution.py:437
  430.5 7.9 %collective-permute-start.39 = (f32[256,768]{1,0:T(8,128)}, f32[256,768]{1,0:T(8,128)}, u32[]{:S(2)}, u32[]{:S(2)}) collective-permute-start(f32[256,768]{1,0:T(8,128)} %get-tuple-element.265), channel_id=1, source_target_pairs={{0,4},{4,0},{8,12},{12,8},{16,20},{20,16},{24,28},{28,24},{1,5},{5... | collective-permute-start | bytes 2359304 | tf_op jit(solution)/shard_map/ppermute | solution.py:437
  455.1 17.1 %collective-permute-start.34 = (bf16[128,2048]{1,0:T(8,128)(2,1)}, bf16[128,2048]{1,0:T(8,128)(2,1)}, u32[]{:S(2)}, u32[]{:S(2)}) collective-permute-start(bf16[128,2048]{1,0:T(8,128)(2,1)} %get-tuple-element.243), channel_id=1, source_target_pairs={{0,1},{1,2},{2,3},{3,0},{4,5},{5,6},{6,7},{7,4},{8,9},{9,10},{10,1... | collective-permute-start | bytes 1572872 | tf_op jit(solution)/shard_map/ppermute | solution.py:437
  455.5 40.5 %collective-permute-start.33 = (bf16[128,2048]{1,0:T(8,128)(2,1)}, bf16[128,2048]{1,0:T(8,128)(2,1)}, u32[]{:S(2)}, u32[]{:S(2)}) collective-permute-start(bf16[128,2048]{1,0:T(8,128)(2,1)} %get-tuple-element.244), channel_id=1, source_target_pairs={{0,2},{1,3},{2,0},{3,1},{4,6},{5,7},{6,4},{7,5},{8,10},{9,11},{10,... | collective-permute-start | bytes 1572872 | tf_op jit(solution)/shard_map/ppermute | solution.py:437
  457.4 38.5 %collective-permute-start.32 = (bf16[128,2048]{1,0:T(8,128)(2,1)}, bf16[128,2048]{1,0:T(8,128)(2,1)}, u32[]{:S(2)}, u32[]{:S(2)}) collective-permute-start(bf16[128,2048]{1,0:T(8,128)(2,1)} %get-tuple-element.242), channel_id=1, source_target_pairs={{0,3},{1,0},{2,1},{3,2},{4,7},{5,4},{6,5},{7,6},{8,11},{9,8},{10,9... | collective-permute-start | bytes 1572872 | tf_op jit(solution)/shard_map/ppermute | solution.py:437
  472.2 45.8 %copy-start.47 = (f32[1,2048]{1,0:T(1,128)S(1)}, f32[1,2048]{1,0:T(1,128)}, u32[]{:S(2)}) copy-start(f32[1,2048]{1,0:T(1,128)} %get-tuple-element.260) | copy-start | bytes 24580
  472.2 45.8 %collective-permute-start.26 = (bf16[128,2048]{1,0:T(8,128)(2,1)S(1)}, bf16[128,2048]{1,0:T(8,128)(2,1)S(1)}, u32[]{:S(2)}, u32[]{:S(2)}) collective-permute-start(bf16[128,2048]{1,0:T(8,128)(2,1)S(1)} %copy-done.41), channel_id=1, source_target_pairs={{0,3},{1,0},{2,1},{3,2},{4,7},{5,4},{6,5},{7,6},{8,11},{9,8},{10,9... | collective-permute-start | bytes 1572872 | tf_op jit(solution)/shard_map/ppermute | solution.py:437
  (59 other events, 498.5 us)
